TPU v7x, 32 devices: a whole 2x2x4 slice. The times are simulated.
32 devices in a mesh: star: 2 (over x), blk: 16 (over z, y, core).
Axes of the slice: x: 2, y: 2, z: 4, core: 2. Of those that a mesh axis runs over, the one named last changes fastest.
Arguments:
- lapse_field: float32 [256, 16, 256], P(('star', 'blk')), may hold values from 0.3 to 1
- conformal: float32 [256, 16, 256], P(('star', 'blk')), may hold values from 0.5 to 1.5
- mean_curv: float32 [256, 16, 256], P(('star', 'blk')), may hold values from -3 to 3
- conformal_metric: float32 [6, 256, 16, 256], P(None, ('star', 'blk')), may hold values from -0.3 to 1.6, as said below
- traceless_curv: float32 [6, 256, 16, 256], P(None, ('star', 'blk')), may hold values from -2 to 2
- shift_vector: float32 [3, 256, 16, 256], P(None, ('star', 'blk')), may hold values from -3 to 3
- density: float32 [2, 256, 16, 256], P('star', 'blk'), may hold values from 0.2 to 2
- momentum: float32 [2, 3, 256, 16, 256], P('star', None, 'blk'), may hold values from -3 to 3
- energy: float32 [2, 256, 16, 256], P('star', 'blk'), may hold values from 0.2 to 2
- velocity: float32 [2, 3, 256, 16, 256], P('star', None, 'blk'), may hold values from -0.5 to 0.5
- pressure: float32 [2, 256, 16, 256], P('star', 'blk'), may hold values from 0.05 to 0.5
Outputs:
- bssn_rhs: float32 [15, 256, 16, 256], P(None, ('star', 'blk'))
- hydro_rhs: float32 [2, 5, 256, 16, 256], P('star', None, 'blk')
Inputs may be any that keep to these rules, and one draw needn't show every extreme that they name: `conformal_metric`: in every cell the symmetric matrix with rows (xx, xy, xz), (xy, yy, yz), (xz, yz, zz) has diagonal entries from 0.8 to 1.6 and off-diagonal entries from -0.3 to 0.3, and each diagonal entry exceeds the sum of the magnitudes of the other entries of its row.
All inputs are finite; a program needn't handle non-finite values.
Results may differ from a plain program's by a relative error of at most 0.0003.
Values sent between devices are 32-bit elements; how exact they have to be, the bound alone decides.
No kernel may reach another device: no remote copies, remote signals or barrier semaphores. Data moves between devices by JAX's collectives and lax.ppermute only.
A program may use at most 128 MiB of HBM per device.

v0:
```python
from functools import reduce
import math

import jax
import jax.numpy as jnp
from jax import lax
from jax.sharding import PartitionSpec as P

pair_index = ((0, 1, 2), (1, 3, 4), (2, 4, 5))
sym_pairs = ((0, 0), (0, 1), (0, 2), (1, 1), (1, 2), (2, 2))
weno_eps = 1e-06


def extended(array, sides, width, wrap):
    for axis, dim in sides:
        count, length = (lax.axis_size(axis), array.shape[dim])
        up = [(i, (i + 1) % count) for i in range(count if wrap else count - 1)]
        down = [(j, i) for i, j in up]
        last = lax.slice_in_dim(array, length - width, length, axis=dim)
        leading = lax.slice_in_dim(array, 0, width, axis=dim)
        before = lax.ppermute(last, axis, up)
        after = lax.ppermute(leading, axis, down)
        array = jnp.concatenate([before, array, after], axis=dim)
    return array


def passed_along(value, axis, steps):
    count = lax.axis_size(axis)
    pairs = [(source, (source + steps) % count) for source in range(count)]
    return lax.ppermute(value, axis, pairs)


def from_behind(array, axis, by):
    count = lax.axis_size(axis)
    pairs = [(i, i + by) for i in range(count) if 0 <= i + by < count]
    return lax.ppermute(array, axis, pairs)


def accumulate(terms):
    return reduce(lambda x, y: x + y, terms)


def xfirst(values):
    return (
        values[..., 0:-4, :, :]
        - 8.0 * values[..., 1:-3, :, :]
        + 8.0 * values[..., 3:-1, :, :]
        - values[..., 4:, :, :]
    ) / 12.0


def xsecond(values):
    return (
        -values[..., 0:-4, :, :]
        + 16.0 * values[..., 1:-3, :, :]
        - 30.0 * values[..., 2:-2, :, :]
        + 16.0 * values[..., 3:-1, :, :]
        - values[..., 4:, :, :]
    ) / 12.0


def rfirst(values, direction):
    return (
        jnp.roll(values, 2, direction)
        - 8.0 * jnp.roll(values, 1, direction)
        + 8.0 * jnp.roll(values, -1, direction)
        - jnp.roll(values, -2, direction)
    ) / 12.0


def rsecond(values, direction):
    return (
        -jnp.roll(values, 2, direction)
        + 16.0 * jnp.roll(values, 1, direction)
        - 30.0 * values
        + 16.0 * jnp.roll(values, -1, direction)
        - jnp.roll(values, -2, direction)
    ) / 12.0


def bssn_rates(padded, sources):
    core_cells = padded[:, 2:-2]
    gradients = (xfirst(padded), rfirst(core_cells, -2), rfirst(core_cells, -1))
    lapse_core = core_cells[0]
    conf_core = core_cells[1]
    mean_core = core_cells[2]
    shift_core = core_cells[15:18]
    advected = (
        shift_core[0] * gradients[0][:15]
        + shift_core[1] * gradients[1][:15]
        + shift_core[2] * gradients[2][:15]
    )

    def metric_at(i, j):
        return core_cells[3 + pair_index[i][j]]

    def curv_at(i, j):
        return core_cells[9 + pair_index[i][j]]

    def dshift(k, i):
        return gradients[k][15 + i]

    div_shift = dshift(0, 0) + dshift(1, 1) + dshift(2, 2)
    a, b, c, d, e, f = [core_cells[3 + n] for n in range(6)]
    cofactor = (
        d * f - e * e,
        c * e - b * f,
        b * e - c * d,
        a * f - c * c,
        b * c - a * e,
        a * d - b * b,
    )
    determ = a * cofactor[0] + b * cofactor[1] + c * cofactor[2]
    inverse = [entry / determ for entry in cofactor]

    def inverse_at(i, j):
        return inverse[pair_index[i][j]]

    lapse_pad = padded[0]
    hessian = (
        xsecond(lapse_pad),
        xfirst(rfirst(lapse_pad, -2)),
        xfirst(rfirst(lapse_pad, -1)),
        rsecond(lapse_core, -2),
        rfirst(rfirst(lapse_core, -1), -2),
        rsecond(lapse_core, -1),
    )

    def hess_at(i, j):
        return hessian[pair_index[i][j]]

    trace_hess = accumulate([inverse_at(i, j) * hess_at(i, j) for i in range(3) for j in range(3)])
    mixed_curv = [
        [accumulate([curv_at(i, l) * inverse_at(l, j) for l in range(3)]) for j in range(3)]
        for i in range(3)
    ]
    square_trace = accumulate(
        [mixed_curv[i][j] * mixed_curv[j][i] for i in range(3) for j in range(3)]
    )
    lapse_rate = advected[0] - 2.0 * lapse_core * mean_core
    conf_rate = advected[1] + 2.0 / 3.0 * conf_core * (lapse_core * mean_core - div_shift)
    mean_rate = (
        advected[2]
        - conf_core * trace_hess
        + lapse_core * (square_trace + mean_core * mean_core / 3.0)
        + 4.0 * math.pi * lapse_core * sources[0]
    )
    metric_rates = []
    curv_rates = []
    for p, (i, j) in enumerate(sym_pairs):
        moved_metric = accumulate(
            [metric_at(i, k) * dshift(j, k) + metric_at(j, k) * dshift(i, k) for k in range(3)]
        )
        metric_rates.append(
            advected[3 + p]
            - 2.0 * lapse_core * curv_at(i, j)
            + moved_metric
            - 2.0 / 3.0 * metric_at(i, j) * div_shift
        )
        moved_curv = accumulate(
            [curv_at(i, k) * dshift(j, k) + curv_at(j, k) * dshift(i, k) for k in range(3)]
        )
        product = accumulate([mixed_curv[i][k] * curv_at(k, j) for k in range(3)])
        curv_rates.append(
            advected[9 + p]
            + lapse_core * (mean_core * curv_at(i, j) - 2.0 * product)
            + moved_curv
            - 2.0 / 3.0 * curv_at(i, j) * div_shift
            - conf_core * (hess_at(i, j) - trace_hess * metric_at(i, j) / 3.0)
        )
    return jnp.stack([lapse_rate, conf_rate, mean_rate] + metric_rates + curv_rates, 0)


def restrict(fine_cells):
    leading = fine_cells.shape[:-3]
    extent_x, extent_y, extent_z = fine_cells.shape[-3:]
    blocks = fine_cells.reshape(leading + (extent_x // 2, 2, extent_y // 2, 2, extent_z // 2, 2))
    return jnp.sum(blocks, axis=(-5, -3, -1)) * 0.125


def refine_axis(coarse, axis_index):
    cell_count = coarse.shape[axis_index] - 2
    center = lax.slice_in_dim(coarse, 1, cell_count + 1, axis=axis_index)
    lower_side = lax.slice_in_dim(coarse, 0, cell_count, axis=axis_index)
    upper_side = lax.slice_in_dim(coarse, 2, cell_count + 2, axis=axis_index)
    even_cells = 0.75 * center + 0.25 * lower_side
    odd_cells = 0.75 * center + 0.25 * upper_side
    stacked = jnp.stack([even_cells, odd_cells], axis_index + 1)
    new_shape = coarse.shape[:axis_index] + (2 * cell_count,) + coarse.shape[axis_index + 1 :]
    return stacked.reshape(new_shape)


def prolong(window):
    return refine_axis(refine_axis(refine_axis(window, 1), 2), 3)


def split_fluxes(conserved, velocity, pressure, fine_metric):
    lapse_fine = fine_metric[0]
    shift_fine = fine_metric[1]
    conf_fine = fine_metric[2]
    transport = lapse_fine * velocity[0] - shift_fine
    weight = lapse_fine * conf_fine ** (-1.5) * pressure
    flux_terms = jnp.stack(
        [
            conserved[0] * transport,
            conserved[1] * transport + weight,
            conserved[2] * transport,
            conserved[3] * transport,
            conserved[4] * transport + weight * velocity[0],
        ],
        0,
    )
    max_speed = lapse_fine + jnp.abs(shift_fine)
    return jnp.concatenate(
        [0.5 * (flux_terms + max_speed * conserved), 0.5 * (flux_terms - max_speed * conserved)], 0
    )


def weno_value(left_two, left_one, middle, right_one, right_two):
    guess_one = (2.0 * left_two - 7.0 * left_one + 11.0 * middle) / 6.0
    guess_two = (-left_one + 5.0 * middle + 2.0 * right_one) / 6.0
    guess_three = (2.0 * middle + 5.0 * right_one - right_two) / 6.0
    smooth_one = (
        13.0 / 12.0 * (left_two - 2.0 * left_one + middle) ** 2
        + 0.25 * (left_two - 4.0 * left_one + 3.0 * middle) ** 2
    )
    smooth_two = (
        13.0 / 12.0 * (left_one - 2.0 * middle + right_one) ** 2
        + 0.25 * (left_one - right_one) ** 2
    )
    smooth_three = (
        13.0 / 12.0 * (middle - 2.0 * right_one + right_two) ** 2
        + 0.25 * (3.0 * middle - 4.0 * right_one + right_two) ** 2
    )
    weight_one = 0.1 / (weno_eps + smooth_one) ** 2
    weight_two = 0.6 / (weno_eps + smooth_two) ** 2
    weight_three = 0.3 / (weno_eps + smooth_three) ** 2
    return (weight_one * guess_one + weight_two * guess_two + weight_three * guess_three) / (
        weight_one + weight_two + weight_three
    )


def weno_rates(ghosts):
    cell_count = ghosts.shape[1] - 6
    plus_part = ghosts[:5]
    minus_part = ghosts[5:]

    def taps(values, start):
        return values[:, start : start + cell_count + 1]

    face_flux = weno_value(
        taps(plus_part, 0),
        taps(plus_part, 1),
        taps(plus_part, 2),
        taps(plus_part, 3),
        taps(plus_part, 4),
    ) + weno_value(
        taps(minus_part, 5),
        taps(minus_part, 4),
        taps(minus_part, 3),
        taps(minus_part, 2),
        taps(minus_part, 1),
    )
    return (face_flux[:, :-1] - face_flux[:, 1:]) * 2.0


def on_device(
    lapse_field,
    conformal,
    mean_curv,
    conformal_metric,
    traceless_curv,
    shift_vector,
    density,
    momentum,
    energy,
    velocity,
    pressure,
):
    metric_state = jnp.concatenate(
        [
            lapse_field[None],
            conformal[None],
            mean_curv[None],
            conformal_metric,
            traceless_curv,
            shift_vector,
        ],
        0,
    )
    extent_x = lapse_field.shape[0]
    extent_y = lapse_field.shape[1]
    extent_z = lapse_field.shape[2]
    conserved = jnp.concatenate([density[:, None], momentum, energy[:, None]], 1)[0]
    source_fine = (
        energy
        + density
        + (
            momentum[:, 0] * velocity[:, 0]
            + momentum[:, 1] * velocity[:, 1]
            + momentum[:, 2] * velocity[:, 2]
        )
        + 3.0 * pressure
    )
    source_coarse = restrict(source_fine)
    footprint = ((0, 0), (0, 0), (extent_y // 4, extent_y // 4), (extent_z // 4, extent_z // 4))
    padded = extended(metric_state, ((("star", "blk"), 1),), 2, True)
    upper_plane = passed_along(source_coarse[:, extent_x - 1 :], ("star", "blk"), 1)
    sources = jnp.pad(
        jnp.concatenate([upper_plane, source_coarse[:, : extent_x - 1]], 1), footprint
    )
    bssn_rhs = bssn_rates(padded, sources)
    window = jnp.stack([padded[0], padded[15], padded[1]], 0)
    window = window[
        :, :, extent_y // 4 - 1 : 3 * extent_y // 4 + 1, extent_z // 4 - 1 : 3 * extent_z // 4 + 1
    ]
    upper_layers = from_behind(window[:, 4:6], ("star", "blk"), -1)
    coarse_wide = jnp.concatenate([window, upper_layers], 1)
    fine_wide = prolong(coarse_wide)[:, 1 : 2 * extent_x + 7]
    fluid = jnp.concatenate([conserved, velocity[0, :1], pressure], 0)
    fluid_wide = extended(fluid, (("blk", 1),), 3, False)
    ghosts = split_fluxes(fluid_wide[:5], fluid_wide[5:6], fluid_wide[6], fine_wide)
    hydro_rhs = weno_rates(ghosts)[None]
    return (bssn_rhs, hydro_rhs)


def solution(mesh):
    in_specs = (
        P(("star", "blk"), None, None),
        P(("star", "blk"), None, None),
        P(("star", "blk"), None, None),
        P(None, ("star", "blk"), None, None),
        P(None, ("star", "blk"), None, None),
        P(None, ("star", "blk"), None, None),
        P("star", "blk", None, None),
        P("star", None, "blk", None, None),
        P("star", "blk", None, None),
        P("star", None, "blk", None, None),
        P("star", "blk", None, None),
    )
    out_specs = (P(None, ("star", "blk"), None, None), P("star", None, "blk", None, None))
    return jax.shard_map(
        on_device, mesh=mesh, in_specs=in_specs, out_specs=out_specs, check_vma=False
    )
```

profile of v0, /device:TPU:29, one launch (start us, length us, event | category | flops | bytes accessed | tf_op | source)
XLA Modules:
  0.0 126.3 jit_solution(13968704860325151483)
XLA Ops:
  3.5 1.2 constant_dynamic-update-slice_fusion.2
  6.7 4.7 %collective-permute-start = (f32[18,2,16,256]{3,2,1,0:T(8,128)}, f32[18,2,16,256]{3,2,1,0:T(8,128)}, u32[]{:S(2)}, u32[]{:S(2)}) collective-permute-start(f32[18,2,16,256]{3,2,1,0:T(8,128)} %get-tuple-element.40), channel_id=1, source_target_pairs={{0,1},{1,2},{2,3},{3,4},{4,5},{5,6},{6,7},{7,8},{8,9},{9,10},{10,1... | collective-permute-start | bytes 1769480 | tf_op jit(solution)/shard_map/ppermute | solution.py:21
  12.4 18.8 %reshape.109 = f32[8,2,8,2,128,2]{5,4,3,2,1,0:T(8,128)} reshape(f32[1,16,16,256]{3,2,1,0:T(8,128)} %fusion.44) | data formatting | bytes 524288 | tf_op jit(solution)/shard_map/reshape | solution.py:177
  31.2 7.0 %reduce_sum.9 = f32[8,8,128]{2,1,0:T(8,128)S(1)} reduce(f32[8,2,8,2,128,2]{5,4,3,2,1,0:T(8,128)} %reshape.109, f32[]{:T(128)} %constant.35.clone.1), dimensions={1,3,5}, to_apply=%region_0.0 | reduce | flops 57344 | bytes 294916 | tf_op jit(solution)/shard_map/reduce_sum | solution.py:178
  39.8 1.5 %maximum_bitcast_fusion = f32[5,16,16,256]{3,2,1,0:T(8,128)S(1)} fusion(f32[1,1,16,16,256]{4,3,2,1,0:T(8,128)} %bitcast.1211, f32[1,3,16,16,256]{4,3,2,1,0:T(8,128)} %param.18, f32[1,1,16,16,256]{4,3,2,1,0:T(8,128)} %bitcast.1212), kind=kLoop, calls=%fused_computation.47 | loop fusion | flops 655360 | bytes 2621440 | tf_op jit(solution)/shard_map/squeeze | solution.py:294
  42.2 3.1 %collective-permute-start.4 = (f32[7,3,16,256]{3,2,1,0:T(8,128)}, f32[7,3,16,256]{3,2,1,0:T(8,128)}, u32[]{:S(2)}, u32[]{:S(2)}) collective-permute-start(f32[7,3,16,256]{3,2,1,0:T(8,128)} %get-tuple-element.59), channel_id=1, source_target_pairs={{1,0},{2,1},{3,2},{4,3},{5,4},{6,5},{7,6},{8,7},{9,8},{10,9},{11,1... | collective-permute-start | bytes 1032200 | tf_op jit(solution)/shard_map/ppermute | solution.py:22
  45.3 1.5 %collective-permute-start.3 = (f32[7,3,16,256]{3,2,1,0:T(8,128)}, f32[7,3,16,256]{3,2,1,0:T(8,128)}, u32[]{:S(2)}, u32[]{:S(2)}) collective-permute-start(f32[7,3,16,256]{3,2,1,0:T(8,128)} %get-tuple-element.58), channel_id=1, source_target_pairs={{0,1},{1,2},{2,3},{3,4},{4,5},{5,6},{6,7},{7,8},{8,9},{9,10},{10,1... | collective-permute-start | bytes 1032200 | tf_op jit(solution)/shard_map/ppermute | solution.py:21
  50.0 1.8 %fusion.318 = (f32[18,8,16,2]{3,2,1,0:T(8,128)}, f32[18,8,16,2]{3,2,1,0:T(8,128)}) fusion(f32[18,8,16,256]{3,2,1,0:T(8,128)S(1)} %constant_dynamic-update-slice_fusion), kind=kLoop, calls=%fused_computation.568 | loop fusion | bytes 73728 | tf_op jit(solution)/shard_map/jit(_roll_static)/slice | solution.py:67
  51.9 2.3 %fusion.317 = (f32[18,8,16,254]{3,2,1,0:T(8,128)S(1)}, f32[18,8,16,254]{3,2,1,0:T(8,128)}) fusion(f32[18,8,16,256]{3,2,1,0:T(8,128)S(1)} %constant_dynamic-update-slice_fusion), kind=kLoop, calls=%fused_computation.567 | loop fusion | bytes 9363456 | tf_op jit(solution)/shard_map/jit(_roll_static)/slice | solution.py:67
  54.2 1.9 %fusion.320 = (f32[18,8,16,1]{3,2,1,0:T(8,128)}, f32[18,8,16,1]{3,2,1,0:T(8,128)}) fusion(f32[18,8,16,256]{3,2,1,0:T(8,128)S(1)} %constant_dynamic-update-slice_fusion), kind=kLoop, calls=%fused_computation.570 | loop fusion | bytes 36864 | tf_op jit(solution)/shard_map/jit(_roll_static)/slice | solution.py:66
  56.1 3.0 %fusion.319 = (f32[18,8,16,255]{3,2,1,0:T(8,128)}, f32[18,8,16,255]{3,2,1,0:T(8,128)}) fusion(f32[18,8,16,256]{3,2,1,0:T(8,128)S(1)} %constant_dynamic-update-slice_fusion), kind=kLoop, calls=%fused_computation.569 | loop fusion | bytes 9400320 | tf_op jit(solution)/shard_map/jit(_roll_static)/slice | solution.py:66
  63.6 7.0 %fusion.12 = (f32[18,8,16,256]{3,2,1,0:T(8,128)S(1)}, f32[18,8,16,256]{3,2,1,0:T(8,128)S(1)}) fusion(f32[18,8,14,256]{3,2,1,0:T(8,128)S(1)} %get-tuple-element.43, f32[18,8,2,256]{3,2,1,0:T(2,128)} %get-tuple-element.45, f32[18,8,15,256]{3,2,1,0:T(8,128)S(1)} %get-tuple-element.47, f32[18,8,1,256]{3,2,1,0:T(1,128)} %get-tuple-element.49, ...), kind=kLoop, calls=%fused_computation.26 | loop fusion | flops 11796480 | bytes 23592960 | tf_op jit(solution)/shard_map/div | solution.py:63
  70.7 3.0 %pad_maximum_fusion = f32[7,22,16,256]{3,2,1,0:T(8,128)} fusion(f32[7,3,16,256]{3,2,1,0:T(8,128)} %collective-permute-done.4, f32[1,16,16,256]{3,2,1,0:T(8,128)S(1)} %copy-done.7, f32[1,16,16,256]{3,2,1,0:T(8,128)} %copy-done.8, f32[5,16,16,256]{3,2,1,0:T(8,128)S(1)} %maximum_bitcast_fusion, f32[7,3,16,256]{3,2,1,0:T(8,128)} %collective-permute-done.3), kind=kLoop, calls=%fused_computation.12 | loop fusion | flops 2523136 | bytes 5046272 | tf_op jit(solution)/shard_map/concatenate | solution.py:23
  75.9 2.4 %fusion.4 = f32[18,8,16,256]{3,2,1,0:T(8,128)S(1)} fusion(f32[18,8,16,256]{3,2,1,0:T(8,128)S(1)} %constant_dynamic-update-slice_fusion, f32[18,2,16,256]{3,2,1,0:T(8,128)} %collective-permute-done.1, f32[18,2,16,256]{3,2,1,0:T(8,128)} %collective-permute-done), kind=kLoop, calls=%fused_computation.17 | loop fusion | flops 5898240 | bytes 5898240 | tf_op jit(solution)/shard_map/div | solution.py:44
  80.8 1.8 %fusion.124 = (f32[15,8,16,256]{3,2,1,0:T(8,128)S(1)}, f32[8,16,256]{2,1,0:T(8,128)S(1)}, f32[8,16,256]{2,1,0:T(8,128)S(1)}, f32[8,16,256]{2,1,0:T(8,128)S(1)}, ...) fusion(f32[15,8,16,256]{3,2,1,0:T(8,128)S(1)} %get-tuple-elemen, ...), kind=kLoop, calls=%fused_computation.217 | loop fusion | flops 5242880 | bytes 11665408
  84.8 3.3 %collective-permute-start.5 = (f32[3,2,10,130]{3,2,1,0:T(8,128)S(1)}, f32[3,2,10,130]{3,2,1,0:T(8,128)S(1)}, u32[]{:S(2)}, u32[]{:S(2)}) collective-permute-start(f32[3,2,10,130]{3,2,1,0:T(8,128)S(1)} %slice.1039), channel_id=1, source_target_pairs={{1,0},{2,1},{3,2},{4,3},{5,4},{6,5},{7,6},{8,7},{9,8},{10,9},{11,1... | collective-permute-start | bytes 93608 | tf_op jit(solution)/shard_map/ppermute | solution.py:36
  90.2 4.2 %collective-permute-done.5 = f32[3,2,10,130]{3,2,1,0:T(8,128)S(1)} collective-permute-done((f32[3,2,10,130]{3,2,1,0:T(8,128)S(1)}, f32[3,2,10,130]{3,2,1,0:T(8,128)S(1)}, u32[]{:S(2)}, u32[]{:S(2)}) %collective-permute-start.5) | collective-permute-done | bytes 31232 | tf_op jit(solution)/shard_map/ppermute | solution.py:36
  96.6 5.9 %copy.76 = f32[3,24,16,128,2]{1,2,4,3,0:T(8,128)} copy(f32[3,24,16,128,2]{3,1,2,0,4:T(8,128)S(1)} %pad_maximum_fusion.3) | data formatting | bytes 2359296 | tf_op jit(solution)/shard_map/stack | solution.py:188
  102.5 6.6 %fusion.311 = (f32[1,22,16,256]{1,2,3,0:T(8,128)}, f32[1,22,16,256]{1,2,3,0:T(8,128)S(1)}, f32[1,22,16,256]{1,2,3,0:T(8,128)}) fusion(f32[3,24,16,256]{1,2,3,0:T(8,128)} %bitcast.1209), kind=kLoop, calls=%fused_computation.561 | loop fusion | bytes 2162688 | tf_op jit(solution)/shard_map/slice | solution.py:200
  109.1 1.9 %copy.82 = f32[1,22,16,256]{3,2,1,0:T(8,128)} copy(f32[1,22,16,256]{1,2,3,0:T(8,128)S(1)} %get-tuple-element.36) | data formatting | bytes 720896
  111.0 2.8 %copy.81 = f32[1,22,16,256]{3,2,1,0:T(8,128)S(1)} copy(f32[1,22,16,256]{1,2,3,0:T(8,128)} %get-tuple-element.37) | data formatting | bytes 720896
  113.8 2.6 %copy.83 = f32[1,22,16,256]{3,2,1,0:T(8,128)S(1)} copy(f32[1,22,16,256]{1,2,3,0:T(8,128)} %get-tuple-element.35) | data formatting | bytes 720896
  118.8 6.2 %divide_add_fusion = f32[5,17,16,256]{3,2,1,0:T(8,128)S(1)} fusion(f32[5,22,16,256]{3,2,1,0:T(8,128)S(1)} %get-tuple-element.39, f32[5,22,16,256]{3,2,1,0:T(8,128)S(1)} %get-tuple-element.38), kind=kLoop, calls=%fused_computation.43 | loop fusion | flops 44912640 | bytes 15319040 | tf_op jit(solution)/shard_map/add | solution.py:251
  125.1 1.2 fusion.19
  (168 shorter events, 29.0 us)
Async XLA Ops:
  0.6 4.1 %copy-start.2 = (f32[6,8,16,256]{3,2,1,0:T(8,128)S(1)}, f32[6,8,16,256]{3,2,1,0:T(8,128)}, u32[]{:S(2)}) copy-start(f32[6,8,16,256]{3,2,1,0:T(8,128)} %param.15) | copy-start | bytes 2359300
  0.6 4.1 %copy-start.9 = (f32[3,8,16,256]{3,2,1,0:T(8,128)S(1)}, f32[3,8,16,256]{3,2,1,0:T(8,128)}, u32[]{:S(2)}) copy-start(f32[3,8,16,256]{3,2,1,0:T(8,128)} %param.16) | copy-start | bytes 1179652
  4.8 6.6 %copy-start.6 = (f32[1,3,16,16,256]{4,3,2,1,0:T(8,128)S(1)}, f32[1,3,16,16,256]{4,3,2,1,0:T(8,128)}, u32[]{:S(2)}) copy-start(f32[1,3,16,16,256]{4,3,2,1,0:T(8,128)} %param.18) | copy-start | bytes 2359300
  4.8 6.6 %copy-start.7 = (f32[1,16,16,256]{3,2,1,0:T(8,128)S(1)}, f32[1,16,16,256]{3,2,1,0:T(8,128)}, u32[]{:S(2)}) copy-start(f32[1,16,16,256]{3,2,1,0:T(8,128)} %param.21) | copy-start | bytes 786436
  4.8 6.6 %copy-start.11 = (f32[1,3,16,16,256]{4,3,2,1,0:T(8,128)S(1)}, f32[1,3,16,16,256]{4,3,2,1,0:T(8,128)}, u32[]{:S(2)}) copy-start(f32[1,3,16,16,256]{4,3,2,1,0:T(8,128)} %param.20) | copy-start | bytes 2359300
  4.8 6.6 %copy-start.18 = (f32[1,16,16,256]{3,2,1,0:T(8,128)S(1)}, f32[1,16,16,256]{3,2,1,0:T(8,128)}, u32[]{:S(2)}) copy-start(f32[1,16,16,256]{3,2,1,0:T(8,128)} %param.19) | copy-start | bytes 786436
  4.8 6.5 %copy-start.19 = (f32[1,16,16,256]{3,2,1,0:T(8,128)S(1)}, f32[1,16,16,256]{3,2,1,0:T(8,128)}, u32[]{:S(2)}) copy-start(f32[1,16,16,256]{3,2,1,0:T(8,128)} %param.17) | copy-start | bytes 786436
  6.0 67.7 %collective-permute-start.1 = (f32[18,2,16,256]{3,2,1,0:T(8,128)}, f32[18,2,16,256]{3,2,1,0:T(8,128)}, u32[]{:S(2)}, u32[]{:S(2)}) collective-permute-start(f32[18,2,16,256]{3,2,1,0:T(8,128)} %get-tuple-element.41), channel_id=1, source_target_pairs={{1,0},{2,1},{3,2},{4,3},{5,4},{6,5},{7,6},{8,7},{9,8},{10,9},{11,1... | collective-permute-start | bytes 1769480 | tf_op jit(solution)/shard_map/ppermute | solution.py:22
  6.7 67.0 %collective-permute-start = (f32[18,2,16,256]{3,2,1,0:T(8,128)}, f32[18,2,16,256]{3,2,1,0:T(8,128)}, u32[]{:S(2)}, u32[]{:S(2)}) collective-permute-start(f32[18,2,16,256]{3,2,1,0:T(8,128)} %get-tuple-element.40), channel_id=1, source_target_pairs={{0,1},{1,2},{2,3},{3,4},{4,5},{5,6},{6,7},{7,8},{8,9},{9,10},{10,1... | collective-permute-start | bytes 1769480 | tf_op jit(solution)/shard_map/ppermute | solution.py:21
  38.2 32.4 %copy-start.39 = (f32[1,8,8,128]{3,2,1,0:T(8,128)}, f32[1,8,8,128]{3,2,1,0:T(8,128)S(1)}, u32[]{:S(2)}) copy-start(f32[1,8,8,128]{3,2,1,0:T(8,128)S(1)} %multiply_bitcast_fusion) | copy-start | bytes 98308
  38.8 41.0 %collective-permute-start.2 = (f32[1,1,8,128]{3,2,1,0:T(8,128)}, f32[1,1,8,128]{3,2,1,0:T(8,128)S(1)}, u32[]{:S(2)}, u32[]{:S(2)}) collective-permute-start(f32[1,1,8,128]{3,2,1,0:T(8,128)} %slice.1017), channel_id=1, source_target_pairs={{0,1},{1,2},{2,3},{3,4},{4,5},{5,6},{6,7},{7,8},{8,9},{9,10},{10,1... | collective-permute-start | bytes 12296 | tf_op jit(solution)/shard_map/ppermute | solution.py:30
  42.2 28.5 %collective-permute-start.4 = (f32[7,3,16,256]{3,2,1,0:T(8,128)}, f32[7,3,16,256]{3,2,1,0:T(8,128)}, u32[]{:S(2)}, u32[]{:S(2)}) collective-permute-start(f32[7,3,16,256]{3,2,1,0:T(8,128)} %get-tuple-element.59), channel_id=1, source_target_pairs={{1,0},{2,1},{3,2},{4,3},{5,4},{6,5},{7,6},{8,7},{9,8},{10,9},{11,1... | collective-permute-start | bytes 1032200 | tf_op jit(solution)/shard_map/ppermute | solution.py:22
  45.3 25.4 %collective-permute-start.3 = (f32[7,3,16,256]{3,2,1,0:T(8,128)}, f32[7,3,16,256]{3,2,1,0:T(8,128)}, u32[]{:S(2)}, u32[]{:S(2)}) collective-permute-start(f32[7,3,16,256]{3,2,1,0:T(8,128)} %get-tuple-element.58), channel_id=1, source_target_pairs={{0,1},{1,2},{2,3},{3,4},{4,5},{5,6},{6,7},{7,8},{8,9},{9,10},{10,1... | collective-permute-start | bytes 1032200 | tf_op jit(solution)/shard_map/ppermute | solution.py:21
  56.1 3.0 %copy-start.10 = (f32[3,8,16,256]{3,2,1,0:T(8,128)S(1)}, f32[3,8,16,256]{3,2,1,0:T(8,128)}, u32[]{:S(2)}) copy-start(f32[3,8,16,256]{3,2,1,0:T(8,128)} %param.16) | copy-start | bytes 1179652
  56.1 3.8 %copy-start.1 = (f32[6,8,16,256]{3,2,1,0:T(8,128)S(1)}, f32[6,8,16,256]{3,2,1,0:T(8,128)}, u32[]{:S(2)}) copy-start(f32[6,8,16,256]{3,2,1,0:T(8,128)} %param.14) | copy-start | bytes 2359300
  60.8 2.7 %copy-start.20 = (f32[8,16,2]{2,1,0:T(8,128)}, f32[8,16,2]{2,1,0:T(8,128)S(1)}, u32[]{:S(2)}) copy-start(f32[8,16,2]{2,1,0:T(8,128)S(1)} %get-tuple-element.94) | copy-start | bytes 3076
  60.8 2.7 %copy-start.22 = (f32[8,16,2]{2,1,0:T(8,128)}, f32[8,16,2]{2,1,0:T(8,128)S(1)}, u32[]{:S(2)}) copy-start(f32[8,16,2]{2,1,0:T(8,128)S(1)} %get-tuple-element.95) | copy-start | bytes 3076
  60.9 2.6 %copy-start.12 = (f32[8,16,254]{2,1,0:T(8,128)}, f32[8,16,254]{2,1,0:T(8,128)S(1)}, u32[]{:S(2)}) copy-start(f32[8,16,254]{2,1,0:T(8,128)S(1)} %get-tuple-element.97) | copy-start | bytes 390148
  61.0 2.6 %copy-start.24 = (f32[8,16,1]{2,1,0:T(8,128)}, f32[8,16,1]{2,1,0:T(8,128)S(1)}, u32[]{:S(2)}) copy-start(f32[8,16,1]{2,1,0:T(8,128)S(1)} %get-tuple-element.98) | copy-start | bytes 1540
  61.0 2.6 %copy-start.26 = (f32[8,16,1]{2,1,0:T(8,128)}, f32[8,16,1]{2,1,0:T(8,128)S(1)}, u32[]{:S(2)}) copy-start(f32[8,16,1]{2,1,0:T(8,128)S(1)} %get-tuple-element.99) | copy-start | bytes 1540
  61.1 2.5 %copy-start.14 = (f32[8,16,255]{2,1,0:T(8,128)}, f32[8,16,255]{2,1,0:T(8,128)S(1)}, u32[]{:S(2)}) copy-start(f32[8,16,255]{2,1,0:T(8,128)S(1)} %get-tuple-element.100) | copy-start | bytes 391684
  84.8 9.5 %collective-permute-start.5 = (f32[3,2,10,130]{3,2,1,0:T(8,128)S(1)}, f32[3,2,10,130]{3,2,1,0:T(8,128)S(1)}, u32[]{:S(2)}, u32[]{:S(2)}) collective-permute-start(f32[3,2,10,130]{3,2,1,0:T(8,128)S(1)} %slice.1039), channel_id=1, source_target_pairs={{1,0},{2,1},{3,2},{4,3},{5,4},{6,5},{7,6},{8,7},{9,8},{10,9},{11,1... | collective-permute-start | bytes 93608 | tf_op jit(solution)/shard_map/ppermute | solution.py:36
  89.9 4.7 %copy-start.43 = (f32[15,8,16,256]{3,2,1,0:T(8,128)}, f32[15,8,16,256]{3,2,1,0:T(8,128)S(1)}, u32[]{:S(2)}) copy-start(f32[15,8,16,256]{3,2,1,0:T(8,128)S(1)} %fusion.59) | copy-start | bytes 5898244
  111.0 5.4 %copy-start.3 = (f32[7,22,16,256]{3,2,1,0:T(8,128)S(1)}, f32[7,22,16,256]{3,2,1,0:T(8,128)}, u32[]{:S(2)}) copy-start(f32[7,22,16,256]{3,2,1,0:T(8,128)} %pad_maximum_fusion) | copy-start | bytes 7569412
  (27 other events, 38.4 us)
where the time goes:
time: 127 us; the launch traced here: 126 us
  local copies, waits for them, and re-layouts  63.7 us (50%)
  other arithmetic  43.7 us (34%)
  starting transfers between devices  13.2 us (10%)
  waiting for transfers between devices  4.22 us (3%)
  between operations  1.5 us (1%)
    reshape x1, local copies, waits for them, and re-layouts, restrict(): fine_cells.reshape(leading + (extent_x // 2, 2, extent_y // 2, 2, extent_...  18.8 us
    unnamed x96, local copies, waits for them, and re-layouts  12.6 us
    div x3, other arithmetic, rfirst(): (jnp.roll(values, 2, direction) - 8.0 * jnp.roll(values, 1, direction) +...  7.47 us
    reduce_sum x1, other arithmetic, restrict(): return jnp.sum(blocks, axis=(-5, -3, -1)) * 0.125  6.98 us
    slice x8, local copies, waits for them, and re-layouts, rfirst(): jnp.roll(values, -1, direction)  6.72 us
    another operation x3, local copies, waits for them, and re-layouts, refine_axis(): stacked = jnp.stack([even_cells, odd_cells], axis_index + 1)  6.63 us
    slice x1, local copies, waits for them, and re-layouts, split_fluxes(): conf_fine = fine_metric[2]  6.62 us
    add x1, other arithmetic, weno_rates(): weno_value(taps(plus_part, 0), taps(plus_part, 1), taps(plus_part, 2), ta...  6.25 us
  transfers between devices with their start and end apart: 6, of which 1 were waited for; matrix products, arithmetic and copies ran while one was open for 52% of the time, Pallas kernels for 0%

commit v1 on v0

v1 whole, which is shorter than its diff:
```python
import functools
import math

import jax
import jax.numpy as jnp
from jax import lax
from jax.experimental import pallas as pl
from jax.experimental.pallas import tpu as pltpu
from jax.sharding import PartitionSpec as P

pair_index = ((0, 1, 2), (1, 3, 4), (2, 4, 5))
sym_pairs = ((0, 0), (0, 1), (0, 2), (1, 1), (1, 2), (2, 2))
weno_eps = 1e-06
RING = ("star", "blk")
LANES = 128
METRIC = 18
FLUID = 7
ANY = pl.BlockSpec(memory_space=pl.ANY)
F32 = jnp.float32


class Copies:
    def __init__(self, sems):
        self.sems = sems
        self.count = 0
        self.groups = {}

    def start(self, group, src, dst):
        copy = pltpu.make_async_copy(src, dst, self.sems.at[self.count])
        copy.start()
        self.count += 1
        self.groups.setdefault(group, []).append(copy)

    def wait(self, group):
        for copy in self.groups.pop(group):
            copy.wait()

    def wait_all(self):
        for group in list(self.groups):
            self.wait(group)


def metric_pieces(lapse, conf, mean, metric, curv, shift):
    singles = [(n, None, ref) for n, ref in enumerate((lapse, conf, mean))]
    return singles + [(3, 6, metric), (9, 6, curv), (15, 3, shift)]


def pack_kernel(lapse, conf, mean, metric, curv, shift, dens, mom, ener, velo, pres, up, down, sems):
    nx = lapse.shape[0]
    fx = dens.shape[1]
    copies = Copies(sems)
    for buf, first, fluid_first in ((up, nx - 2, fx - 3), (down, 0, 0)):
        for k in range(2):
            for field, count, ref in metric_pieces(lapse, conf, mean, metric, curv, shift):
                at = k * METRIC + field
                if count is None:
                    copies.start(0, ref.at[first + k], buf.at[at])
                else:
                    copies.start(0, ref.at[:, first + k], buf.at[pl.ds(at, count)])
        for k in range(3):
            at = 2 * METRIC + k * FLUID
            row = fluid_first + k
            copies.start(0, dens.at[0, row], buf.at[at])
            copies.start(0, mom.at[0, :, row], buf.at[pl.ds(at + 1, 3)])
            copies.start(0, ener.at[0, row], buf.at[at + 4])
            copies.start(0, velo.at[0, 0, row], buf.at[at + 5])
            copies.start(0, pres.at[0, row], buf.at[at + 6])
    tail = 2 * METRIC + 3 * FLUID
    for k in range(2):
        copies.start(0, velo.at[0, pl.ds(1, 2), fx - 2 + k], up.at[pl.ds(tail + 2 * k, 2)])
    copies.start(0, lapse.at[2], down.at[tail])
    copies.start(0, shift.at[0, 2], down.at[tail + 1])
    copies.start(0, conf.at[2], down.at[tail + 2])
    copies.wait_all()


def bssn_layer(state, sources, out, at, src_at, out_at):
    ny, nz = state.shape[-2:]

    def value(field, off=0):
        return state[field, at + off]

    def rolled(v, axis):
        n = (ny, nz)[axis]
        return tuple(pltpu.roll(v, s % n, axis) for s in (2, 1, -1, -2))

    def first(taps):
        m2, m1, p1, p2 = taps
        return (m2 - p2) + 8.0 * (p1 - m1)

    def second(taps, mid):
        m2, m1, p1, p2 = taps
        return 16.0 * (m1 + p1) - (m2 + p2) - 30.0 * mid

    def xtaps(field):
        return tuple(value(field, o) for o in (-2, -1, 1, 2))

    twelfth = 1.0 / 12.0
    third = 1.0 / 3.0
    lapse = value(0)
    conf = value(1)
    mean = value(2)
    shift12 = [value(15 + n) * twelfth for n in range(3)]

    def gradient(field):
        v = value(field)
        return first(xtaps(field)), first(rolled(v, 0)), first(rolled(v, 1))

    def along_shift(field):
        gx, gy, gz = gradient(field)
        return shift12[0] * gx + shift12[1] * gy + shift12[2] * gz

    dshift = [[None] * 3 for _ in range(3)]
    for n in range(3):
        for k, g in enumerate(gradient(15 + n)):
            dshift[k][n] = g * twelfth
    div_shift = dshift[0][0] + dshift[1][1] + dshift[2][2]
    div23 = (2.0 / 3.0) * div_shift

    taps_x = xtaps(0)
    taps_y = rolled(lapse, 0)
    taps_z = rolled(lapse, 1)
    lx, ly, lz = first(taps_x), first(taps_y), first(taps_z)
    out[0, out_at] = (shift12[0] * lx + shift12[1] * ly + shift12[2] * lz) - 2.0 * lapse * mean
    sq = twelfth * twelfth
    hess = (
        second(taps_x, lapse) * twelfth,
        first(rolled(lx, 0)) * sq,
        first(rolled(lx, 1)) * sq,
        second(taps_y, lapse) * twelfth,
        first(rolled(lz, 0)) * sq,
        second(taps_z, lapse) * twelfth,
    )
    out[1, out_at] = along_shift(1) + conf * ((2.0 / 3.0) * (lapse * mean) - div23)

    a, b, c, d, e, f = g = [value(3 + n) for n in range(6)]
    cof = (d * f - e * e, c * e - b * f, b * e - c * d, a * f - c * c, b * c - a * e, a * d - b * b)
    scale = 1.0 / (a * cof[0] + b * cof[1] + c * cof[2])
    inv = [entry * scale for entry in cof]
    trace = (inv[0] * hess[0] + inv[3] * hess[3] + inv[5] * hess[5]) + 2.0 * (
        inv[1] * hess[1] + inv[2] * hess[2] + inv[4] * hess[4]
    )
    trace3 = trace * third
    curv = [value(9 + n) for n in range(6)]

    def pick(six, i, j):
        return six[pair_index[i][j]]

    def total(terms):
        return functools.reduce(lambda x, y: x + y, terms)

    mixed = [
        [total([pick(curv, i, l) * pick(inv, l, j) for l in range(3)]) for j in range(3)]
        for i in range(3)
    ]
    square = (mixed[0][0] * mixed[0][0] + mixed[1][1] * mixed[1][1] + mixed[2][2] * mixed[2][2]) + 2.0 * (
        mixed[0][1] * mixed[1][0] + mixed[0][2] * mixed[2][0] + mixed[1][2] * mixed[2][1]
    )
    out[2, out_at] = (
        along_shift(2)
        - conf * trace
        + lapse * (square + mean * mean * third + (4.0 * math.pi) * sources[src_at])
    )
    lapse2 = 2.0 * lapse
    mean_lapse = lapse * mean

    def stretched(six, i, j):
        if i == j:
            return 2.0 * total([pick(six, i, k) * dshift[i][k] for k in range(3)])
        return total([pick(six, i, k) * dshift[j][k] + pick(six, j, k) * dshift[i][k] for k in range(3)])

    for p, (i, j) in enumerate(sym_pairs):
        product = total([mixed[i][k] * pick(curv, k, j) for k in range(3)])
        out[9 + p, out_at] = (
            along_shift(9 + p)
            + (mean_lapse - div23) * curv[p]
            - lapse2 * product
            + stretched(curv, i, j)
            - conf * (hess[p] - trace3 * g[p])
        )
    for p, (i, j) in enumerate(sym_pairs):
        out[3 + p, out_at] = along_shift(3 + p) - lapse2 * curv[p] + stretched(g, i, j) - div23 * g[p]


def lane_matrix(nz, weights):
    row = lax.broadcasted_iota(jnp.int32, (nz, nz), 0)
    col = lax.broadcasted_iota(jnp.int32, (nz, nz), 1)
    return weights(row, col)


def dot(x, y):
    return jnp.dot(x, y, precision=lax.Precision.HIGHEST, preferred_element_type=F32)


def restrict_planes(pairs, rows, out, out_first):
    ny, nz = out.shape[-2:]
    half = ny // 2
    quarter_y, quarter_z = ny // 4, nz // 4
    count = len(pairs)
    for n, plane in enumerate(pairs):
        for h in range(nz // LANES):
            rows[h, pl.ds(n * ny, ny), :] = plane()[:, h * LANES : (h + 1) * LANES]
    halves = [
        rows[h, pl.ds(0, count * half, stride=2), :] + rows[h, pl.ds(1, count * half, stride=2), :]
        for h in range(nz // LANES)
    ]
    matrix = lane_matrix(
        nz, lambda r, c: jnp.where(c == quarter_z + lax.shift_right_logical(r, 1), 0.125, 0.0).astype(F32)
    )
    level = dot(jnp.concatenate(halves, axis=1), matrix)
    for n in range(count):
        out[out_first + n] = jnp.zeros((ny, nz), F32)
        out[out_first + n, pl.ds(quarter_y, half), :] = level[n * half : (n + 1) * half]


def prolong_yz(planes, rows, out):
    ny, nz = out.shape[-2:]
    half = ny // 2
    start_y, start_z = ny // 4, nz // 4
    flat = [plane for field in planes for plane in field]
    for n, plane in enumerate(flat):
        mid = 0.75 * plane(pl.ds(start_y, half))
        even = mid + 0.25 * plane(pl.ds(start_y - 1, half))
        odd = mid + 0.25 * plane(pl.ds(start_y + 1, half))
        for h in range(nz // LANES):
            lanes = slice(h * LANES, (h + 1) * LANES)
            rows[h, pl.ds(n * ny, half, stride=2), :] = even[:, lanes]
            rows[h, pl.ds(n * ny + 1, half, stride=2), :] = odd[:, lanes]

    def weights(r, c):
        mid = start_z + lax.shift_right_logical(c, 1)
        side = mid - 1 + 2 * (c & 1)
        return jnp.where(r == mid, 0.75, jnp.where(r == side, 0.25, 0.0)).astype(F32)

    matrix = lane_matrix(nz, weights)
    wide = jnp.concatenate([rows[h, pl.ds(0, len(flat) * ny), :] for h in range(nz // LANES)], axis=1)
    fine = dot(wide, matrix)
    at = 0
    for field, layers in enumerate(planes):
        for n in range(len(layers)):
            out[field, n] = fine[at * ny : (at + 1) * ny]
            at += 1


def split_flux(fluid, lapse, shift, conf, out, out_at, scale=None):
    root = lax.rsqrt(conf)
    transport = lapse * fluid(5) - shift
    weight = lapse * (root * root * root) * fluid(6)
    speed = lapse + jnp.abs(shift)
    for n in range(5):
        u = fluid(n)
        flux = u * transport
        if n == 1:
            flux = flux + weight
        if n == 4:
            flux = flux + weight * fluid(5)
        moved = speed * u
        plus, minus = flux + moved, flux - moved
        if scale is not None:
            plus, minus = plus * scale, minus * scale
        out[n, out_at] = plus
        out[5 + n, out_at] = minus


def weno_cells(flux, field, rows, first, count, emit):
    def differences(which, low, high):
        v = {j: flux[which, j, rows, :] for j in range(low, high + 1)}
        e = {j: v[j + 1] - v[j] for j in range(low, high)}
        d = {j: e[j] - e[j - 1] for j in range(low + 1, high)}
        t = {j: d[j + 1] - d[j] for j in range(low + 1, high - 1)}
        h = {j: 0.5 * d[j] for j in d}
        s = {j: (13.0 / 12.0) * (d[j] * d[j]) + 4.0 * weno_eps for j in d}
        return v, e, d, t, h, s

    faces = range(first - 1, first + count)
    v, e, d, t, h, s = differences(field, first - 3, first + count + 1)
    u, eu, du, tu, hu, su = differences(5 + field, first - 2, first + count + 2)

    def quotient(b0, b1, b2, t0, t2):
        w0, w1, w2 = b1 * b2, b0 * b2, b0 * b1
        w0, w1, w2 = w0 * w0, 6.0 * (w1 * w1), w2 * w2
        return (w0 * t0 + 1.5 * (w2 * t2)) / (w0 + w1 + 3.0 * w2)

    def square(x):
        return x * x

    previous = None
    for i in faces:
        left = quotient(
            s[i - 1] + square(h[i - 1] + e[i - 1]),
            s[i] + square(h[i] + e[i - 1]),
            s[i + 1] + square(h[i + 1] - e[i]),
            t[i - 1],
            t[i],
        )
        right = quotient(
            su[i + 2] + square(hu[i + 2] - eu[i + 1]),
            su[i + 1] + square(hu[i + 1] - eu[i + 1]),
            su[i] + square(hu[i] + eu[i]),
            tu[i + 1],
            tu[i],
        )
        face = (
            3.0 * (v[i] + u[i + 1])
            + 0.5 * (e[i - 1] - eu[i + 1])
            + (e[i] - eu[i])
            + (right - left)
        )
        if previous is not None:
            emit(i, (previous - face) * (1.0 / 3.0))
        previous = face


def local_kernel(
    lapse, conf, mean, metric, curv, shift, dens, mom, ener, velo, pres,
    rates, hydro, flux_out, source_out,
    state, fluid, coarse, flux, sources, rows, stage, hstage, sems,
):
    nx, ny, nz = lapse.shape
    fx = dens.shape[1]
    copies = Copies(sems)
    copies.start("c", lapse, state.at[0])
    copies.start("c", conf, state.at[1])
    copies.start("c", shift, state.at[pl.ds(15, 3)])
    copies.start("f", dens.at[0], fluid.at[0])
    copies.start("f", mom.at[0], fluid.at[pl.ds(1, 3)])
    copies.start("f", ener.at[0], fluid.at[4])
    copies.start("f", velo.at[0, 0], fluid.at[5])
    copies.start("f", pres.at[0], fluid.at[6])
    copies.start("f", velo.at[0, pl.ds(1, 2)], fluid.at[pl.ds(7, 2)])
    copies.start("m", mean, state.at[2])
    copies.start("m", metric, state.at[pl.ds(3, 6)])
    copies.start("m", curv, state.at[pl.ds(9, 6)])

    copies.wait("c")

    def coarse_plane(field, layer):
        return lambda sl: state[field, layer, sl, :]

    prolong_yz([[coarse_plane(f, l) for l in range(nx)] for f in (0, 15, 1)], rows, coarse)
    copies.wait("f")

    good = fx - 3

    @pl.loop(0, good)
    def _(i):
        mid = lax.shift_right_logical(i, 1) + 1
        side = mid - 1 + 2 * (i & 1)
        parts = [0.75 * coarse[n, mid] + 0.25 * coarse[n, side] for n in range(3)]
        split_flux(lambda n: fluid[n, i], *parts, flux, i)

    copies.start("o", flux, flux_out)

    def pair(layer):
        def one(x):
            return (
                fluid[4, x]
                + fluid[0, x]
                + (fluid[1, x] * fluid[5, x] + fluid[2, x] * fluid[7, x] + fluid[3, x] * fluid[8, x])
                + 3.0 * fluid[6, x]
            )

        return lambda: one(2 * layer) + one(2 * layer + 1)

    restrict_planes([pair(l) for l in range(nx - 1)], rows, sources, 1)
    copies.start("o", sources, source_out)

    @pl.loop(0, 5)
    def _(n):
        for part in range(ny // 8):
            sl = pl.ds(part * 8, 8)

            def emit(i, value):
                hstage[n, i - 3, sl, :] = value

            weno_cells(flux, n, sl, 3, fx - 9, emit)

    copies.start("o", hstage, hydro.at[0, :, pl.ds(3, fx - 9)])
    copies.wait("m")

    @pl.loop(0, nx - 4)
    def _(l):
        bssn_layer(state, sources, stage, l + 2, l + 2, l)

    copies.start("o", stage, rates.at[:, pl.ds(2, nx - 4)])
    copies.wait_all()


def halo_kernel(
    inside, below, above, rates_in, hydro_in, flux_in, source_in,
    lapse, conf, mean, metric, curv, shift, dens, mom, ener, velo, pres,
    rates, hydro,
    state, extra, own, fbelow, fabove, coarse, flux, sources, rows, stage, hstage, sems,
):
    nx, ny, nz = lapse.shape
    fx = dens.shape[1]
    copies = Copies(sems)
    tail = 2 * METRIC + 3 * FLUID
    for k in range(2):
        copies.start("m", below.at[pl.ds(k * METRIC, METRIC)], state.at[:, k])
        copies.start("m", above.at[pl.ds(k * METRIC, METRIC)], state.at[:, nx + 2 + k])
    for field, count, ref in metric_pieces(lapse, conf, mean, metric, curv, shift):
        if count is None:
            copies.start("m", ref, state.at[field, pl.ds(2, nx)])
        else:
            copies.start("m", ref, state.at[pl.ds(field, count), pl.ds(2, nx)])
    copies.start("m", above.at[pl.ds(tail, 3)], extra)
    for k in range(3):
        copies.start("f", below.at[pl.ds(2 * METRIC + k * FLUID, FLUID)], fbelow.at[pl.ds(0, FLUID), k])
        copies.start("f", above.at[pl.ds(2 * METRIC + k * FLUID, FLUID)], fabove.at[:, k])
    for k in range(2):
        copies.start("f", below.at[pl.ds(tail + 2 * k, 2)], fbelow.at[pl.ds(FLUID, 2), k + 1])
    last = pl.ds(fx - 3, 3)
    copies.start("f", dens.at[0, last], own.at[0])
    copies.start("f", mom.at[0, :, last], own.at[pl.ds(1, 3)])
    copies.start("f", ener.at[0, last], own.at[4])
    copies.start("f", velo.at[0, 0, last], own.at[5])
    copies.start("f", pres.at[0, last], own.at[6])
    copies.start("s", source_in, sources)
    copies.start("x", flux_in.at[:, pl.ds(0, 6)], flux.at[:, pl.ds(3, 6)])
    copies.start("x", flux_in.at[:, pl.ds(fx - 9, 6)], flux.at[:, pl.ds(fx - 6, 6)])

    copies.wait("m")

    def coarse_plane(field, layer):
        if layer == nx + 2:
            return lambda sl: extra[(0, 15, 1).index(field), sl, :]
        return lambda sl: state[field, layer + 2, sl, :]

    layers = (-1, 0, 1, nx - 1, nx, nx + 1, nx + 2)
    prolong_yz([[coarse_plane(f, l) for l in layers] for f in (0, 15, 1)], rows, coarse)
    copies.wait("f")

    for i in (-3, -2, -1) + tuple(range(fx - 3, fx + 3)):
        mid = i // 2 + 1
        side = mid - 1 + 2 * (i % 2)
        mid, side = layers.index(mid), layers.index(side)
        parts = [0.75 * coarse[n, mid] + 0.25 * coarse[n, side] for n in range(3)]
        if i < 0:
            source, at, scale = fbelow, i + 3, inside[0]
        elif i < fx:
            source, at, scale = own, i - fx + 3, None
        else:
            source, at, scale = fabove, i - fx, inside[1]
        split_flux(lambda n, s=source, a=at: s[n, a], *parts, flux, i + 3, scale)

    copies.wait("x")

    @pl.loop(0, 5)
    def _(n):
        for part in range(ny // 8):
            sl = pl.ds(part * 8, 8)

            def emit_low(i, value):
                hstage[n, i - 3, sl, :] = value

            def emit_high(i, value):
                hstage[n, 3 + i - (fx - 3), sl, :] = value

            weno_cells(flux, n, sl, 3, 3, emit_low)
            weno_cells(flux, n, sl, fx - 3, 6, emit_high)

    copies.start("o", hstage.at[:, pl.ds(0, 3)], hydro.at[0, :, pl.ds(0, 3)])
    copies.start("o", hstage.at[:, pl.ds(3, 6)], hydro.at[0, :, pl.ds(fx - 6, 6)])
    copies.wait("s")

    def pair():
        def one(x):
            return (
                fbelow[4, x]
                + fbelow[0, x]
                + (fbelow[1, x] * fbelow[5, x] + fbelow[2, x] * fbelow[7, x] + fbelow[3, x] * fbelow[8, x])
                + 3.0 * fbelow[6, x]
            )

        return one(1) + one(2)

    restrict_planes([pair], rows, sources, 0)

    @pl.loop(0, 4)
    def _(k):
        l = jnp.where(k < 2, k, k + nx - 4)
        bssn_layer(state, sources, stage, l + 2, l, k)

    copies.start("o", stage.at[:, pl.ds(0, 2)], rates.at[:, pl.ds(0, 2)])
    copies.start("o", stage.at[:, pl.ds(2, 2)], rates.at[:, pl.ds(nx - 2, 2)])
    copies.wait_all()


def on_device(*fields):
    lapse, dens = fields[0], fields[6]
    nx, ny, nz = lapse.shape
    fx = dens.shape[1]
    layer = (ny, nz)

    def shape(*leading):
        return jax.ShapeDtypeStruct(leading + layer, F32)

    def vmem(*leading):
        return pltpu.VMEM(leading + layer, F32)

    tail = 2 * METRIC + 3 * FLUID
    up, down = pl.pallas_call(
        pack_kernel,
        out_shape=(shape(tail + 4), shape(tail + 3)),
        in_specs=[ANY] * 11,
        out_specs=[ANY] * 2,
        scratch_shapes=[pltpu.SemaphoreType.DMA((64,))],
        name="pack",
    )(*fields)
    count = lax.axis_size(RING)
    pairs = [(i, (i + 1) % count) for i in range(count)]
    below = lax.ppermute(up, RING, pairs)
    above = lax.ppermute(down, RING, [(j, i) for i, j in pairs])

    def row_scratch(planes):
        return pltpu.VMEM((nz // LANES, planes * ny, LANES), F32)

    partial = pl.pallas_call(
        local_kernel,
        out_shape=(shape(15, nx), shape(1, 5, fx), shape(10, fx - 3), shape(nx)),
        in_specs=[ANY] * 11,
        out_specs=[ANY] * 4,
        scratch_shapes=[
            vmem(METRIC, nx),
            vmem(9, fx),
            vmem(3, nx),
            vmem(10, fx - 3),
            vmem(nx),
            row_scratch(3 * nx),
            vmem(15, nx - 4),
            vmem(5, fx - 9),
            pltpu.SemaphoreType.DMA((32,)),
        ],
        cost_estimate=pl.CostEstimate(flops=400_000_000, transcendentals=0, bytes_accessed=12_000_000),
        name="local",
    )(*fields)
    place = lax.axis_index("blk")
    inside = jnp.stack([place > 0, place < lax.axis_size("blk") - 1]).astype(F32)
    return pl.pallas_call(
        halo_kernel,
        out_shape=(shape(15, nx), shape(1, 5, fx)),
        in_specs=[pl.BlockSpec(memory_space=pltpu.SMEM)] + [ANY] * 17,
        out_specs=[ANY] * 2,
        input_output_aliases={3: 0, 4: 1},
        scratch_shapes=[
            vmem(METRIC, nx + 4),
            vmem(3),
            vmem(FLUID, 3),
            vmem(9, 3),
            vmem(FLUID, 3),
            vmem(3, 7),
            vmem(10, fx + 6),
            vmem(nx),
            row_scratch(21),
            vmem(15, 4),
            vmem(5, 9),
            pltpu.SemaphoreType.DMA((64,)),
        ],
        cost_estimate=pl.CostEstimate(flops=400_000_000, transcendentals=0, bytes_accessed=12_000_000),
        name="halo",
    )(inside, below, above, *partial, *fields)


def solution(mesh):
    in_specs = (
        P(RING, None, None),
        P(RING, None, None),
        P(RING, None, None),
        P(None, RING, None, None),
        P(None, RING, None, None),
        P(None, RING, None, None),
        P("star", "blk", None, None),
        P("star", None, "blk", None, None),
        P("star", "blk", None, None),
        P("star", None, "blk", None, None),
        P("star", "blk", None, None),
    )
    out_specs = (P(None, RING, None, None), P("star", None, "blk", None, None))
    return jax.shard_map(
        on_device, mesh=mesh, in_specs=in_specs, out_specs=out_specs, check_vma=False
    )
```

time: 127 us -> 101 us (0.80)
  the two profiles are of different devices: /device:TPU:29 before, /device:TPU:1 now
where the time goes in v1:
time: 101 us
  Pallas kernels  80.5 us (80%)
  waiting for transfers between devices  15.6 us (15%)
  starting transfers between devices  2.67 us (3%)
  local copies, waits for them, and re-layouts  1.28 us (1%)
    pallas_call x1, Pallas kernels, on_device(): pl.pallas_call(pack_kernel, out_shape=(shape(tail + 4), shape(tail + 3)),...  61.7 us
    ppermute x1, waiting for transfers between devices, on_device(): above = lax.ppermute(down, RING, [(j, i) for i, j in pairs])  15.6 us
    pallas_call x1, Pallas kernels, on_device(): pl.pallas_call(halo_kernel, out_shape=(shape(15, nx), shape(1, 5, fx)), i...  10.5 us
    pallas_call x1, Pallas kernels, on_device(): pl.pallas_call(local_kernel, out_shape=(shape(15, nx), shape(1, 5, fx), s...  8.27 us
    ppermute x1, starting transfers between devices, on_device(): below = lax.ppermute(up, RING, pairs)  2.67 us
  transfers between devices with their start and end apart: 2, of which 1 were waited for; matrix products, arithmetic and copies ran while one was open for 1% of the time, Pallas kernels for 8%

profile of v1, /device:TPU:1, one launch (start us, length us, event | category | flops | bytes accessed | tf_op | source)
XLA Modules:
  0.0 101.3 jit_solution(10671298897695106970)
XLA Ops:
  0.6 61.7 %pack.1 = (f32[61,16,256]{2,1,0:T(8,128)}, f32[60,16,256]{2,1,0:T(8,128)}) custom-call(f32[8,16,256]{2,1,0:T(8,128)} %lapse.5, f32[8,16,256]{2,1,0:T(8,128)} %conf.5, f32[8,16,256]{2,1,0:T(8,128)} %mean.5, f32[6,8,16,256]{3,2,1,0:T(8,128)} %metric.5, f32[6,8,16,256]{3,2,1,0:T(8,128)} %curv.5, f32[3,8,16,256]{3,2,1,0:T(8,128)} %shift.5, ...), custom_call_target="tpu_custom_call" | custom-call | tf_op jit(solution)/shard_map/pack/pallas_call | solution.py:503
  62.4 2.7 %collective-permute-start = (f32[61,16,256]{2,1,0:T(8,128)}, f32[61,16,256]{2,1,0:T(8,128)S(1)}, u32[]{:S(2)}, u32[]{:S(2)}) collective-permute-start(f32[61,16,256]{2,1,0:T(8,128)} %get-tuple-element.8), channel_id=1, source_target_pairs={{0,1},{1,2},{2,3},{3,4},{4,5},{5,6},{6,7},{7,8},{8,9},{9,10},{10,1... | collective-permute-start | bytes 2998280 | tf_op jit(solution)/shard_map/ppermute | solution.py:513
  65.0 0.0 collective-permute-start.1
  65.0 8.3 %local.1 = (f32[15,8,16,256]{3,2,1,0:T(8,128)}, f32[1,5,16,16,256]{4,3,2,1,0:T(8,128)}, f32[10,13,16,256]{3,2,1,0:T(8,128)}, f32[8,16,256]{2,1,0:T(8,128)}) custom-call(f32[8,16,256]{2,1,0:T(8,128)} %lapse.5, f32[8,16,256]{2,1,0:T(8,128)} %conf.5, f32[8,16,256]{2,1,0:T(8,128)} %mean.5, f32[6,8,16,256]{3,2,1,0:T(8,128)} %metric.5, f32[6,8,16,256]{3,2,1,0:T(8,128)} %curv.5, ...), custom_call_target="tpu_custom_call" | custom-call | flops 400000000 | bytes 12000000 | tf_op jit(solution)/shard_map/local/pallas_call | solution.py:519
  73.3 0.6 add_convert_fusion.inside
  73.9 15.6 %collective-permute-done.1.above = f32[60,16,256]{2,1,0:T(8,128)S(1)} collective-permute-done((f32[60,16,256]{2,1,0:T(8,128)}, f32[60,16,256]{2,1,0:T(8,128)S(1)}, u32[]{:S(2)}, u32[]{:S(2)}) %collective-permute-start.1) | collective-permute-done | bytes 983072 | tf_op jit(solution)/shard_map/ppermute | solution.py:514
  89.5 0.0 copy-start.1
  89.5 0.0 collective-permute-done.below
  89.5 0.0 copy-start
  89.5 1.0 copy-done.1
  90.5 0.3 copy-done
  90.8 10.5 %halo.1 = (f32[15,8,16,256]{3,2,1,0:T(8,128)}, f32[1,5,16,16,256]{4,3,2,1,0:T(8,128)}) custom-call(f32[2]{0:T(128)} %add_convert_fusion.inside, f32[61,16,256]{2,1,0:T(8,128)} %copy-done, f32[60,16,256]{2,1,0:T(8,128)} %copy-done.1, f32[15,8,16,256]{3,2,1,0:T(8,128)} %get-tuple-element.10.rates_in, ...), custom_call_target="tpu_custom_call", output_to_operand_aliasing={{0}: (3, {}), {1}: (4, {})} | custom-call | flops 400000000 | bytes 12000000 | tf_op jit(solution)/shard_map/halo/pallas_call | solution.py:540
Async XLA Ops:
  62.4 27.1 %collective-permute-start = (f32[61,16,256]{2,1,0:T(8,128)}, f32[61,16,256]{2,1,0:T(8,128)S(1)}, u32[]{:S(2)}, u32[]{:S(2)}) collective-permute-start(f32[61,16,256]{2,1,0:T(8,128)} %get-tuple-element.8), channel_id=1, source_target_pairs={{0,1},{1,2},{2,3},{3,4},{4,5},{5,6},{6,7},{7,8},{8,9},{9,10},{10,1... | collective-permute-start | bytes 2998280 | tf_op jit(solution)/shard_map/ppermute | solution.py:513
  65.0 24.4 %collective-permute-start.1 = (f32[60,16,256]{2,1,0:T(8,128)}, f32[60,16,256]{2,1,0:T(8,128)S(1)}, u32[]{:S(2)}, u32[]{:S(2)}) collective-permute-start(f32[60,16,256]{2,1,0:T(8,128)} %get-tuple-element.9), channel_id=1, source_target_pairs={{1,0},{2,1},{3,2},{4,3},{5,4},{6,5},{7,6},{8,7},{9,8},{10,9},{11,1... | collective-permute-start | bytes 2949128 | tf_op jit(solution)/shard_map/ppermute | solution.py:514
  89.5 1.0 copy-start.1
  89.5 1.3 %copy-start = (f32[61,16,256]{2,1,0:T(8,128)}, f32[61,16,256]{2,1,0:T(8,128)S(1)}, u32[]{:S(2)}) copy-start(f32[61,16,256]{2,1,0:T(8,128)S(1)} %collective-permute-done.below) | copy-start | bytes 2998276

commit v2 on v1

--- a/solution.py
+++ b/solution.py
@@ -16,6 +16,7 @@
 METRIC = 18
 FLUID = 7
 ANY = pl.BlockSpec(memory_space=pl.ANY)
+VMEM = pl.BlockSpec(memory_space=pltpu.VMEM)
 F32 = jnp.float32
 
 
@@ -387,7 +388,7 @@
 
 
 def halo_kernel(
-    inside, below, above, rates_in, hydro_in, flux_in, source_in,
+    below, above, rates_in, hydro_in, flux_in, source_in,
     lapse, conf, mean, metric, curv, shift, dens, mom, ener, velo, pres,
     rates, hydro,
     state, extra, own, fbelow, fabove, coarse, flux, sources, rows, stage, hstage, sems,
@@ -396,6 +397,11 @@
     fx = dens.shape[1]
     copies = Copies(sems)
     tail = 2 * METRIC + 3 * FLUID
+    place = lax.axis_index("blk")
+    inside = (
+        jnp.where(place > 0, 1.0, 0.0).astype(F32),
+        jnp.where(place < lax.axis_size("blk") - 1, 1.0, 0.0).astype(F32),
+    )
     for k in range(2):
         copies.start("m", below.at[pl.ds(k * METRIC, METRIC)], state.at[:, k])
         copies.start("m", above.at[pl.ds(k * METRIC, METRIC)], state.at[:, nx + 2 + k])
@@ -504,7 +510,7 @@
         pack_kernel,
         out_shape=(shape(tail + 4), shape(tail + 3)),
         in_specs=[ANY] * 11,
-        out_specs=[ANY] * 2,
+        out_specs=[VMEM] * 2,
         scratch_shapes=[pltpu.SemaphoreType.DMA((64,))],
         name="pack",
     )(*fields)
@@ -535,14 +541,12 @@
         cost_estimate=pl.CostEstimate(flops=400_000_000, transcendentals=0, bytes_accessed=12_000_000),
         name="local",
     )(*fields)
-    place = lax.axis_index("blk")
-    inside = jnp.stack([place > 0, place < lax.axis_size("blk") - 1]).astype(F32)
     return pl.pallas_call(
         halo_kernel,
         out_shape=(shape(15, nx), shape(1, 5, fx)),
-        in_specs=[pl.BlockSpec(memory_space=pltpu.SMEM)] + [ANY] * 17,
+        in_specs=[VMEM] * 2 + [ANY] * 15,
         out_specs=[ANY] * 2,
-        input_output_aliases={3: 0, 4: 1},
+        input_output_aliases={2: 0, 3: 1},
         scratch_shapes=[
             vmem(METRIC, nx + 4),
             vmem(3),
@@ -559,7 +563,7 @@
         ],
         cost_estimate=pl.CostEstimate(flops=400_000_000, transcendentals=0, bytes_accessed=12_000_000),
         name="halo",
-    )(inside, below, above, *partial, *fields)
+    )(below, above, *partial, *fields)
 
 
 def solution(mesh):

time: 101 us -> 43.8 us (0.43)
  Pallas kernels: 80.5 us -> 22.7 us
    pallas_call x1, Pallas kernels: 61.7 us -> 3.34 us  [on_device(): pl.pallas_call(pack_kernel, out_shape=(shape(tail + 4), shape(tail + 3)),...]
  transfers between devices with their start and end apart: 2 -> 2, of which waited for: 1 -> 1; matrix products, arithmetic and copies ran while one was open for 1% -> 0% of each run, Pallas kernels for 8% -> 19%
where the time goes in v2:
time: 43.8 us; the launch traced here: 43.5 us
  Pallas kernels  22.7 us (52%)
  waiting for transfers between devices  16.2 us (37%)
  starting transfers between devices  2.67 us (6%)
  local copies, waits for them, and re-layouts  1.28 us (3%)
  between operations  0.65 us (1%)
    ppermute x1, waiting for transfers between devices, on_device(): above = lax.ppermute(down, RING, [(j, i) for i, j in pairs])  16.2 us
    pallas_call x1, Pallas kernels, on_device(): pl.pallas_call(halo_kernel, out_shape=(shape(15, nx), shape(1, 5, fx)), i...  11.1 us
    pallas_call x1, Pallas kernels, on_device(): pl.pallas_call(local_kernel, out_shape=(shape(15, nx), shape(1, 5, fx), s...  8.27 us
    pallas_call x1, Pallas kernels, on_device(): pl.pallas_call(pack_kernel, out_shape=(shape(tail + 4), shape(tail + 3)),...  3.34 us
    ppermute x1, starting transfers between devices, on_device(): below = lax.ppermute(up, RING, pairs)  2.67 us
    unnamed x4, local copies, waits for them, and re-layouts  1.28 us
  transfers between devices with their start and end apart: 2, of which 1 were waited for; matrix products, arithmetic and copies ran while one was open for 0% of the time, Pallas kernels for 19%

profile of v2, /device:TPU:1, one launch (start us, length us, event | category | flops | bytes accessed | tf_op | source)
XLA Modules:
  0.0 43.5 jit_solution(9304004040183795303)
XLA Ops:
  0.6 3.3 %pack.1 = (f32[61,16,256]{2,1,0:T(8,128)}, f32[60,16,256]{2,1,0:T(8,128)}) custom-call(f32[8,16,256]{2,1,0:T(8,128)} %lapse.5, f32[8,16,256]{2,1,0:T(8,128)} %conf.5, f32[8,16,256]{2,1,0:T(8,128)} %mean.5, f32[6,8,16,256]{3,2,1,0:T(8,128)} %metric.5, f32[6,8,16,256]{3,2,1,0:T(8,128)} %curv.5, f32[3,8,16,256]{3,2,1,0:T(8,128)} %shift.5, ...), custom_call_target="tpu_custom_call" | custom-call | tf_op jit(solution)/shard_map/pack/pallas_call | solution.py:509
  4.0 2.7 %collective-permute-start = (f32[61,16,256]{2,1,0:T(8,128)}, f32[61,16,256]{2,1,0:T(8,128)S(1)}, u32[]{:S(2)}, u32[]{:S(2)}) collective-permute-start(f32[61,16,256]{2,1,0:T(8,128)} %get-tuple-element.8), channel_id=1, source_target_pairs={{0,1},{1,2},{2,3},{3,4},{4,5},{5,6},{6,7},{7,8},{8,9},{9,10},{10,1... | collective-permute-start | bytes 2998280 | tf_op jit(solution)/shard_map/ppermute | solution.py:519
  6.6 0.0 collective-permute-start.1
  6.6 8.3 %local.1 = (f32[15,8,16,256]{3,2,1,0:T(8,128)}, f32[1,5,16,16,256]{4,3,2,1,0:T(8,128)}, f32[10,13,16,256]{3,2,1,0:T(8,128)}, f32[8,16,256]{2,1,0:T(8,128)}) custom-call(f32[8,16,256]{2,1,0:T(8,128)} %lapse.5, f32[8,16,256]{2,1,0:T(8,128)} %conf.5, f32[8,16,256]{2,1,0:T(8,128)} %mean.5, f32[6,8,16,256]{3,2,1,0:T(8,128)} %metric.5, f32[6,8,16,256]{3,2,1,0:T(8,128)} %curv.5, ...), custom_call_target="tpu_custom_call" | custom-call | flops 400000000 | bytes 12000000 | tf_op jit(solution)/shard_map/local/pallas_call | solution.py:525
  14.9 16.2 %collective-permute-done.1.above = f32[60,16,256]{2,1,0:T(8,128)S(1)} collective-permute-done((f32[60,16,256]{2,1,0:T(8,128)}, f32[60,16,256]{2,1,0:T(8,128)S(1)}, u32[]{:S(2)}, u32[]{:S(2)}) %collective-permute-start.1) | collective-permute-done | bytes 983072 | tf_op jit(solution)/shard_map/ppermute | solution.py:520
  31.1 0.0 copy-start.1
  31.1 0.0 collective-permute-done.below
  31.1 0.0 copy-start
  31.1 1.0 %copy-done.1 = f32[60,16,256]{2,1,0:T(8,128)} copy-done((f32[60,16,256]{2,1,0:T(8,128)}, f32[60,16,256]{2,1,0:T(8,128)S(1)}, u32[]{:S(2)}) %copy-start.1) | copy-done | bytes 983064
  32.0 0.3 copy-done
  32.4 11.1 %halo.1 = (f32[15,8,16,256]{3,2,1,0:T(8,128)}, f32[1,5,16,16,256]{4,3,2,1,0:T(8,128)}) custom-call(f32[61,16,256]{2,1,0:T(8,128)} %copy-done, f32[60,16,256]{2,1,0:T(8,128)} %copy-done.1, f32[15,8,16,256]{3,2,1,0:T(8,128)} %get-tuple-element.10.rates_in, ...), custom_call_target="tpu_custom_call", output_to_operand_aliasing={{0}: (2, {}), {1}: (3, {})} | custom-call | flops 400000000 | bytes 12000000 | tf_op jit(solution)/shard_map/halo/pallas_call | solution.py:544
Async XLA Ops:
  4.0 27.1 %collective-permute-start = (f32[61,16,256]{2,1,0:T(8,128)}, f32[61,16,256]{2,1,0:T(8,128)S(1)}, u32[]{:S(2)}, u32[]{:S(2)}) collective-permute-start(f32[61,16,256]{2,1,0:T(8,128)} %get-tuple-element.8), channel_id=1, source_target_pairs={{0,1},{1,2},{2,3},{3,4},{4,5},{5,6},{6,7},{7,8},{8,9},{9,10},{10,1... | collective-permute-start | bytes 2998280 | tf_op jit(solution)/shard_map/ppermute | solution.py:519
  6.6 24.4 %collective-permute-start.1 = (f32[60,16,256]{2,1,0:T(8,128)}, f32[60,16,256]{2,1,0:T(8,128)S(1)}, u32[]{:S(2)}, u32[]{:S(2)}) collective-permute-start(f32[60,16,256]{2,1,0:T(8,128)} %get-tuple-element.9), channel_id=1, source_target_pairs={{1,0},{2,1},{3,2},{4,3},{5,4},{6,5},{7,6},{8,7},{9,8},{10,9},{11,1... | collective-permute-start | bytes 2949128 | tf_op jit(solution)/shard_map/ppermute | solution.py:520
  31.1 1.0 %copy-start.1 = (f32[60,16,256]{2,1,0:T(8,128)}, f32[60,16,256]{2,1,0:T(8,128)S(1)}, u32[]{:S(2)}) copy-start(f32[60,16,256]{2,1,0:T(8,128)S(1)} %collective-permute-done.1.above) | copy-start | bytes 2949124
  31.1 1.3 %copy-start = (f32[61,16,256]{2,1,0:T(8,128)}, f32[61,16,256]{2,1,0:T(8,128)S(1)}, u32[]{:S(2)}) copy-start(f32[61,16,256]{2,1,0:T(8,128)S(1)} %collective-permute-done.below) | copy-start | bytes 2998276

commit v3 on v2

--- a/solution.py
+++ b/solution.py
@@ -16,6 +16,7 @@
 METRIC = 18
 FLUID = 7
 ANY = pl.BlockSpec(memory_space=pl.ANY)
+GRANT = 24 * 1024 * 1024
 VMEM = pl.BlockSpec(memory_space=pltpu.VMEM)
 F32 = jnp.float32
 
@@ -512,6 +513,7 @@
         in_specs=[ANY] * 11,
         out_specs=[VMEM] * 2,
         scratch_shapes=[pltpu.SemaphoreType.DMA((64,))],
+        compiler_params=pltpu.CompilerParams(vmem_limit_bytes=GRANT),
         name="pack",
     )(*fields)
     count = lax.axis_size(RING)
@@ -539,6 +541,7 @@
             pltpu.SemaphoreType.DMA((32,)),
         ],
         cost_estimate=pl.CostEstimate(flops=400_000_000, transcendentals=0, bytes_accessed=12_000_000),
+        compiler_params=pltpu.CompilerParams(vmem_limit_bytes=GRANT),
         name="local",
     )(*fields)
     return pl.pallas_call(
@@ -562,6 +565,7 @@
             pltpu.SemaphoreType.DMA((64,)),
         ],
         cost_estimate=pl.CostEstimate(flops=400_000_000, transcendentals=0, bytes_accessed=12_000_000),
+        compiler_params=pltpu.CompilerParams(vmem_limit_bytes=GRANT),
         name="halo",
     )(below, above, *partial, *fields)
 

time: 43.8 us -> 50.6 us (1.16)
  local copies, waits for them, and re-layouts: 1.28 us -> 11.1 us
  Pallas kernels: 22.7 us -> 20 us
    unnamed x4 -> x22, local copies, waits for them, and re-layouts: 1.28 us -> 11.1 us
    pallas_call x1, Pallas kernels: 11.1 us -> 9.59 us  [on_device(): pl.pallas_call(halo_kernel, out_shape=(shape(15, nx), shape(1, 5, fx)), i...]
    pallas_call x1, Pallas kernels: 3.34 us -> 1.9 us  [on_device(): pl.pallas_call(pack_kernel, out_shape=(shape(tail + 4), shape(tail + 3)),...]
  transfers between devices with their start and end apart: 2 -> 2, of which waited for: 1 -> 1; matrix products, arithmetic and copies ran while one was open for 0% -> 0% of each run, Pallas kernels for 19% -> 17%
where the time goes in v3:
time: 50.6 us; the launch traced here: 50.1 us
  Pallas kernels  20 us (40%)
  waiting for transfers between devices  15.8 us (31%)
  local copies, waits for them, and re-layouts  11.1 us (22%)
  starting transfers between devices  2.67 us (5%)
  between operations  0.67 us (1%)
    ppermute x1, waiting for transfers between devices, on_device(): above = lax.ppermute(down, RING, [(j, i) for i, j in pairs])  15.8 us
    unnamed x22, local copies, waits for them, and re-layouts  11.1 us
    pallas_call x1, Pallas kernels, on_device(): pl.pallas_call(halo_kernel, out_shape=(shape(15, nx), shape(1, 5, fx)), i...  9.59 us
    pallas_call x1, Pallas kernels, on_device(): pl.pallas_call(local_kernel, out_shape=(shape(15, nx), shape(1, 5, fx), s...  8.46 us
    ppermute x1, starting transfers between devices, on_device(): below = lax.ppermute(up, RING, pairs)  2.67 us
    pallas_call x1, Pallas kernels, on_device(): pl.pallas_call(pack_kernel, out_shape=(shape(tail + 4), shape(tail + 3)),...  1.9 us
  transfers between devices with their start and end apart: 2, of which 1 were waited for; matrix products, arithmetic and copies ran while one was open for 0% of the time, Pallas kernels for 17%

profile of v3, /device:TPU:1, one launch (start us, length us, event | category | flops | bytes accessed | tf_op | source)
XLA Modules:
  0.0 50.1 jit_solution(17874674930501917469)
XLA Ops:
  0.6 0.0 copy-start
  0.6 1.1 %copy-done = f32[6,8,16,256]{3,2,1,0:T(8,128)S(1)} copy-done((f32[6,8,16,256]{3,2,1,0:T(8,128)S(1)}, f32[6,8,16,256]{3,2,1,0:T(8,128)}, u32[]{:S(2)}) %copy-start) | copy-done | bytes 786456
  1.8 0.0 copy-start.1
  1.8 1.1 %copy-done.1 = f32[6,8,16,256]{3,2,1,0:T(8,128)S(1)} copy-done((f32[6,8,16,256]{3,2,1,0:T(8,128)S(1)}, f32[6,8,16,256]{3,2,1,0:T(8,128)}, u32[]{:S(2)}) %copy-start.1) | copy-done | bytes 786456
  2.9 0.0 copy-start.2
  2.9 1.1 %copy-done.2 = f32[1,3,16,16,256]{4,3,2,1,0:T(8,128)S(1)} copy-done((f32[1,3,16,16,256]{4,3,2,1,0:T(8,128)S(1)}, f32[1,3,16,16,256]{4,3,2,1,0:T(8,128)}, u32[]{:S(2)}) %copy-start.2) | copy-done | bytes 786456
  4.0 0.0 copy-start.3
  4.0 1.1 %copy-done.3 = f32[1,3,16,16,256]{4,3,2,1,0:T(8,128)S(1)} copy-done((f32[1,3,16,16,256]{4,3,2,1,0:T(8,128)S(1)}, f32[1,3,16,16,256]{4,3,2,1,0:T(8,128)}, u32[]{:S(2)}) %copy-start.3) | copy-done | bytes 786456
  5.2 0.0 copy-start.4
  5.2 1.0 %copy-done.4 = f32[3,8,16,256]{3,2,1,0:T(8,128)S(1)} copy-done((f32[3,8,16,256]{3,2,1,0:T(8,128)S(1)}, f32[3,8,16,256]{3,2,1,0:T(8,128)}, u32[]{:S(2)}) %copy-start.4) | copy-done | bytes 393240
  6.2 0.0 copy-start.5
  6.2 0.9 %copy-done.5 = f32[1,16,16,256]{3,2,1,0:T(8,128)S(1)} copy-done((f32[1,16,16,256]{3,2,1,0:T(8,128)S(1)}, f32[1,16,16,256]{3,2,1,0:T(8,128)}, u32[]{:S(2)}) %copy-start.5) | copy-done | bytes 262168
  7.1 0.9 %copy-done.6 = f32[1,16,16,256]{3,2,1,0:T(8,128)S(1)} copy-done((f32[1,16,16,256]{3,2,1,0:T(8,128)S(1)}, f32[1,16,16,256]{3,2,1,0:T(8,128)}, u32[]{:S(2)}) %copy-start.6) | copy-done | bytes 262168
  8.1 0.9 %copy-done.7 = f32[1,16,16,256]{3,2,1,0:T(8,128)S(1)} copy-done((f32[1,16,16,256]{3,2,1,0:T(8,128)S(1)}, f32[1,16,16,256]{3,2,1,0:T(8,128)}, u32[]{:S(2)}) %copy-start.7) | copy-done | bytes 262168
  9.0 0.9 %copy-done.8 = f32[8,16,256]{2,1,0:T(8,128)S(1)} copy-done((f32[8,16,256]{2,1,0:T(8,128)S(1)}, f32[8,16,256]{2,1,0:T(8,128)}, u32[]{:S(2)}) %copy-start.8) | copy-done | bytes 131096
  9.9 0.9 %copy-done.9 = f32[8,16,256]{2,1,0:T(8,128)S(1)} copy-done((f32[8,16,256]{2,1,0:T(8,128)S(1)}, f32[8,16,256]{2,1,0:T(8,128)}, u32[]{:S(2)}) %copy-start.9) | copy-done | bytes 131096
  10.8 0.9 %copy-done.10 = f32[8,16,256]{2,1,0:T(8,128)S(1)} copy-done((f32[8,16,256]{2,1,0:T(8,128)S(1)}, f32[8,16,256]{2,1,0:T(8,128)}, u32[]{:S(2)}) %copy-start.10) | copy-done | bytes 131096
  11.7 1.9 %pack.1 = (f32[61,16,256]{2,1,0:T(8,128)S(1)}, f32[60,16,256]{2,1,0:T(8,128)S(1)}) custom-call(f32[8,16,256]{2,1,0:T(8,128)S(1)} %copy-done.8, f32[8,16,256]{2,1,0:T(8,128)S(1)} %copy-done.9, f32[8,16,256]{2,1,0:T(8,128)S(1)} %copy-done.10, f32[6,8,16,256]{3,2,1,0:T(8,128)S(1)} %copy-done, f32[6,8,16,256]{3,2,1,0:T(8,128)S(1)} %copy-done.1, ...), custom_call_target="tpu_custom_call" | custom-call | tf_op jit(solution)/shard_map/pack/pallas_call | solution.py:510
  13.6 2.7 %collective-permute-start = (f32[61,16,256]{2,1,0:T(8,128)S(1)}, f32[61,16,256]{2,1,0:T(8,128)S(1)}, u32[]{:S(2)}, u32[]{:S(2)}) collective-permute-start(f32[61,16,256]{2,1,0:T(8,128)S(1)} %get-tuple-element.8), channel_id=1, source_target_pairs={{0,1},{1,2},{2,3},{3,4},{4,5},{5,6},{6,7},{7,8},{8,9},{9,10},{10,1... | collective-permute-start | bytes 2998280 | tf_op jit(solution)/shard_map/ppermute | solution.py:521
  16.3 0.0 collective-permute-start.1
  16.3 8.5 %local.1 = (f32[15,8,16,256]{3,2,1,0:T(8,128)}, f32[1,5,16,16,256]{4,3,2,1,0:T(8,128)}, f32[10,13,16,256]{3,2,1,0:T(8,128)S(1)}, f32[8,16,256]{2,1,0:T(8,128)S(1)}) custom-call(f32[8,16,256]{2,1,0:T(8,128)S(1)} %copy-done.8, f32[8,16,256]{2,1,0:T(8,128)S(1)} %copy-done.9, f32[8,16,256]{2,1,0:T(8,128)S(1)} %copy-done.10, f32[6,8,16,256]{3,2,1,0:T(8,128)S(1)} %copy-done, ...), custom_call_target="tpu_custom_call" | custom-call | flops 400000000 | bytes 12000000 | tf_op jit(solution)/shard_map/local/pallas_call | solution.py:527
  24.8 15.8 %collective-permute-done.1.above = f32[60,16,256]{2,1,0:T(8,128)S(1)} collective-permute-done((f32[60,16,256]{2,1,0:T(8,128)S(1)}, f32[60,16,256]{2,1,0:T(8,128)S(1)}, u32[]{:S(2)}, u32[]{:S(2)}) %collective-permute-start.1) | collective-permute-done | bytes 983072 | tf_op jit(solution)/shard_map/ppermute | solution.py:522
  40.5 0.0 collective-permute-done.below
  40.5 9.6 %halo.1 = (f32[15,8,16,256]{3,2,1,0:T(8,128)}, f32[1,5,16,16,256]{4,3,2,1,0:T(8,128)}) custom-call(f32[61,16,256]{2,1,0:T(8,128)S(1)} %collective-permute-done.below, f32[60,16,256]{2,1,0:T(8,128)S(1)} %collective-permute-done.1.above, f32[15,8,16,256]{3,2,1,0:T(8,128)} %get-tuple-element.10.rates_in, ...), custom_call_target="tpu_custom_call", output_to_operand_aliasing={{0}: (2, {}), {1}: (3, {})} | custom-call | flops 400000000 | bytes 12000000 | tf_op jit(solution)/shard_map/halo/pallas_call | solution.py:547
  (5 shorter events, 0.0 us)
Async XLA Ops:
  0.6 1.1 %copy-start = (f32[6,8,16,256]{3,2,1,0:T(8,128)S(1)}, f32[6,8,16,256]{3,2,1,0:T(8,128)}, u32[]{:S(2)}) copy-start(f32[6,8,16,256]{3,2,1,0:T(8,128)} %metric.5) | copy-start | bytes 2359300
  1.8 1.1 %copy-start.1 = (f32[6,8,16,256]{3,2,1,0:T(8,128)S(1)}, f32[6,8,16,256]{3,2,1,0:T(8,128)}, u32[]{:S(2)}) copy-start(f32[6,8,16,256]{3,2,1,0:T(8,128)} %curv.5) | copy-start | bytes 2359300
  2.9 1.1 %copy-start.2 = (f32[1,3,16,16,256]{4,3,2,1,0:T(8,128)S(1)}, f32[1,3,16,16,256]{4,3,2,1,0:T(8,128)}, u32[]{:S(2)}) copy-start(f32[1,3,16,16,256]{4,3,2,1,0:T(8,128)} %mom.5) | copy-start | bytes 2359300
  4.0 1.1 %copy-start.3 = (f32[1,3,16,16,256]{4,3,2,1,0:T(8,128)S(1)}, f32[1,3,16,16,256]{4,3,2,1,0:T(8,128)}, u32[]{:S(2)}) copy-start(f32[1,3,16,16,256]{4,3,2,1,0:T(8,128)} %velo.5) | copy-start | bytes 2359300
  5.2 1.0 %copy-start.4 = (f32[3,8,16,256]{3,2,1,0:T(8,128)S(1)}, f32[3,8,16,256]{3,2,1,0:T(8,128)}, u32[]{:S(2)}) copy-start(f32[3,8,16,256]{3,2,1,0:T(8,128)} %shift.5) | copy-start | bytes 1179652
  6.2 0.9 %copy-start.5 = (f32[1,16,16,256]{3,2,1,0:T(8,128)S(1)}, f32[1,16,16,256]{3,2,1,0:T(8,128)}, u32[]{:S(2)}) copy-start(f32[1,16,16,256]{3,2,1,0:T(8,128)} %dens.5) | copy-start | bytes 786436
  7.1 0.9 %copy-start.6 = (f32[1,16,16,256]{3,2,1,0:T(8,128)S(1)}, f32[1,16,16,256]{3,2,1,0:T(8,128)}, u32[]{:S(2)}) copy-start(f32[1,16,16,256]{3,2,1,0:T(8,128)} %ener.5) | copy-start | bytes 786436
  8.1 0.9 %copy-start.7 = (f32[1,16,16,256]{3,2,1,0:T(8,128)S(1)}, f32[1,16,16,256]{3,2,1,0:T(8,128)}, u32[]{:S(2)}) copy-start(f32[1,16,16,256]{3,2,1,0:T(8,128)} %pres.5) | copy-start | bytes 786436
  9.0 0.9 %copy-start.8 = (f32[8,16,256]{2,1,0:T(8,128)S(1)}, f32[8,16,256]{2,1,0:T(8,128)}, u32[]{:S(2)}) copy-start(f32[8,16,256]{2,1,0:T(8,128)} %lapse.5) | copy-start | bytes 393220
  9.9 0.9 %copy-start.9 = (f32[8,16,256]{2,1,0:T(8,128)S(1)}, f32[8,16,256]{2,1,0:T(8,128)}, u32[]{:S(2)}) copy-start(f32[8,16,256]{2,1,0:T(8,128)} %conf.5) | copy-start | bytes 393220
  10.8 0.9 %copy-start.10 = (f32[8,16,256]{2,1,0:T(8,128)S(1)}, f32[8,16,256]{2,1,0:T(8,128)}, u32[]{:S(2)}) copy-start(f32[8,16,256]{2,1,0:T(8,128)} %mean.5) | copy-start | bytes 393220
  13.6 26.9 %collective-permute-start = (f32[61,16,256]{2,1,0:T(8,128)S(1)}, f32[61,16,256]{2,1,0:T(8,128)S(1)}, u32[]{:S(2)}, u32[]{:S(2)}) collective-permute-start(f32[61,16,256]{2,1,0:T(8,128)S(1)} %get-tuple-element.8), channel_id=1, source_target_pairs={{0,1},{1,2},{2,3},{3,4},{4,5},{5,6},{6,7},{7,8},{8,9},{9,10},{10,1... | collective-permute-start | bytes 2998280 | tf_op jit(solution)/shard_map/ppermute | solution.py:521
  16.3 24.2 %collective-permute-start.1 = (f32[60,16,256]{2,1,0:T(8,128)S(1)}, f32[60,16,256]{2,1,0:T(8,128)S(1)}, u32[]{:S(2)}, u32[]{:S(2)}) collective-permute-start(f32[60,16,256]{2,1,0:T(8,128)S(1)} %get-tuple-element.9), channel_id=1, source_target_pairs={{1,0},{2,1},{3,2},{4,3},{5,4},{6,5},{7,6},{8,7},{9,8},{10,9},{11,1... | collective-permute-start | bytes 2949128 | tf_op jit(solution)/shard_map/ppermute | solution.py:522

commit v4 on v1

--- a/solution.py
+++ b/solution.py
@@ -14,8 +14,12 @@
 RING = ("star", "blk")
 LANES = 128
 METRIC = 18
+EARLY = 5
+LATE = 13
 FLUID = 7
-ANY = pl.BlockSpec(memory_space=pl.ANY)
+HBM = pl.BlockSpec(memory_space=pltpu.HBM)
+GRANT = 24 * 1024 * 1024
+VMEM = pl.BlockSpec(memory_space=pltpu.VMEM)
 F32 = jnp.float32
 
 
@@ -40,34 +44,25 @@
             self.wait(group)
 
 
-def metric_pieces(lapse, conf, mean, metric, curv, shift):
-    singles = [(n, None, ref) for n, ref in enumerate((lapse, conf, mean))]
-    return singles + [(3, 6, metric), (9, 6, curv), (15, 3, shift)]
-
-
-def pack_kernel(lapse, conf, mean, metric, curv, shift, dens, mom, ener, velo, pres, up, down, sems):
+def pack_kernel(lapse, conf, shift, dens, mom, ener, velo, pres, up, down, sems):
     nx = lapse.shape[0]
     fx = dens.shape[1]
     copies = Copies(sems)
     for buf, first, fluid_first in ((up, nx - 2, fx - 3), (down, 0, 0)):
         for k in range(2):
-            for field, count, ref in metric_pieces(lapse, conf, mean, metric, curv, shift):
-                at = k * METRIC + field
-                if count is None:
-                    copies.start(0, ref.at[first + k], buf.at[at])
-                else:
-                    copies.start(0, ref.at[:, first + k], buf.at[pl.ds(at, count)])
+            at = k * EARLY
+            copies.start(0, lapse.at[first + k], buf.at[at])
+            copies.start(0, conf.at[first + k], buf.at[at + 1])
+            copies.start(0, shift.at[:, first + k], buf.at[pl.ds(at + 2, 3)])
         for k in range(3):
-            at = 2 * METRIC + k * FLUID
+            at = 2 * EARLY + k * FLUID
             row = fluid_first + k
             copies.start(0, dens.at[0, row], buf.at[at])
             copies.start(0, mom.at[0, :, row], buf.at[pl.ds(at + 1, 3)])
             copies.start(0, ener.at[0, row], buf.at[at + 4])
             copies.start(0, velo.at[0, 0, row], buf.at[at + 5])
             copies.start(0, pres.at[0, row], buf.at[at + 6])
-    tail = 2 * METRIC + 3 * FLUID
-    for k in range(2):
-        copies.start(0, velo.at[0, pl.ds(1, 2), fx - 2 + k], up.at[pl.ds(tail + 2 * k, 2)])
+    tail = 2 * EARLY + 3 * FLUID
     copies.start(0, lapse.at[2], down.at[tail])
     copies.start(0, shift.at[0, 2], down.at[tail + 1])
     copies.start(0, conf.at[2], down.at[tail + 2])
@@ -192,8 +187,8 @@
     return jnp.dot(x, y, precision=lax.Precision.HIGHEST, preferred_element_type=F32)
 
 
-def restrict_planes(pairs, rows, out, out_first):
-    ny, nz = out.shape[-2:]
+def restrict_planes(pairs, rows, outs):
+    ny, nz = outs[0][0].shape[-2:]
     half = ny // 2
     quarter_y, quarter_z = ny // 4, nz // 4
     count = len(pairs)
@@ -208,9 +203,9 @@
         nz, lambda r, c: jnp.where(c == quarter_z + lax.shift_right_logical(r, 1), 0.125, 0.0).astype(F32)
     )
     level = dot(jnp.concatenate(halves, axis=1), matrix)
-    for n in range(count):
-        out[out_first + n] = jnp.zeros((ny, nz), F32)
-        out[out_first + n, pl.ds(quarter_y, half), :] = level[n * half : (n + 1) * half]
+    for n, (out, at) in enumerate(outs):
+        out[at] = jnp.zeros((ny, nz), F32)
+        out[at, pl.ds(quarter_y, half), :] = level[n * half : (n + 1) * half]
 
 
 def prolong_yz(planes, rows, out):
@@ -313,43 +308,50 @@
 
 def local_kernel(
     lapse, conf, mean, metric, curv, shift, dens, mom, ener, velo, pres,
-    rates, hydro, flux_out, source_out,
-    state, fluid, coarse, flux, sources, rows, stage, hstage, sems,
+    rates, hydro, state, flux, sources, up, down,
+    fluid, coarse, rows, stage, hstage, sems,
 ):
     nx, ny, nz = lapse.shape
     fx = dens.shape[1]
     copies = Copies(sems)
-    copies.start("c", lapse, state.at[0])
-    copies.start("c", conf, state.at[1])
-    copies.start("c", shift, state.at[pl.ds(15, 3)])
+    inner = pl.ds(2, nx)
+    copies.start("c", lapse, state.at[0, inner])
+    copies.start("c", conf, state.at[1, inner])
+    copies.start("c", shift, state.at[pl.ds(15, 3), inner])
     copies.start("f", dens.at[0], fluid.at[0])
     copies.start("f", mom.at[0], fluid.at[pl.ds(1, 3)])
     copies.start("f", ener.at[0], fluid.at[4])
     copies.start("f", velo.at[0, 0], fluid.at[5])
     copies.start("f", pres.at[0], fluid.at[6])
     copies.start("f", velo.at[0, pl.ds(1, 2)], fluid.at[pl.ds(7, 2)])
-    copies.start("m", mean, state.at[2])
-    copies.start("m", metric, state.at[pl.ds(3, 6)])
-    copies.start("m", curv, state.at[pl.ds(9, 6)])
+    copies.start("m", mean, state.at[2, inner])
+    copies.start("m", metric, state.at[pl.ds(3, 6), inner])
+    copies.start("m", curv, state.at[pl.ds(9, 6), inner])
+    for buf, first in ((up, nx - 2), (down, 0)):
+        for k in range(2):
+            copies.start("o", mean.at[first + k], buf.at[k * LATE])
+            copies.start("o", metric.at[:, first + k], buf.at[pl.ds(k * LATE + 1, 6)])
+            copies.start("o", curv.at[:, first + k], buf.at[pl.ds(k * LATE + 7, 6)])
+
+    @pl.loop(2, 15)
+    def _(n):
+        for k in (0, 1, nx + 2, nx + 3):
+            state[n, k] = jnp.zeros((ny, nz), F32)
 
     copies.wait("c")
 
     def coarse_plane(field, layer):
-        return lambda sl: state[field, layer, sl, :]
+        return lambda sl: state[field, layer + 2, sl, :]
 
     prolong_yz([[coarse_plane(f, l) for l in range(nx)] for f in (0, 15, 1)], rows, coarse)
     copies.wait("f")
 
-    good = fx - 3
-
-    @pl.loop(0, good)
+    @pl.loop(0, fx - 3)
     def _(i):
         mid = lax.shift_right_logical(i, 1) + 1
         side = mid - 1 + 2 * (i & 1)
         parts = [0.75 * coarse[n, mid] + 0.25 * coarse[n, side] for n in range(3)]
-        split_flux(lambda n: fluid[n, i], *parts, flux, i)
-
-    copies.start("o", flux, flux_out)
+        split_flux(lambda n: fluid[n, i], *parts, flux, i + 3)
 
     def pair(layer):
         def one(x):
@@ -362,8 +364,12 @@
 
         return lambda: one(2 * layer) + one(2 * layer + 1)
 
-    restrict_planes([pair(l) for l in range(nx - 1)], rows, sources, 1)
-    copies.start("o", sources, source_out)
+    restrict_planes(
+        [pair(l) for l in range(nx)],
+        rows,
+        [(sources, l + 1) for l in range(nx - 1)] + [(up, 2 * LATE)],
+    )
+    sources[0] = jnp.zeros((ny, nz), F32)
 
     @pl.loop(0, 5)
     def _(n):
@@ -371,60 +377,49 @@
             sl = pl.ds(part * 8, 8)
 
             def emit(i, value):
-                hstage[n, i - 3, sl, :] = value
-
-            weno_cells(flux, n, sl, 3, fx - 9, emit)
+                hstage[n, i - 6, sl, :] = value
+
+            weno_cells(flux, n, sl, 6, fx - 9, emit)
 
     copies.start("o", hstage, hydro.at[0, :, pl.ds(3, fx - 9)])
     copies.wait("m")
 
     @pl.loop(0, nx - 4)
     def _(l):
-        bssn_layer(state, sources, stage, l + 2, l + 2, l)
+        bssn_layer(state, sources, stage, l + 4, l + 2, l)
 
     copies.start("o", stage, rates.at[:, pl.ds(2, nx - 4)])
     copies.wait_all()
 
 
 def halo_kernel(
-    inside, below, above, rates_in, hydro_in, flux_in, source_in,
-    lapse, conf, mean, metric, curv, shift, dens, mom, ener, velo, pres,
-    rates, hydro,
-    state, extra, own, fbelow, fabove, coarse, flux, sources, rows, stage, hstage, sems,
+    below, above, hydro_in, state_in, flux_in, sources, dens, mom, ener, velo, pres,
+    hydro, state, flux, stage,
+    own, coarse, rows, hstage, sems,
 ):
-    nx, ny, nz = lapse.shape
+    nx = sources.shape[0]
+    ny, nz = sources.shape[-2:]
     fx = dens.shape[1]
     copies = Copies(sems)
-    tail = 2 * METRIC + 3 * FLUID
-    for k in range(2):
-        copies.start("m", below.at[pl.ds(k * METRIC, METRIC)], state.at[:, k])
-        copies.start("m", above.at[pl.ds(k * METRIC, METRIC)], state.at[:, nx + 2 + k])
-    for field, count, ref in metric_pieces(lapse, conf, mean, metric, curv, shift):
-        if count is None:
-            copies.start("m", ref, state.at[field, pl.ds(2, nx)])
-        else:
-            copies.start("m", ref, state.at[pl.ds(field, count), pl.ds(2, nx)])
-    copies.start("m", above.at[pl.ds(tail, 3)], extra)
-    for k in range(3):
-        copies.start("f", below.at[pl.ds(2 * METRIC + k * FLUID, FLUID)], fbelow.at[pl.ds(0, FLUID), k])
-        copies.start("f", above.at[pl.ds(2 * METRIC + k * FLUID, FLUID)], fabove.at[:, k])
-    for k in range(2):
-        copies.start("f", below.at[pl.ds(tail + 2 * k, 2)], fbelow.at[pl.ds(FLUID, 2), k + 1])
     last = pl.ds(fx - 3, 3)
     copies.start("f", dens.at[0, last], own.at[0])
     copies.start("f", mom.at[0, :, last], own.at[pl.ds(1, 3)])
     copies.start("f", ener.at[0, last], own.at[4])
     copies.start("f", velo.at[0, 0, last], own.at[5])
     copies.start("f", pres.at[0, last], own.at[6])
-    copies.start("s", source_in, sources)
-    copies.start("x", flux_in.at[:, pl.ds(0, 6)], flux.at[:, pl.ds(3, 6)])
-    copies.start("x", flux_in.at[:, pl.ds(fx - 9, 6)], flux.at[:, pl.ds(fx - 6, 6)])
-
-    copies.wait("m")
+    place = lax.axis_index("blk")
+    inside = (
+        jnp.where(place > 0, 1.0, 0.0).astype(F32),
+        jnp.where(place < lax.axis_size("blk") - 1, 1.0, 0.0).astype(F32),
+    )
+    for k in range(2):
+        for n, field in enumerate((0, 1, 15, 16, 17)):
+            state[field, k] = below[k * EARLY + n]
+            state[field, nx + 2 + k] = above[k * EARLY + n]
 
     def coarse_plane(field, layer):
         if layer == nx + 2:
-            return lambda sl: extra[(0, 15, 1).index(field), sl, :]
+            return lambda sl: above[2 * EARLY + 3 * FLUID + (0, 15, 1).index(field), sl, :]
         return lambda sl: state[field, layer + 2, sl, :]
 
     layers = (-1, 0, 1, nx - 1, nx, nx + 1, nx + 2)
@@ -437,14 +432,15 @@
         mid, side = layers.index(mid), layers.index(side)
         parts = [0.75 * coarse[n, mid] + 0.25 * coarse[n, side] for n in range(3)]
         if i < 0:
-            source, at, scale = fbelow, i + 3, inside[0]
+            fluid = lambda n, at=2 * EARLY + (i + 3) * FLUID: below[at + n]
+            scale = inside[0]
         elif i < fx:
-            source, at, scale = own, i - fx + 3, None
+            fluid = lambda n, at=i - fx + 3: own[n, at]
+            scale = None
         else:
-            source, at, scale = fabove, i - fx, inside[1]
-        split_flux(lambda n, s=source, a=at: s[n, a], *parts, flux, i + 3, scale)
-
-    copies.wait("x")
+            fluid = lambda n, at=2 * EARLY + (i - fx) * FLUID: above[at + n]
+            scale = inside[1]
+        split_flux(fluid, *parts, flux, i + 3, scale)
 
     @pl.loop(0, 5)
     def _(n):
@@ -462,33 +458,48 @@
 
     copies.start("o", hstage.at[:, pl.ds(0, 3)], hydro.at[0, :, pl.ds(0, 3)])
     copies.start("o", hstage.at[:, pl.ds(3, 6)], hydro.at[0, :, pl.ds(fx - 6, 6)])
-    copies.wait("s")
-
-    def pair():
-        def one(x):
-            return (
-                fbelow[4, x]
-                + fbelow[0, x]
-                + (fbelow[1, x] * fbelow[5, x] + fbelow[2, x] * fbelow[7, x] + fbelow[3, x] * fbelow[8, x])
-                + 3.0 * fbelow[6, x]
-            )
-
-        return one(1) + one(2)
-
-    restrict_planes([pair], rows, sources, 0)
 
     @pl.loop(0, 4)
     def _(k):
         l = jnp.where(k < 2, k, k + nx - 4)
         bssn_layer(state, sources, stage, l + 2, l, k)
 
+    copies.wait_all()
+
+
+def late_kernel(below, above, stage_in, lapse, shift, rates_in, rates, stage, edge, sems):
+    nx = lapse.shape[0]
+    copies = Copies(sems)
+    copies.start("i", shift.at[0, pl.ds(0, 2)], edge.at[pl.ds(0, 2)])
+    copies.start("i", shift.at[0, pl.ds(nx - 2, 2)], edge.at[pl.ds(2, 2)])
+    copies.start("i", lapse.at[0], edge.at[4])
+    copies.wait("i")
+    steps = [edge[k] * (1.0 / 12.0) for k in range(4)]
+    for field in range(15):
+        late = field - 2
+        for k in range(4):
+            value = stage_in[field, k]
+            if late >= 0:
+                if k == 0:
+                    tap = below[late] - 8.0 * below[LATE + late]
+                elif k == 1:
+                    tap = below[LATE + late]
+                elif k == 2:
+                    tap = -above[late]
+                else:
+                    tap = 8.0 * above[late] - above[LATE + late]
+                value = value + steps[k] * tap
+            if field == 2 and k == 0:
+                value = value + (4.0 * math.pi) * edge[4] * below[2 * LATE]
+            stage[field, k] = value
     copies.start("o", stage.at[:, pl.ds(0, 2)], rates.at[:, pl.ds(0, 2)])
     copies.start("o", stage.at[:, pl.ds(2, 2)], rates.at[:, pl.ds(nx - 2, 2)])
     copies.wait_all()
 
 
 def on_device(*fields):
-    lapse, dens = fields[0], fields[6]
+    fields = [pltpu.with_memory_space_constraint(field, pltpu.HBM) for field in fields]
+    lapse, conf, mean, metric, curv, shift, dens, mom, ener, velo, pres = fields
     nx, ny, nz = lapse.shape
     fx = dens.shape[1]
     layer = (ny, nz)
@@ -499,67 +510,79 @@
     def vmem(*leading):
         return pltpu.VMEM(leading + layer, F32)
 
-    tail = 2 * METRIC + 3 * FLUID
-    up, down = pl.pallas_call(
-        pack_kernel,
-        out_shape=(shape(tail + 4), shape(tail + 3)),
-        in_specs=[ANY] * 11,
-        out_specs=[ANY] * 2,
-        scratch_shapes=[pltpu.SemaphoreType.DMA((64,))],
-        name="pack",
-    )(*fields)
+    def row_scratch(planes):
+        return pltpu.VMEM((nz // LANES, planes * ny, LANES), F32)
+
+    def sems(n):
+        return pltpu.SemaphoreType.DMA((n,))
+
     count = lax.axis_size(RING)
     pairs = [(i, (i + 1) % count) for i in range(count)]
-    below = lax.ppermute(up, RING, pairs)
-    above = lax.ppermute(down, RING, [(j, i) for i, j in pairs])
-
-    def row_scratch(planes):
-        return pltpu.VMEM((nz // LANES, planes * ny, LANES), F32)
-
-    partial = pl.pallas_call(
+
+    def exchanged(up, down):
+        return lax.ppermute(up, RING, pairs), lax.ppermute(down, RING, [(j, i) for i, j in pairs])
+
+    params = pltpu.CompilerParams(vmem_limit_bytes=GRANT)
+    early = 2 * EARLY + 3 * FLUID
+    early_halo = exchanged(
+        *pl.pallas_call(
+            pack_kernel,
+            out_shape=(shape(early), shape(early + 3)),
+            in_specs=[HBM] * 8,
+            out_specs=[VMEM] * 2,
+            scratch_shapes=[sems(48)],
+            compiler_params=params,
+            name="pack",
+        )(lapse, conf, shift, dens, mom, ener, velo, pres)
+    )
+    rates, hydro, state, flux, sources, up, down = pl.pallas_call(
         local_kernel,
-        out_shape=(shape(15, nx), shape(1, 5, fx), shape(10, fx - 3), shape(nx)),
-        in_specs=[ANY] * 11,
-        out_specs=[ANY] * 4,
+        out_shape=(
+            shape(15, nx),
+            shape(1, 5, fx),
+            shape(METRIC, nx + 4),
+            shape(10, fx + 6),
+            shape(nx),
+            shape(2 * LATE + 1),
+            shape(2 * LATE),
+        ),
+        in_specs=[HBM] * 11,
+        out_specs=[HBM] * 2 + [VMEM] * 5,
         scratch_shapes=[
-            vmem(METRIC, nx),
             vmem(9, fx),
             vmem(3, nx),
-            vmem(10, fx - 3),
-            vmem(nx),
             row_scratch(3 * nx),
             vmem(15, nx - 4),
             vmem(5, fx - 9),
-            pltpu.SemaphoreType.DMA((32,)),
+            sems(32),
         ],
         cost_estimate=pl.CostEstimate(flops=400_000_000, transcendentals=0, bytes_accessed=12_000_000),
+        compiler_params=params,
         name="local",
     )(*fields)
-    place = lax.axis_index("blk")
-    inside = jnp.stack([place > 0, place < lax.axis_size("blk") - 1]).astype(F32)
-    return pl.pallas_call(
+    late_halo = exchanged(up, down)
+    hydro, _, _, stage = pl.pallas_call(
         halo_kernel,
-        out_shape=(shape(15, nx), shape(1, 5, fx)),
-        in_specs=[pl.BlockSpec(memory_space=pltpu.SMEM)] + [ANY] * 17,
-        out_specs=[ANY] * 2,
-        input_output_aliases={3: 0, 4: 1},
-        scratch_shapes=[
-            vmem(METRIC, nx + 4),
-            vmem(3),
-            vmem(FLUID, 3),
-            vmem(9, 3),
-            vmem(FLUID, 3),
-            vmem(3, 7),
-            vmem(10, fx + 6),
-            vmem(nx),
-            row_scratch(21),
-            vmem(15, 4),
-            vmem(5, 9),
-            pltpu.SemaphoreType.DMA((64,)),
-        ],
+        out_shape=(shape(1, 5, fx), shape(METRIC, nx + 4), shape(10, fx + 6), shape(15, 4)),
+        in_specs=[VMEM] * 2 + [HBM] + [VMEM] * 3 + [HBM] * 5,
+        out_specs=[HBM] + [VMEM] * 3,
+        input_output_aliases={2: 0, 3: 1, 4: 2},
+        scratch_shapes=[vmem(FLUID, 3), vmem(3, 7), row_scratch(21), vmem(5, 9), sems(16)],
         cost_estimate=pl.CostEstimate(flops=400_000_000, transcendentals=0, bytes_accessed=12_000_000),
+        compiler_params=params,
         name="halo",
-    )(inside, below, above, *partial, *fields)
+    )(*early_halo, hydro, state, flux, sources, dens, mom, ener, velo, pres)
+    rates = pl.pallas_call(
+        late_kernel,
+        out_shape=shape(15, nx),
+        in_specs=[VMEM] * 3 + [HBM] * 3,
+        out_specs=HBM,
+        input_output_aliases={5: 0},
+        scratch_shapes=[vmem(15, 4), vmem(5), sems(8)],
+        compiler_params=params,
+        name="late",
+    )(*late_halo, stage, lapse, shift, rates)
+    return rates, hydro
 
 
 def solution(mesh):

time: 101 us -> 31.6 us (0.31)
  Pallas kernels: 80.5 us -> 18.3 us
  waiting for transfers between devices: 15.6 us -> 5.77 us
  starting transfers between devices: 2.67 us -> 6.59 us
  local copies, waits for them, and re-layouts: 1.28 us -> 0 us
    pallas_call x2 -> x3, Pallas kernels: 72.3 us -> 9.94 us  [the longest x1 6.42 us: on_device(): pl.pallas_call(halo_kernel, out_shape=(shape(1, 5, fx), shape(METRIC, nx...]
    ppermute x2 -> x4, waiting for transfers between devices: 15.6 us -> 5.77 us  [the longest x2 5.77 us: exchanged(): lax.ppermute(down, RING, [(j, i) for i, j in pairs])]
    ppermute x2 -> x4, starting transfers between devices: 2.67 us -> 6.59 us  [the longest x2 3.43 us: exchanged(): lax.ppermute(down, RING, [(j, i) for i, j in pairs])]
    unnamed x4 -> x0, local copies, waits for them, and re-layouts: 1.28 us -> none
  transfers between devices with their start and end apart: 2 -> 4, of which waited for: 1 -> 1; matrix products, arithmetic and copies ran while one was open for 1% -> 0% of each run, Pallas kernels for 8% -> 47%
where the time goes in v4:
time: 31.6 us; the launch traced here: 31.3 us
  Pallas kernels  18.3 us (58%)
  starting transfers between devices  6.59 us (21%)
  waiting for transfers between devices  5.77 us (18%)
  between operations  0.66 us (2%)
    pallas_call x1, Pallas kernels, on_device(): pl.pallas_call(local_kernel, out_shape=(shape(15, nx), shape(1, 5, fx), s...  8.31 us
    pallas_call x1, Pallas kernels, on_device(): pl.pallas_call(halo_kernel, out_shape=(shape(1, 5, fx), shape(METRIC, nx...  6.42 us
    ppermute x2, waiting for transfers between devices, exchanged(): lax.ppermute(down, RING, [(j, i) for i, j in pairs])  5.77 us
    ppermute x2, starting transfers between devices, exchanged(): lax.ppermute(down, RING, [(j, i) for i, j in pairs])  3.43 us
    ppermute x2, starting transfers between devices, exchanged(): lax.ppermute(up, RING, pairs)  3.17 us
    pallas_call x1, Pallas kernels, on_device(): pl.pallas_call(late_kernel, out_shape=shape(15, nx), in_specs=[VMEM] * 3...  1.89 us
    pallas_call x1, Pallas kernels, on_device(): pl.pallas_call(pack_kernel, out_shape=(shape(early), shape(early + 3)), i...  1.63 us
  transfers between devices with their start and end apart: 4, of which 1 were waited for; matrix products, arithmetic and copies ran while one was open for 0% of the time, Pallas kernels for 47%

profile of v4, /device:TPU:1, one launch (start us, length us, event | category | flops | bytes accessed | tf_op | source)
XLA Modules:
  0.0 31.3 jit_solution(3794106289633959718)
XLA Ops:
  0.6 1.6 %pack.1 = (f32[31,16,256]{2,1,0:T(8,128)S(1)}, f32[34,16,256]{2,1,0:T(8,128)S(1)}) custom-call(f32[8,16,256]{2,1,0:T(8,128)} %lapse.5, f32[8,16,256]{2,1,0:T(8,128)} %conf.3, f32[3,8,16,256]{3,2,1,0:T(8,128)} %shift.5, f32[1,16,16,256]{3,2,1,0:T(8,128)} %dens.5, f32[1,3,16,16,256]{4,3,2,1,0:T(8,128)} %mom.5, f32[1,16,16,256]{3,2,1,0:T(8,128)} %ener.5, ...), custom_call_target="tpu_custom_call" | custom-call | tf_op jit(solution)/shard_map/pack/pallas_call | solution.py:528
  2.3 0.1 collective-permute-start.3
  2.3 2.7 %collective-permute-start.2 = (f32[31,16,256]{2,1,0:T(8,128)S(1)}, f32[31,16,256]{2,1,0:T(8,128)S(1)}, u32[]{:S(2)}, u32[]{:S(2)}) collective-permute-start(f32[31,16,256]{2,1,0:T(8,128)S(1)} %get-tuple-element.15), channel_id=1, source_target_pairs={{0,1},{1,2},{2,3},{3,4},{4,5},{5,6},{6,7},{7,8},{8,9},{9,10},{10,1... | collective-permute-start | bytes 1523720 | tf_op jit(solution)/shard_map/ppermute | solution.py:523
  5.0 8.3 %local.1 = (f32[15,8,16,256]{3,2,1,0:T(8,128)}, f32[1,5,16,16,256]{4,3,2,1,0:T(8,128)}, f32[18,12,16,256]{3,2,1,0:T(8,128)S(1)}, f32[10,22,16,256]{3,2,1,0:T(8,1...) custom-call(f32[8,16,256]{2,1,0:T(8,128)} %lapse.5, ...), custom_call_target="tpu_custom_call" | custom-call | flops 400000000 | bytes 12000000 | tf_op jit(solution)/shard_map/local/pallas_call | solution.py:538
  13.3 0.5 %collective-permute-start = (f32[27,16,256]{2,1,0:T(8,128)S(1)}, f32[27,16,256]{2,1,0:T(8,128)S(1)}, u32[]{:S(2)}, u32[]{:S(2)}) collective-permute-start(f32[27,16,256]{2,1,0:T(8,128)S(1)} %get-tuple-element.13), channel_id=1, source_target_pairs={{0,1},{1,2},{2,3},{3,4},{4,5},{5,6},{6,7},{7,8},{8,9},{9,10},{10,1... | collective-permute-start | bytes 1327112 | tf_op jit(solution)/shard_map/ppermute | solution.py:523
  13.8 3.4 %collective-permute-start.1 = (f32[26,16,256]{2,1,0:T(8,128)S(1)}, f32[26,16,256]{2,1,0:T(8,128)S(1)}, u32[]{:S(2)}, u32[]{:S(2)}) collective-permute-start(f32[26,16,256]{2,1,0:T(8,128)S(1)} %get-tuple-element.14), channel_id=1, source_target_pairs={{1,0},{2,1},{3,2},{4,3},{5,4},{6,5},{7,6},{8,7},{9,8},{10,9},{11,1... | collective-permute-start | bytes 1277960 | tf_op jit(solution)/shard_map/ppermute | solution.py:523
  17.2 0.0 collective-permute-done.2.below
  17.2 0.0 collective-permute-done.3.above
  17.2 6.4 %halo.1 = (f32[1,5,16,16,256]{4,3,2,1,0:T(8,128)}, f32[18,12,16,256]{3,2,1,0:T(8,128)S(1)}, f32[10,22,16,256]{3,2,1,0:T(8,128)S(1)}, f32[15,4,16,256]{3,2,1,0:T(8,128)S(1)}) custom-call(f32[31,16,256]{2,1,0:T(8,128)S(1)} %collective-permute-done.2.below, ...), custom_call_target="tpu_custom_call", output_to_operand_aliasing={{0}: (2, {}), {1}: (3, {}), {2}: (4, {})} | custom-call | flops 400000000 | bytes 12000000 | tf_op jit(solution)/shard_map/halo/pallas_call | solution.py:564
  23.6 5.8 %collective-permute-done.1.above = f32[26,16,256]{2,1,0:T(8,128)S(1)} collective-permute-done((f32[26,16,256]{2,1,0:T(8,128)S(1)}, f32[26,16,256]{2,1,0:T(8,128)S(1)}, u32[]{:S(2)}, u32[]{:S(2)}) %collective-permute-start.1) | collective-permute-done | bytes 426016 | tf_op jit(solution)/shard_map/ppermute | solution.py:523
  29.4 0.0 collective-permute-done.below
  29.4 1.9 %late.1 = f32[15,8,16,256]{3,2,1,0:T(8,128)} custom-call(f32[27,16,256]{2,1,0:T(8,128)S(1)} %collective-permute-done.below, f32[26,16,256]{2,1,0:T(8,128)S(1)} %collective-permute-done.1.above, f32[15,4,16,256]{3,2,1,0:T(8,128)S(1)} %get-tuple-element.21.stage_in, f32[8,16,256]{2,1,0:T(8,128)} %lapse.5, ...), custom_call_target="tpu_custom_call", output_to_operand_aliasing={{}: (5, {})} | custom-call | tf_op jit(solution)/shard_map/late/pallas_call | solution.py:575
Async XLA Ops:
  2.3 14.9 %collective-permute-start.3 = (f32[34,16,256]{2,1,0:T(8,128)S(1)}, f32[34,16,256]{2,1,0:T(8,128)S(1)}, u32[]{:S(2)}, u32[]{:S(2)}) collective-permute-start(f32[34,16,256]{2,1,0:T(8,128)S(1)} %get-tuple-element.16), channel_id=1, source_target_pairs={{1,0},{2,1},{3,2},{4,3},{5,4},{6,5},{7,6},{8,7},{9,8},{10,9},{11,1... | collective-permute-start | bytes 1671176 | tf_op jit(solution)/shard_map/ppermute | solution.py:523
  2.3 14.8 %collective-permute-start.2 = (f32[31,16,256]{2,1,0:T(8,128)S(1)}, f32[31,16,256]{2,1,0:T(8,128)S(1)}, u32[]{:S(2)}, u32[]{:S(2)}) collective-permute-start(f32[31,16,256]{2,1,0:T(8,128)S(1)} %get-tuple-element.15), channel_id=1, source_target_pairs={{0,1},{1,2},{2,3},{3,4},{4,5},{5,6},{6,7},{7,8},{8,9},{9,10},{10,1... | collective-permute-start | bytes 1523720 | tf_op jit(solution)/shard_map/ppermute | solution.py:523
  13.3 16.1 %collective-permute-start = (f32[27,16,256]{2,1,0:T(8,128)S(1)}, f32[27,16,256]{2,1,0:T(8,128)S(1)}, u32[]{:S(2)}, u32[]{:S(2)}) collective-permute-start(f32[27,16,256]{2,1,0:T(8,128)S(1)} %get-tuple-element.13), channel_id=1, source_target_pairs={{0,1},{1,2},{2,3},{3,4},{4,5},{5,6},{6,7},{7,8},{8,9},{9,10},{10,1... | collective-permute-start | bytes 1327112 | tf_op jit(solution)/shard_map/ppermute | solution.py:523
  13.8 15.6 %collective-permute-start.1 = (f32[26,16,256]{2,1,0:T(8,128)S(1)}, f32[26,16,256]{2,1,0:T(8,128)S(1)}, u32[]{:S(2)}, u32[]{:S(2)}) collective-permute-start(f32[26,16,256]{2,1,0:T(8,128)S(1)} %get-tuple-element.14), channel_id=1, source_target_pairs={{1,0},{2,1},{3,2},{4,3},{5,4},{6,5},{7,6},{8,7},{9,8},{10,9},{11,1... | collective-permute-start | bytes 1277960 | tf_op jit(solution)/shard_map/ppermute | solution.py:523

commit v5 on v4

--- a/solution.py
+++ b/solution.py
@@ -48,20 +48,19 @@
     nx = lapse.shape[0]
     fx = dens.shape[1]
     copies = Copies(sems)
+    layer = lapse.shape[1:]
     for buf, first, fluid_first in ((up, nx - 2, fx - 3), (down, 0, 0)):
-        for k in range(2):
-            at = k * EARLY
-            copies.start(0, lapse.at[first + k], buf.at[at])
-            copies.start(0, conf.at[first + k], buf.at[at + 1])
-            copies.start(0, shift.at[:, first + k], buf.at[pl.ds(at + 2, 3)])
-        for k in range(3):
-            at = 2 * EARLY + k * FLUID
-            row = fluid_first + k
-            copies.start(0, dens.at[0, row], buf.at[at])
-            copies.start(0, mom.at[0, :, row], buf.at[pl.ds(at + 1, 3)])
-            copies.start(0, ener.at[0, row], buf.at[at + 4])
-            copies.start(0, velo.at[0, 0, row], buf.at[at + 5])
-            copies.start(0, pres.at[0, row], buf.at[at + 6])
+        rows = pl.ds(first, 2)
+        copies.start(0, lapse.at[rows], buf.at[pl.ds(0, 2)])
+        copies.start(0, conf.at[rows], buf.at[pl.ds(2, 2)])
+        copies.start(0, shift.at[:, rows], buf.at[pl.ds(4, 6)].reshape(3, 2, *layer))
+        rows = pl.ds(fluid_first, 3)
+        at = 2 * EARLY
+        copies.start(0, dens.at[0, rows], buf.at[pl.ds(at, 3)])
+        copies.start(0, mom.at[0, :, rows], buf.at[pl.ds(at + 3, 9)].reshape(3, 3, *layer))
+        copies.start(0, ener.at[0, rows], buf.at[pl.ds(at + 12, 3)])
+        copies.start(0, velo.at[0, 0, rows], buf.at[pl.ds(at + 15, 3)])
+        copies.start(0, pres.at[0, rows], buf.at[pl.ds(at + 18, 3)])
     tail = 2 * EARLY + 3 * FLUID
     copies.start(0, lapse.at[2], down.at[tail])
     copies.start(0, shift.at[0, 2], down.at[tail + 1])
@@ -308,8 +307,8 @@
 
 def local_kernel(
     lapse, conf, mean, metric, curv, shift, dens, mom, ener, velo, pres,
-    rates, hydro, state, flux, sources, up, down,
-    fluid, coarse, rows, stage, hstage, sems,
+    state, flux, sources, up, down,
+    fluid, coarse, rows, sems,
 ):
     nx, ny, nz = lapse.shape
     fx = dens.shape[1]
@@ -371,6 +370,14 @@
     )
     sources[0] = jnp.zeros((ny, nz), F32)
 
+    copies.wait_all()
+
+
+def inner_kernel(state, flux, sources, rates, hydro, stage, hstage, sems):
+    nx, ny, nz = sources.shape
+    fx = hydro.shape[2]
+    copies = Copies(sems)
+
     @pl.loop(0, 5)
     def _(n):
         for part in range(ny // 8):
@@ -382,8 +389,6 @@
             weno_cells(flux, n, sl, 6, fx - 9, emit)
 
     copies.start("o", hstage, hydro.at[0, :, pl.ds(3, fx - 9)])
-    copies.wait("m")
-
     @pl.loop(0, nx - 4)
     def _(l):
         bssn_layer(state, sources, stage, l + 4, l + 2, l)
@@ -414,8 +419,8 @@
     )
     for k in range(2):
         for n, field in enumerate((0, 1, 15, 16, 17)):
-            state[field, k] = below[k * EARLY + n]
-            state[field, nx + 2 + k] = above[k * EARLY + n]
+            state[field, k] = below[2 * n + k]
+            state[field, nx + 2 + k] = above[2 * n + k]
 
     def coarse_plane(field, layer):
         if layer == nx + 2:
@@ -432,13 +437,13 @@
         mid, side = layers.index(mid), layers.index(side)
         parts = [0.75 * coarse[n, mid] + 0.25 * coarse[n, side] for n in range(3)]
         if i < 0:
-            fluid = lambda n, at=2 * EARLY + (i + 3) * FLUID: below[at + n]
+            fluid = lambda n, at=2 * EARLY + i + 3: below[at + 3 * n]
             scale = inside[0]
         elif i < fx:
             fluid = lambda n, at=i - fx + 3: own[n, at]
             scale = None
         else:
-            fluid = lambda n, at=2 * EARLY + (i - fx) * FLUID: above[at + n]
+            fluid = lambda n, at=2 * EARLY + i - fx: above[at + 3 * n]
             scale = inside[1]
         split_flux(fluid, *parts, flux, i + 3, scale)
 
@@ -467,14 +472,10 @@
     copies.wait_all()
 
 
-def late_kernel(below, above, stage_in, lapse, shift, rates_in, rates, stage, edge, sems):
-    nx = lapse.shape[0]
+def late_kernel(below, above, stage_in, state, rates_in, rates, stage, sems):
+    nx = rates.shape[1]
     copies = Copies(sems)
-    copies.start("i", shift.at[0, pl.ds(0, 2)], edge.at[pl.ds(0, 2)])
-    copies.start("i", shift.at[0, pl.ds(nx - 2, 2)], edge.at[pl.ds(2, 2)])
-    copies.start("i", lapse.at[0], edge.at[4])
-    copies.wait("i")
-    steps = [edge[k] * (1.0 / 12.0) for k in range(4)]
+    steps = [state[15, at] * (1.0 / 12.0) for at in (2, 3, nx, nx + 1)]
     for field in range(15):
         late = field - 2
         for k in range(4):
@@ -490,7 +491,7 @@
                     tap = 8.0 * above[late] - above[LATE + late]
                 value = value + steps[k] * tap
             if field == 2 and k == 0:
-                value = value + (4.0 * math.pi) * edge[4] * below[2 * LATE]
+                value = value + (4.0 * math.pi) * state[0, 2] * below[2 * LATE]
             stage[field, k] = value
     copies.start("o", stage.at[:, pl.ds(0, 2)], rates.at[:, pl.ds(0, 2)])
     copies.start("o", stage.at[:, pl.ds(2, 2)], rates.at[:, pl.ds(nx - 2, 2)])
@@ -535,11 +536,9 @@
             name="pack",
         )(lapse, conf, shift, dens, mom, ener, velo, pres)
     )
-    rates, hydro, state, flux, sources, up, down = pl.pallas_call(
+    state, flux, sources, up, down = pl.pallas_call(
         local_kernel,
         out_shape=(
-            shape(15, nx),
-            shape(1, 5, fx),
             shape(METRIC, nx + 4),
             shape(10, fx + 6),
             shape(nx),
@@ -547,21 +546,24 @@
             shape(2 * LATE),
         ),
         in_specs=[HBM] * 11,
-        out_specs=[HBM] * 2 + [VMEM] * 5,
-        scratch_shapes=[
-            vmem(9, fx),
-            vmem(3, nx),
-            row_scratch(3 * nx),
-            vmem(15, nx - 4),
-            vmem(5, fx - 9),
-            sems(32),
-        ],
-        cost_estimate=pl.CostEstimate(flops=400_000_000, transcendentals=0, bytes_accessed=12_000_000),
+        out_specs=[VMEM] * 5,
+        scratch_shapes=[vmem(9, fx), vmem(3, nx), row_scratch(3 * nx), sems(32)],
+        cost_estimate=pl.CostEstimate(flops=200_000_000, transcendentals=0, bytes_accessed=6_000_000),
         compiler_params=params,
         name="local",
     )(*fields)
     late_halo = exchanged(up, down)
-    hydro, _, _, stage = pl.pallas_call(
+    rates, hydro = pl.pallas_call(
+        inner_kernel,
+        out_shape=(shape(15, nx), shape(1, 5, fx)),
+        in_specs=[VMEM] * 3,
+        out_specs=[HBM] * 2,
+        scratch_shapes=[vmem(15, nx - 4), vmem(5, fx - 9), sems(4)],
+        cost_estimate=pl.CostEstimate(flops=400_000_000, transcendentals=0, bytes_accessed=6_000_000),
+        compiler_params=params,
+        name="inner",
+    )(state, flux, sources)
+    hydro, state, _, stage = pl.pallas_call(
         halo_kernel,
         out_shape=(shape(1, 5, fx), shape(METRIC, nx + 4), shape(10, fx + 6), shape(15, 4)),
         in_specs=[VMEM] * 2 + [HBM] + [VMEM] * 3 + [HBM] * 5,
@@ -575,13 +577,13 @@
     rates = pl.pallas_call(
         late_kernel,
         out_shape=shape(15, nx),
-        in_specs=[VMEM] * 3 + [HBM] * 3,
+        in_specs=[VMEM] * 4 + [HBM],
         out_specs=HBM,
-        input_output_aliases={5: 0},
-        scratch_shapes=[vmem(15, 4), vmem(5), sems(8)],
+        input_output_aliases={4: 0},
+        scratch_shapes=[vmem(15, 4), sems(8)],
         compiler_params=params,
         name="late",
-    )(*late_halo, stage, lapse, shift, rates)
+    )(*late_halo, stage, state, rates)
     return rates, hydro
 
 

time: 31.6 us -> 30.4 us (0.962)
  the two profiles are of different devices: /device:TPU:1 before, /device:TPU:0 now
where the time goes in v5:
time: 30.4 us; the launch traced here: 30.2 us
  Pallas kernels  17.6 us (58%)
  starting transfers between devices  11.9 us (39%)
  between operations  0.7 us (2%)
    ppermute x2, starting transfers between devices, exchanged(): lax.ppermute(down, RING, [(j, i) for i, j in pairs])  11.8 us
    pallas_call x1, Pallas kernels, on_device(): pl.pallas_call(halo_kernel, out_shape=(shape(1, 5, fx), shape(METRIC, nx...  6.42 us
    pallas_call x1, Pallas kernels, on_device(): pl.pallas_call(inner_kernel, out_shape=(shape(15, nx), shape(1, 5, fx)),...  5.37 us
    pallas_call x1, Pallas kernels, on_device(): pl.pallas_call(local_kernel, out_shape=(shape(METRIC, nx + 4), shape(10,...  3 us
    pallas_call x1, Pallas kernels, on_device(): pl.pallas_call(pack_kernel, out_shape=(shape(early), shape(early + 3)), i...  1.68 us
    pallas_call x1, Pallas kernels, on_device(): pl.pallas_call(late_kernel, out_shape=shape(15, nx), in_specs=[VMEM] * 4...  1.12 us
  transfers between devices with their start and end apart: 4, of which 0 were waited for; matrix products, arithmetic and copies ran while one was open for 0% of the time, Pallas kernels for 49%

profile of v5, /device:TPU:0, one launch (start us, length us, event | category | flops | bytes accessed | tf_op | source)
XLA Modules:
  0.0 30.2 jit_solution(4416611749972115585)
XLA Ops:
  0.6 1.7 %pack.1 = (f32[31,16,256]{2,1,0:T(8,128)S(1)}, f32[34,16,256]{2,1,0:T(8,128)S(1)}) custom-call(f32[8,16,256]{2,1,0:T(8,128)} %lapse.3, f32[8,16,256]{2,1,0:T(8,128)} %conf.3, f32[3,8,16,256]{3,2,1,0:T(8,128)} %shift.3, f32[1,16,16,256]{3,2,1,0:T(8,128)} %dens.5, f32[1,3,16,16,256]{4,3,2,1,0:T(8,128)} %mom.5, f32[1,16,16,256]{3,2,1,0:T(8,128)} %ener.5, ...), custom_call_target="tpu_custom_call" | custom-call | tf_op jit(solution)/shard_map/pack/pallas_call | solution.py:529
  2.3 6.5 %collective-permute-start.3 = (f32[34,16,256]{2,1,0:T(8,128)S(1)}, f32[34,16,256]{2,1,0:T(8,128)S(1)}, u32[]{:S(2)}, u32[]{:S(2)}) collective-permute-start(f32[34,16,256]{2,1,0:T(8,128)S(1)} %get-tuple-element.17), channel_id=1, source_target_pairs={{1,0},{2,1},{3,2},{4,3},{5,4},{6,5},{7,6},{8,7},{9,8},{10,9},{11,1... | collective-permute-start | bytes 1671176 | tf_op jit(solution)/shard_map/ppermute | solution.py:524
  8.8 0.0 collective-permute-start.2
  8.8 3.0 %local.1 = (f32[18,12,16,256]{3,2,1,0:T(8,128)S(1)}, f32[10,22,16,256]{3,2,1,0:T(8,128)S(1)}, f32[8,16,256]{2,1,0:T(8,128)S(1)}, f32[27,16,256]{2,1,0:T(8,128)S(1)}, f32[26,16,256]{2,1,0:T(8,128)S(1)}) custom-call(f32[8,16,256]{2,1,0:T(8,128)} %lapse.3, f32[8,16,256]{2,1,0:T(8,128)} %conf.3, f32[8,16,256]{2,1,0:T(8,128)} %mean.1, f32[6,8,16,256]{3,2,1,0:T(8,128)} %metric.1, ...), custom_call_target="tpu_custom_call" | custom-call | flops 200000000 | bytes 6000000 | tf_op jit(solution)/shard_map/local/pallas_call | solution.py:539
  11.8 0.1 collective-permute-start
  11.8 5.4 %collective-permute-start.1 = (f32[26,16,256]{2,1,0:T(8,128)S(1)}, f32[26,16,256]{2,1,0:T(8,128)S(1)}, u32[]{:S(2)}, u32[]{:S(2)}) collective-permute-start(f32[26,16,256]{2,1,0:T(8,128)S(1)} %get-tuple-element.15), channel_id=1, source_target_pairs={{1,0},{2,1},{3,2},{4,3},{5,4},{6,5},{7,6},{8,7},{9,8},{10,9},{11,1... | collective-permute-start | bytes 1277960 | tf_op jit(solution)/shard_map/ppermute | solution.py:524
  17.2 5.4 %inner.1 = (f32[15,8,16,256]{3,2,1,0:T(8,128)}, f32[1,5,16,16,256]{4,3,2,1,0:T(8,128)}) custom-call(f32[18,12,16,256]{3,2,1,0:T(8,128)S(1)} %get-tuple-element.18.state.state_in, f32[10,22,16,256]{3,2,1,0:T(8,128)S(1)} %get-tuple-element.19.flux.flux_in, f32[8,16,256]{2,1,0:T(8,128)S(1)} %get-tuple-element.20.sources), custom_call_target="tpu_custom_call" | custom-call | flops 400000000 | bytes 6000000 | tf_op jit(solution)/shard_map/inner/pallas_call | solution.py:556
  22.6 0.0 collective-permute-done.2.below
  22.6 0.0 collective-permute-done.3.above
  22.6 6.4 %halo.1 = (f32[1,5,16,16,256]{4,3,2,1,0:T(8,128)}, f32[18,12,16,256]{3,2,1,0:T(8,128)S(1)}, f32[10,22,16,256]{3,2,1,0:T(8,128)S(1)}, f32[15,4,16,256]{3,2,1,0:T(8,128)S(1)}) custom-call(f32[31,16,256]{2,1,0:T(8,128)S(1)} %collective-permute-done.2.below, ...), custom_call_target="tpu_custom_call", output_to_operand_aliasing={{0}: (2, {}), {1}: (3, {}), {2}: (4, {})} | custom-call | flops 400000000 | bytes 12000000 | tf_op jit(solution)/shard_map/halo/pallas_call | solution.py:566
  29.1 0.0 collective-permute-done.1.above
  29.1 0.0 collective-permute-done.below
  29.1 1.1 %late.1 = f32[15,8,16,256]{3,2,1,0:T(8,128)} custom-call(f32[27,16,256]{2,1,0:T(8,128)S(1)} %collective-permute-done.below, f32[26,16,256]{2,1,0:T(8,128)S(1)} %collective-permute-done.1.above, f32[15,4,16,256]{3,2,1,0:T(8,128)S(1)} %get-tuple-element.22.stage_in, f32[18,12,16,256]{3,2,1,0:T(8,128)S(1)} %get-tuple-element.23.state, ...), custom_call_target="tpu_custom_call", output_to_operand_aliasing={{}: (4, {})} | custom-call | tf_op jit(solution)/shard_map/late/pallas_call | solution.py:577
Async XLA Ops:
  2.3 20.3 %collective-permute-start.3 = (f32[34,16,256]{2,1,0:T(8,128)S(1)}, f32[34,16,256]{2,1,0:T(8,128)S(1)}, u32[]{:S(2)}, u32[]{:S(2)}) collective-permute-start(f32[34,16,256]{2,1,0:T(8,128)S(1)} %get-tuple-element.17), channel_id=1, source_target_pairs={{1,0},{2,1},{3,2},{4,3},{5,4},{6,5},{7,6},{8,7},{9,8},{10,9},{11,1... | collective-permute-start | bytes 1671176 | tf_op jit(solution)/shard_map/ppermute | solution.py:524
  8.8 13.8 %collective-permute-start.2 = (f32[31,16,256]{2,1,0:T(8,128)S(1)}, f32[31,16,256]{2,1,0:T(8,128)S(1)}, u32[]{:S(2)}, u32[]{:S(2)}) collective-permute-start(f32[31,16,256]{2,1,0:T(8,128)S(1)} %get-tuple-element.16), channel_id=1, source_target_pairs={{0,1},{1,2},{2,3},{3,4},{4,5},{5,6},{6,7},{7,8},{8,9},{9,10},{10,1... | collective-permute-start | bytes 1523720 | tf_op jit(solution)/shard_map/ppermute | solution.py:524
  11.8 17.3 %collective-permute-start = (f32[27,16,256]{2,1,0:T(8,128)S(1)}, f32[27,16,256]{2,1,0:T(8,128)S(1)}, u32[]{:S(2)}, u32[]{:S(2)}) collective-permute-start(f32[27,16,256]{2,1,0:T(8,128)S(1)} %get-tuple-element.14), channel_id=1, source_target_pairs={{0,1},{1,2},{2,3},{3,4},{4,5},{5,6},{6,7},{7,8},{8,9},{9,10},{10,1... | collective-permute-start | bytes 1327112 | tf_op jit(solution)/shard_map/ppermute | solution.py:524
  11.8 17.2 %collective-permute-start.1 = (f32[26,16,256]{2,1,0:T(8,128)S(1)}, f32[26,16,256]{2,1,0:T(8,128)S(1)}, u32[]{:S(2)}, u32[]{:S(2)}) collective-permute-start(f32[26,16,256]{2,1,0:T(8,128)S(1)} %get-tuple-element.15), channel_id=1, source_target_pairs={{1,0},{2,1},{3,2},{4,3},{5,4},{6,5},{7,6},{8,7},{9,8},{10,9},{11,1... | collective-permute-start | bytes 1277960 | tf_op jit(solution)/shard_map/ppermute | solution.py:524

commit v6 on v5

--- a/solution.py
+++ b/solution.py
@@ -7,6 +7,7 @@
 from jax.experimental import pallas as pl
 from jax.experimental.pallas import tpu as pltpu
 from jax.sharding import PartitionSpec as P
+
 
 pair_index = ((0, 1, 2), (1, 3, 4), (2, 4, 5))
 sym_pairs = ((0, 0), (0, 1), (0, 2), (1, 1), (1, 2), (2, 2))
@@ -17,6 +18,7 @@
 EARLY = 5
 LATE = 13
 FLUID = 7
+EARLY_LAYERS = 2 * EARLY + 3 * FLUID + 3
 HBM = pl.BlockSpec(memory_space=pltpu.HBM)
 GRANT = 24 * 1024 * 1024
 VMEM = pl.BlockSpec(memory_space=pltpu.VMEM)
@@ -44,31 +46,44 @@
             self.wait(group)
 
 
-def pack_kernel(lapse, conf, shift, dens, mom, ener, velo, pres, up, down, sems):
-    nx = lapse.shape[0]
-    fx = dens.shape[1]
+def slow_side():
+    return lax.rem(lax.axis_index(RING[-1]), 2)
+
+
+def send_early(copies, group, side, lapse, conf, shift, dens, mom, ener, velo, pres, buf):
+    layer = lapse.shape[1:]
+    rows = pl.ds(side * (lapse.shape[0] - 2), 2)
+    copies.start(group, lapse.at[rows], buf.at[pl.ds(0, 2)])
+    copies.start(group, conf.at[rows], buf.at[pl.ds(2, 2)])
+    copies.start(group, shift.at[:, rows], buf.at[pl.ds(4, 6)].reshape(3, 2, *layer))
+    rows = pl.ds(side * (dens.shape[1] - 3), 3)
+    at = 2 * EARLY
+    copies.start(group, dens.at[0, rows], buf.at[pl.ds(at, 3)])
+    copies.start(group, mom.at[0, :, rows], buf.at[pl.ds(at + 3, 9)].reshape(3, 3, *layer))
+    copies.start(group, ener.at[0, rows], buf.at[pl.ds(at + 12, 3)])
+    copies.start(group, velo.at[0, 0, rows], buf.at[pl.ds(at + 15, 3)])
+    copies.start(group, pres.at[0, rows], buf.at[pl.ds(at + 18, 3)])
+    at = at + 3 * FLUID
+    copies.start(group, lapse.at[2], buf.at[at])
+    copies.start(group, conf.at[2], buf.at[at + 1])
+    copies.start(group, shift.at[0, 2], buf.at[at + 2])
+
+
+def send_late(copies, group, side, mean, metric, curv, buf, at):
+    layer = mean.shape[1:]
+    rows = pl.ds(side * (mean.shape[0] - 2), 2)
+    copies.start(group, mean.at[rows], buf.at[pl.ds(at, 2)])
+    copies.start(group, metric.at[:, rows], buf.at[pl.ds(at + 2, 12)].reshape(6, 2, *layer))
+    copies.start(group, curv.at[:, rows], buf.at[pl.ds(at + 14, 12)].reshape(6, 2, *layer))
+
+
+def pack_kernel(lapse, conf, shift, dens, mom, ener, velo, pres, buf, sems):
     copies = Copies(sems)
-    layer = lapse.shape[1:]
-    for buf, first, fluid_first in ((up, nx - 2, fx - 3), (down, 0, 0)):
-        rows = pl.ds(first, 2)
-        copies.start(0, lapse.at[rows], buf.at[pl.ds(0, 2)])
-        copies.start(0, conf.at[rows], buf.at[pl.ds(2, 2)])
-        copies.start(0, shift.at[:, rows], buf.at[pl.ds(4, 6)].reshape(3, 2, *layer))
-        rows = pl.ds(fluid_first, 3)
-        at = 2 * EARLY
-        copies.start(0, dens.at[0, rows], buf.at[pl.ds(at, 3)])
-        copies.start(0, mom.at[0, :, rows], buf.at[pl.ds(at + 3, 9)].reshape(3, 3, *layer))
-        copies.start(0, ener.at[0, rows], buf.at[pl.ds(at + 12, 3)])
-        copies.start(0, velo.at[0, 0, rows], buf.at[pl.ds(at + 15, 3)])
-        copies.start(0, pres.at[0, rows], buf.at[pl.ds(at + 18, 3)])
-    tail = 2 * EARLY + 3 * FLUID
-    copies.start(0, lapse.at[2], down.at[tail])
-    copies.start(0, shift.at[0, 2], down.at[tail + 1])
-    copies.start(0, conf.at[2], down.at[tail + 2])
+    send_early(copies, 0, slow_side(), lapse, conf, shift, dens, mom, ener, velo, pres, buf)
     copies.wait_all()
 
 
-def bssn_layer(state, sources, out, at, src_at, out_at):
+def bssn_layer(state, source, out, at, out_at):
     ny, nz = state.shape[-2:]
 
     def value(field, off=0):
@@ -153,7 +168,7 @@
     out[2, out_at] = (
         along_shift(2)
         - conf * trace
-        + lapse * (square + mean * mean * third + (4.0 * math.pi) * sources[src_at])
+        + lapse * (square + mean * mean * third + (4.0 * math.pi) * source)
     )
     lapse2 = 2.0 * lapse
     mean_lapse = lapse * mean
@@ -236,7 +251,7 @@
             at += 1
 
 
-def split_flux(fluid, lapse, shift, conf, out, out_at, scale=None):
+def split_flux(fluid, lapse, shift, conf, out, out_at):
     root = lax.rsqrt(conf)
     transport = lapse * fluid(5) - shift
     weight = lapse * (root * root * root) * fluid(6)
@@ -250,15 +265,13 @@
             flux = flux + weight * fluid(5)
         moved = speed * u
         plus, minus = flux + moved, flux - moved
-        if scale is not None:
-            plus, minus = plus * scale, minus * scale
         out[n, out_at] = plus
         out[5 + n, out_at] = minus
 
 
-def weno_cells(flux, field, rows, first, count, emit):
+def weno_cells(flux, field, rows, base, count, emit):
     def differences(which, low, high):
-        v = {j: flux[which, j, rows, :] for j in range(low, high + 1)}
+        v = {j: flux[which, base + j, rows, :] for j in range(low, high + 1)}
         e = {j: v[j + 1] - v[j] for j in range(low, high)}
         d = {j: e[j] - e[j - 1] for j in range(low + 1, high)}
         t = {j: d[j + 1] - d[j] for j in range(low + 1, high - 1)}
@@ -266,9 +279,9 @@
         s = {j: (13.0 / 12.0) * (d[j] * d[j]) + 4.0 * weno_eps for j in d}
         return v, e, d, t, h, s
 
-    faces = range(first - 1, first + count)
-    v, e, d, t, h, s = differences(field, first - 3, first + count + 1)
-    u, eu, du, tu, hu, su = differences(5 + field, first - 2, first + count + 2)
+    faces = range(-1, count)
+    v, e, _, t, h, s = differences(field, -3, count + 1)
+    u, eu, _, tu, hu, su = differences(5 + field, -2, count + 2)
 
     def quotient(b0, b1, b2, t0, t2):
         w0, w1, w2 = b1 * b2, b0 * b2, b0 * b1
@@ -306,9 +319,9 @@
 
 
 def local_kernel(
-    lapse, conf, mean, metric, curv, shift, dens, mom, ener, velo, pres,
-    state, flux, sources, up, down,
-    fluid, coarse, rows, sems,
+    packed, lapse, conf, mean, metric, curv, shift, dens, mom, ener, velo, pres,
+    state, flux, sources, fluid, fast, late,
+    coarse, rows, sems,
 ):
     nx, ny, nz = lapse.shape
     fx = dens.shape[1]
@@ -323,14 +336,13 @@
     copies.start("f", velo.at[0, 0], fluid.at[5])
     copies.start("f", pres.at[0], fluid.at[6])
     copies.start("f", velo.at[0, pl.ds(1, 2)], fluid.at[pl.ds(7, 2)])
-    copies.start("m", mean, state.at[2, inner])
-    copies.start("m", metric, state.at[pl.ds(3, 6), inner])
-    copies.start("m", curv, state.at[pl.ds(9, 6), inner])
-    for buf, first in ((up, nx - 2), (down, 0)):
-        for k in range(2):
-            copies.start("o", mean.at[first + k], buf.at[k * LATE])
-            copies.start("o", metric.at[:, first + k], buf.at[pl.ds(k * LATE + 1, 6)])
-            copies.start("o", curv.at[:, first + k], buf.at[pl.ds(k * LATE + 7, 6)])
+    side = slow_side()
+    send_late(copies, "o", side, mean, metric, curv, late, 0)
+    send_early(copies, "o", 1 - side, lapse, conf, shift, dens, mom, ener, velo, pres, fast)
+    send_late(copies, "o", 1 - side, mean, metric, curv, fast, EARLY_LAYERS)
+    copies.start("o", mean, state.at[2, inner])
+    copies.start("o", metric, state.at[pl.ds(3, 6), inner])
+    copies.start("o", curv, state.at[pl.ds(9, 6), inner])
 
     @pl.loop(2, 15)
     def _(n):
@@ -363,18 +375,19 @@
 
         return lambda: one(2 * layer) + one(2 * layer + 1)
 
+    plane = EARLY_LAYERS + 2 * LATE
     restrict_planes(
         [pair(l) for l in range(nx)],
         rows,
-        [(sources, l + 1) for l in range(nx - 1)] + [(up, 2 * LATE)],
-    )
+        [(sources, l + 1) for l in range(nx - 1)] + [(late, 2 * LATE)],
+    )
+    fast[plane] = late[2 * LATE]
     sources[0] = jnp.zeros((ny, nz), F32)
-
     copies.wait_all()
 
 
 def inner_kernel(state, flux, sources, rates, hydro, stage, hstage, sems):
-    nx, ny, nz = sources.shape
+    nx, ny, _ = sources.shape
     fx = hydro.shape[2]
     copies = Copies(sems)
 
@@ -384,123 +397,131 @@
             sl = pl.ds(part * 8, 8)
 
             def emit(i, value):
-                hstage[n, i - 6, sl, :] = value
-
-            weno_cells(flux, n, sl, 6, fx - 9, emit)
-
-    copies.start("o", hstage, hydro.at[0, :, pl.ds(3, fx - 9)])
+                hstage[n, i, sl, :] = value
+
+            weno_cells(flux, n, sl, 9, fx - 12, emit)
+
+    copies.start("o", hstage, hydro.at[0, :, pl.ds(6, fx - 12)])
+
     @pl.loop(0, nx - 4)
     def _(l):
-        bssn_layer(state, sources, stage, l + 4, l + 2, l)
+        bssn_layer(state, sources[l + 2], stage, l + 4, l)
 
     copies.start("o", stage, rates.at[:, pl.ds(2, nx - 4)])
     copies.wait_all()
 
 
-def halo_kernel(
-    below, above, hydro_in, state_in, flux_in, sources, dens, mom, ener, velo, pres,
-    hydro, state, flux, stage,
-    own, coarse, rows, hstage, sems,
-):
+def side_work(copies, side, recv, complete, state, flux, sources, fluid, hydro, stage, six, coarse, rows, hstage):
     nx = sources.shape[0]
-    ny, nz = sources.shape[-2:]
-    fx = dens.shape[1]
-    copies = Copies(sems)
-    last = pl.ds(fx - 3, 3)
-    copies.start("f", dens.at[0, last], own.at[0])
-    copies.start("f", mom.at[0, :, last], own.at[pl.ds(1, 3)])
-    copies.start("f", ener.at[0, last], own.at[4])
-    copies.start("f", velo.at[0, 0, last], own.at[5])
-    copies.start("f", pres.at[0, last], own.at[6])
-    place = lax.axis_index("blk")
-    inside = (
-        jnp.where(place > 0, 1.0, 0.0).astype(F32),
-        jnp.where(place < lax.axis_size("blk") - 1, 1.0, 0.0).astype(F32),
-    )
+    ny, _ = sources.shape[-2:]
+    fx = fluid.shape[1]
+    halo = side * (nx + 2)
     for k in range(2):
         for n, field in enumerate((0, 1, 15, 16, 17)):
-            state[field, k] = below[2 * n + k]
-            state[field, nx + 2 + k] = above[2 * n + k]
+            state[field, halo + k] = recv[2 * n + k]
+    for n, field in enumerate((0, 1, 15)):
+        state[field, nx + 4] = recv[2 * EARLY + 3 * FLUID + n]
+    if complete:
+
+        @pl.loop(0, LATE)
+        def _(n):
+            for k in range(2):
+                state[2 + n, halo + k] = recv[EARLY_LAYERS + 2 * n + k]
+
+    place = lax.axis_index(RING[-1])
+    outer = jnp.where(side == 0, place == 0, place == lax.axis_size(RING[-1]) - 1)
+    inside = jnp.where(outer, 0.0, 1.0).astype(F32)
+    for n in range(FLUID):
+        for k in range(3):
+            value = recv[2 * EARLY + 3 * n + k]
+            six[n, 3 * side + k] = value if n == 5 else value * inside
+            six[n, 3 - 3 * side + k] = fluid[n, side * (fx - 3) + k]
 
     def coarse_plane(field, layer):
-        if layer == nx + 2:
-            return lambda sl: above[2 * EARLY + 3 * FLUID + (0, 15, 1).index(field), sl, :]
-        return lambda sl: state[field, layer + 2, sl, :]
-
-    layers = (-1, 0, 1, nx - 1, nx, nx + 1, nx + 2)
-    prolong_yz([[coarse_plane(f, l) for l in layers] for f in (0, 15, 1)], rows, coarse)
-    copies.wait("f")
-
-    for i in (-3, -2, -1) + tuple(range(fx - 3, fx + 3)):
-        mid = i // 2 + 1
-        side = mid - 1 + 2 * (i % 2)
-        mid, side = layers.index(mid), layers.index(side)
-        parts = [0.75 * coarse[n, mid] + 0.25 * coarse[n, side] for n in range(3)]
-        if i < 0:
-            fluid = lambda n, at=2 * EARLY + i + 3: below[at + 3 * n]
-            scale = inside[0]
-        elif i < fx:
-            fluid = lambda n, at=i - fx + 3: own[n, at]
-            scale = None
-        else:
-            fluid = lambda n, at=2 * EARLY + i - fx: above[at + 3 * n]
-            scale = inside[1]
-        split_flux(fluid, *parts, flux, i + 3, scale)
+        return lambda sl: state[field, side * nx + 1 + layer, sl, :]
+
+    prolong_yz([[coarse_plane(f, l) for l in range(4)] for f in (0, 15, 1)], rows, coarse)
+
+    @pl.loop(0, 6)
+    def _(j):
+        mid = lax.shift_right_logical(j + 1, 1)
+        other = mid + 1 - 2 * (j & 1)
+        parts = [0.75 * coarse[n, mid] + 0.25 * coarse[n, other] for n in range(3)]
+        split_flux(lambda n: six[n, j], *parts, flux, side * fx + j)
+
+    first = side * (fx - 6)
 
     @pl.loop(0, 5)
     def _(n):
         for part in range(ny // 8):
             sl = pl.ds(part * 8, 8)
 
-            def emit_low(i, value):
-                hstage[n, i - 3, sl, :] = value
-
-            def emit_high(i, value):
-                hstage[n, 3 + i - (fx - 3), sl, :] = value
-
-            weno_cells(flux, n, sl, 3, 3, emit_low)
-            weno_cells(flux, n, sl, fx - 3, 6, emit_high)
-
-    copies.start("o", hstage.at[:, pl.ds(0, 3)], hydro.at[0, :, pl.ds(0, 3)])
-    copies.start("o", hstage.at[:, pl.ds(3, 6)], hydro.at[0, :, pl.ds(fx - 6, 6)])
-
-    @pl.loop(0, 4)
+            def emit(i, value):
+                hstage[n, i, sl, :] = value
+
+            weno_cells(flux, n, sl, first + 3, 6, emit)
+
+    copies.start("o", hstage, hydro.at[0, :, pl.ds(first, 6)])
+
+    @pl.loop(0, 2)
     def _(k):
-        l = jnp.where(k < 2, k, k + nx - 4)
-        bssn_layer(state, sources, stage, l + 2, l, k)
-
+        l = side * (nx - 2) + k
+        source = sources[l]
+        if complete:
+            source = source + jnp.where(l == 0, 1.0, 0.0).astype(F32) * recv[EARLY_LAYERS + 2 * LATE]
+        bssn_layer(state, source, stage, l + 2, k)
+
+
+def fast_kernel(
+    recv, rates_in, hydro_in, state_in, flux_in, sources, fluid,
+    rates, hydro, state, flux,
+    stage, six, coarse, rows, hstage, sems,
+):
+    copies = Copies(sems)
+    side = 1 - slow_side()
+    side_work(copies, side, recv, True, state, flux, sources, fluid, hydro, stage, six, coarse, rows, hstage)
+    copies.start("o", stage, rates.at[:, pl.ds(side * (rates.shape[1] - 2), 2)])
     copies.wait_all()
 
 
-def late_kernel(below, above, stage_in, state, rates_in, rates, stage, sems):
+def slow_kernel(
+    recv, hydro_in, state_in, flux_in, sources, fluid,
+    hydro, state, flux, stage,
+    six, coarse, rows, hstage, sems,
+):
+    copies = Copies(sems)
+    side_work(copies, slow_side(), recv, False, state, flux, sources, fluid, hydro, stage, six, coarse, rows, hstage)
+    copies.wait_all()
+
+
+def late_kernel(recv, stage_in, state, rates_in, rates, stage, sems):
     nx = rates.shape[1]
     copies = Copies(sems)
-    steps = [state[15, at] * (1.0 / 12.0) for at in (2, 3, nx, nx + 1)]
-    for field in range(15):
-        late = field - 2
-        for k in range(4):
+    side = slow_side()
+    low = side == 0
+
+    def pick(below, above):
+        return jnp.where(low, below, above).astype(F32)
+
+    taps = ((pick(1.0, -1.0), pick(-8.0, 0.0)), (pick(0.0, 8.0), pick(1.0, -1.0)))
+    first = side * (nx - 2)
+    for k in range(2):
+        step = state[15, first + 2 + k] * (1.0 / 12.0)
+        for field in range(15):
             value = stage_in[field, k]
-            if late >= 0:
-                if k == 0:
-                    tap = below[late] - 8.0 * below[LATE + late]
-                elif k == 1:
-                    tap = below[LATE + late]
-                elif k == 2:
-                    tap = -above[late]
-                else:
-                    tap = 8.0 * above[late] - above[LATE + late]
-                value = value + steps[k] * tap
+            if field >= 2:
+                at = 2 * (field - 2)
+                value = value + step * (taps[k][0] * recv[at] + taps[k][1] * recv[at + 1])
             if field == 2 and k == 0:
-                value = value + (4.0 * math.pi) * state[0, 2] * below[2 * LATE]
+                value = value + pick(4.0 * math.pi, 0.0) * state[0, 2] * recv[2 * LATE]
             stage[field, k] = value
-    copies.start("o", stage.at[:, pl.ds(0, 2)], rates.at[:, pl.ds(0, 2)])
-    copies.start("o", stage.at[:, pl.ds(2, 2)], rates.at[:, pl.ds(nx - 2, 2)])
+    copies.start("o", stage, rates.at[:, pl.ds(first, 2)])
     copies.wait_all()
 
 
-def on_device(*fields):
+def substep(*fields):
     fields = [pltpu.with_memory_space_constraint(field, pltpu.HBM) for field in fields]
-    lapse, conf, mean, metric, curv, shift, dens, mom, ener, velo, pres = fields
+    lapse, conf, _, _, _, shift, dens, mom, ener, velo, pres = fields
     nx, ny, nz = lapse.shape
     fx = dens.shape[1]
     layer = (ny, nz)
@@ -518,72 +539,87 @@
         return pltpu.SemaphoreType.DMA((n,))
 
     count = lax.axis_size(RING)
-    pairs = [(i, (i + 1) % count) for i in range(count)]
-
-    def exchanged(up, down):
-        return lax.ppermute(up, RING, pairs), lax.ppermute(down, RING, [(j, i) for i, j in pairs])
-
+    fast_pairs = [(i, i ^ 1) for i in range(count)]
+    slow_pairs = [(i, (i + (1 if i % 2 else -1)) % count) for i in range(count)]
     params = pltpu.CompilerParams(vmem_limit_bytes=GRANT)
-    early = 2 * EARLY + 3 * FLUID
-    early_halo = exchanged(
-        *pl.pallas_call(
-            pack_kernel,
-            out_shape=(shape(early), shape(early + 3)),
-            in_specs=[HBM] * 8,
-            out_specs=[VMEM] * 2,
-            scratch_shapes=[sems(48)],
-            compiler_params=params,
-            name="pack",
-        )(lapse, conf, shift, dens, mom, ener, velo, pres)
-    )
-    state, flux, sources, up, down = pl.pallas_call(
+
+    def cost(flops):
+        return pl.CostEstimate(flops=flops, transcendentals=0, bytes_accessed=6_000_000)
+
+    early = pl.pallas_call(
+        pack_kernel,
+        out_shape=shape(EARLY_LAYERS),
+        in_specs=[HBM] * 8,
+        out_specs=VMEM,
+        scratch_shapes=[sems(16)],
+        compiler_params=params,
+        name="pack",
+    )(lapse, conf, shift, dens, mom, ener, velo, pres)
+    packed = early
+    early = lax.ppermute(early, RING, slow_pairs)
+    local = pl.pallas_call(
         local_kernel,
         out_shape=(
-            shape(METRIC, nx + 4),
+            shape(METRIC, nx + 5),
             shape(10, fx + 6),
             shape(nx),
+            shape(9, fx),
+            shape(EARLY_LAYERS + 2 * LATE + 1),
             shape(2 * LATE + 1),
-            shape(2 * LATE),
         ),
-        in_specs=[HBM] * 11,
-        out_specs=[VMEM] * 5,
-        scratch_shapes=[vmem(9, fx), vmem(3, nx), row_scratch(3 * nx), sems(32)],
-        cost_estimate=pl.CostEstimate(flops=200_000_000, transcendentals=0, bytes_accessed=6_000_000),
+        in_specs=[VMEM] + [HBM] * 11,
+        out_specs=[VMEM] * 6,
+        scratch_shapes=[vmem(3, nx), row_scratch(3 * nx), sems(40)],
+        cost_estimate=cost(200_000_000),
         compiler_params=params,
         name="local",
-    )(*fields)
-    late_halo = exchanged(up, down)
+    )
+    state, flux, sources, fluid, fast, late = local(packed, *fields)
+    fast = lax.ppermute(fast, RING, fast_pairs)
+    late = lax.ppermute(late, RING, slow_pairs)
     rates, hydro = pl.pallas_call(
         inner_kernel,
         out_shape=(shape(15, nx), shape(1, 5, fx)),
         in_specs=[VMEM] * 3,
         out_specs=[HBM] * 2,
-        scratch_shapes=[vmem(15, nx - 4), vmem(5, fx - 9), sems(4)],
-        cost_estimate=pl.CostEstimate(flops=400_000_000, transcendentals=0, bytes_accessed=6_000_000),
+        scratch_shapes=[vmem(15, nx - 4), vmem(5, fx - 12), sems(4)],
+        cost_estimate=cost(400_000_000),
         compiler_params=params,
         name="inner",
     )(state, flux, sources)
+    work = [vmem(FLUID, 6), vmem(3, 4), row_scratch(12), vmem(5, 6), sems(4)]
+    rates, hydro, state, flux = pl.pallas_call(
+        fast_kernel,
+        out_shape=(shape(15, nx), shape(1, 5, fx), shape(METRIC, nx + 5), shape(10, fx + 6)),
+        in_specs=[VMEM] + [HBM] * 2 + [VMEM] * 4,
+        out_specs=[HBM] * 2 + [VMEM] * 2,
+        input_output_aliases={1: 0, 2: 1, 3: 2, 4: 3},
+        scratch_shapes=[vmem(15, 2)] + work,
+        cost_estimate=cost(300_000_000),
+        compiler_params=params,
+        name="fast",
+    )(fast, rates, hydro, state, flux, sources, fluid)
     hydro, state, _, stage = pl.pallas_call(
-        halo_kernel,
-        out_shape=(shape(1, 5, fx), shape(METRIC, nx + 4), shape(10, fx + 6), shape(15, 4)),
-        in_specs=[VMEM] * 2 + [HBM] + [VMEM] * 3 + [HBM] * 5,
+        slow_kernel,
+        out_shape=(shape(1, 5, fx), shape(METRIC, nx + 5), shape(10, fx + 6), shape(15, 2)),
+        in_specs=[VMEM, HBM] + [VMEM] * 4,
         out_specs=[HBM] + [VMEM] * 3,
-        input_output_aliases={2: 0, 3: 1, 4: 2},
-        scratch_shapes=[vmem(FLUID, 3), vmem(3, 7), row_scratch(21), vmem(5, 9), sems(16)],
-        cost_estimate=pl.CostEstimate(flops=400_000_000, transcendentals=0, bytes_accessed=12_000_000),
+        input_output_aliases={1: 0, 2: 1, 3: 2},
+        scratch_shapes=work,
+        cost_estimate=cost(300_000_000),
         compiler_params=params,
-        name="halo",
-    )(*early_halo, hydro, state, flux, sources, dens, mom, ener, velo, pres)
+        name="slow",
+    )(early, hydro, state, flux, sources, fluid)
     rates = pl.pallas_call(
         late_kernel,
         out_shape=shape(15, nx),
-        in_specs=[VMEM] * 4 + [HBM],
+        in_specs=[VMEM] * 3 + [HBM],
         out_specs=HBM,
-        input_output_aliases={4: 0},
-        scratch_shapes=[vmem(15, 4), sems(8)],
+        input_output_aliases={3: 0},
+        scratch_shapes=[vmem(15, 2), sems(4)],
         compiler_params=params,
         name="late",
-    )(*late_halo, stage, state, rates)
+    )(late, stage, state, rates)
     return rates, hydro
 
 
@@ -602,6 +638,4 @@
         P("star", "blk", None, None),
     )
     out_specs = (P(None, RING, None, None), P("star", None, "blk", None, None))
-    return jax.shard_map(
-        on_device, mesh=mesh, in_specs=in_specs, out_specs=out_specs, check_vma=False
-    )
+    return jax.shard_map(substep, mesh=mesh, in_specs=in_specs, out_specs=out_specs, check_vma=False)

time: 30.4 us -> 31.6 us (1.039)
  the two profiles are of different devices: /device:TPU:0 before, /device:TPU:1 now
where the time goes in v6:
time: 31.6 us; the launch traced here: 31.3 us
  Pallas kernels  18.3 us (58%)
  waiting for transfers between devices  9.68 us (31%)
  starting transfers between devices  2.68 us (8%)
  between operations  0.69 us (2%)
    ppermute x1, waiting for transfers between devices, substep(): early = lax.ppermute(early, RING, slow_pairs)  8.58 us
    pallas_call x1, Pallas kernels, substep(): pl.pallas_call(inner_kernel, out_shape=(shape(15, nx), shape(1, 5, fx)),...  4.74 us
    pallas_call x1, Pallas kernels, substep(): pl.pallas_call(fast_kernel, out_shape=(shape(15, nx), shape(1, 5, fx), sh...  4.5 us
    pallas_call x1, Pallas kernels, substep(): pl.pallas_call(slow_kernel, out_shape=(shape(1, 5, fx), shape(METRIC, nx...  3.64 us
    pallas_call x1, Pallas kernels, substep(): state, flux, sources, fluid, fast, late = local(packed, *fields)  3.33 us
    ppermute x1, starting transfers between devices, substep(): early = lax.ppermute(early, RING, slow_pairs)  2.53 us
    pallas_call x1, Pallas kernels, substep(): pl.pallas_call(pack_kernel, out_shape=shape(EARLY_LAYERS), in_specs=[HBM]...  1.19 us
    ppermute x1, waiting for transfers between devices, substep(): late = lax.ppermute(late, RING, slow_pairs)  1.09 us
  transfers between devices with their start and end apart: 3, of which 2 were waited for; matrix products, arithmetic and copies ran while one was open for 0% of the time, Pallas kernels for 41%

profile of v6, /device:TPU:1, one launch (start us, length us, event | category | flops | bytes accessed | tf_op | source)
XLA Modules:
  0.0 31.3 jit_solution(7070489188165418026)
XLA Ops:
  0.6 1.2 %pack.1.packed = f32[34,16,256]{2,1,0:T(8,128)S(1)} custom-call(f32[8,16,256]{2,1,0:T(8,128)} %lapse.3, f32[8,16,256]{2,1,0:T(8,128)} %conf.3, f32[3,8,16,256]{3,2,1,0:T(8,128)} %shift.3, f32[1,16,16,256]{3,2,1,0:T(8,128)} %dens.3, f32[1,3,16,16,256]{4,3,2,1,0:T(8,128)} %mom.3, f32[1,16,16,256]{3,2,1,0:T(8,128)} %ener.3, f32[1,3,16,16,256]{4,3,2,1,0:T(8,128)} %velo.3, ...), custom_call_target="tpu_custom_call" | custom-call | tf_op jit(solution)/shard_map/pack/pallas_call | solution.py:549
  1.8 3.3 %local.1 = (f32[18,13,16,256]{3,2,1,0:T(8,128)S(1)}, f32[10,22,16,256]{3,2,1,0:T(8,128)S(1)}, f32[8,16,256]{2,1,0:T(8,128)S(1)}, f32[9,16,16,256]{3,2,1,0:T(8,12...) custom-call(f32[34,16,256]{2,1,0:T(8,128)S(1)} %pack.1.packed, f32[8,16,256]{2,1,0:T(8,128)} %lapse.3, ...), custom_call_target="tpu_custom_call" | custom-call | flops 200000000 | bytes 6000000 | tf_op jit(solution)/shard_map/local/pallas_call | solution.py:577
  5.2 0.1 collective-permute-start.2
  5.2 2.5 %collective-permute-start.1 = (f32[34,16,256]{2,1,0:T(8,128)S(1)}, f32[34,16,256]{2,1,0:T(8,128)S(1)}, u32[]{:S(2)}, u32[]{:S(2)}) collective-permute-start(f32[34,16,256]{2,1,0:T(8,128)S(1)} %pack.1.packed), channel_id=1, source_target_pairs={{0,31},{1,2},{2,1},{3,4},{4,3},{5,6},{6,5},{7,8},{8,7},{9,10},{10,... | collective-permute-start | bytes 1671176 | tf_op jit(solution)/shard_map/ppermute | solution.py:559
  7.8 0.1 collective-permute-start
  7.8 4.7 %inner.1 = (f32[15,8,16,256]{3,2,1,0:T(8,128)}, f32[1,5,16,16,256]{4,3,2,1,0:T(8,128)}) custom-call(f32[18,13,16,256]{3,2,1,0:T(8,128)S(1)} %get-tuple-element.19.state.state_in, f32[10,22,16,256]{3,2,1,0:T(8,128)S(1)} %get-tuple-element.20.flux.flux_in, f32[8,16,256]{2,1,0:T(8,128)S(1)} %get-tuple-element.21.sources), custom_call_target="tpu_custom_call" | custom-call | flops 400000000 | bytes 6000000 | tf_op jit(solution)/shard_map/inner/pallas_call | solution.py:580
  12.6 0.0 collective-permute-done.2.recv
  12.6 4.5 %fast.1 = (f32[15,8,16,256]{3,2,1,0:T(8,128)}, f32[1,5,16,16,256]{4,3,2,1,0:T(8,128)}, f32[18,13,16,256]{3,2,1,0:T(8,128)S(1)}, f32[10,22,16,256]{3,2,1,0:T(8,128)S(1)}) custom-call(f32[61,16,256]{2,1,0:T(8,128)S(1)} %collective-permute-done.2.recv, ...), custom_call_target="tpu_custom_call", output_to_operand_aliasing={{0}: (1, {}), {1}: (2, {}), {2}: (3, {}), {3}: (4, {})} | custom-call | flops 300000000 | bytes 6000000 | tf_op jit(solution)/shard_map/fast/pallas_call | solution.py:591
  17.1 8.6 %collective-permute-done.1.recv = f32[34,16,256]{2,1,0:T(8,128)S(1)} collective-permute-done((f32[34,16,256]{2,1,0:T(8,128)S(1)}, f32[34,16,256]{2,1,0:T(8,128)S(1)}, u32[]{:S(2)}, u32[]{:S(2)}) %collective-permute-start.1) | collective-permute-done | bytes 557088 | tf_op jit(solution)/shard_map/ppermute | solution.py:559
  25.7 3.6 %slow.1 = (f32[1,5,16,16,256]{4,3,2,1,0:T(8,128)}, f32[18,13,16,256]{3,2,1,0:T(8,128)S(1)}, f32[10,22,16,256]{3,2,1,0:T(8,128)S(1)}, f32[15,2,16,256]{3,2,1,0:T(8,128)S(1)}) custom-call(f32[34,16,256]{2,1,0:T(8,128)S(1)} %collective-permute-done.1.recv, ...), custom_call_target="tpu_custom_call", output_to_operand_aliasing={{0}: (1, {}), {1}: (2, {}), {2}: (3, {})} | custom-call | flops 300000000 | bytes 6000000 | tf_op jit(solution)/shard_map/slow/pallas_call | solution.py:602
  29.3 1.1 %collective-permute-done.recv = f32[27,16,256]{2,1,0:T(8,128)S(1)} collective-permute-done((f32[27,16,256]{2,1,0:T(8,128)S(1)}, f32[27,16,256]{2,1,0:T(8,128)S(1)}, u32[]{:S(2)}, u32[]{:S(2)}) %collective-permute-start) | collective-permute-done | bytes 442400 | tf_op jit(solution)/shard_map/ppermute | solution.py:579
  30.4 0.9 %late.1 = f32[15,8,16,256]{3,2,1,0:T(8,128)} custom-call(f32[27,16,256]{2,1,0:T(8,128)S(1)} %collective-permute-done.recv, f32[15,2,16,256]{3,2,1,0:T(8,128)S(1)} %get-tuple-element.28.stage_in, f32[18,13,16,256]{3,2,1,0:T(8,128)S(1)} %get-tuple-element.29.state, f32[15,8,16,256]{3,2,1,0:T(8,128)} %get-tuple-element.30.rates_in), custom_call_target="tpu_custom_call", output_to_operand_aliasing={{}: (3, {})} | custom-call | tf_op jit(solution)/shard_map/late/pallas_call | solution.py:613
Async XLA Ops:
  5.2 7.4 %collective-permute-start.2 = (f32[61,16,256]{2,1,0:T(8,128)S(1)}, f32[61,16,256]{2,1,0:T(8,128)S(1)}, u32[]{:S(2)}, u32[]{:S(2)}) collective-permute-start(f32[61,16,256]{2,1,0:T(8,128)S(1)} %get-tuple-element.18), channel_id=1, source_target_pairs={{0,1},{1,0},{2,3},{3,2},{4,5},{5,4},{6,7},{7,6},{8,9},{9,8},{10,11... | collective-permute-start | bytes 2998280 | tf_op jit(solution)/shard_map/ppermute | solution.py:578
  5.2 20.5 %collective-permute-start.1 = (f32[34,16,256]{2,1,0:T(8,128)S(1)}, f32[34,16,256]{2,1,0:T(8,128)S(1)}, u32[]{:S(2)}, u32[]{:S(2)}) collective-permute-start(f32[34,16,256]{2,1,0:T(8,128)S(1)} %pack.1.packed), channel_id=1, source_target_pairs={{0,31},{1,2},{2,1},{3,4},{4,3},{5,6},{6,5},{7,8},{8,7},{9,10},{10,... | collective-permute-start | bytes 1671176 | tf_op jit(solution)/shard_map/ppermute | solution.py:559
  7.8 22.7 %collective-permute-start = (f32[27,16,256]{2,1,0:T(8,128)S(1)}, f32[27,16,256]{2,1,0:T(8,128)S(1)}, u32[]{:S(2)}, u32[]{:S(2)}) collective-permute-start(f32[27,16,256]{2,1,0:T(8,128)S(1)} %get-tuple-element.17), channel_id=1, source_target_pairs={{0,31},{1,2},{2,1},{3,4},{4,3},{5,6},{6,5},{7,8},{8,7},{9,10},{10,... | collective-permute-start | bytes 1327112 | tf_op jit(solution)/shard_map/ppermute | solution.py:579

commit v7 on v6

--- a/solution.py
+++ b/solution.py
@@ -17,8 +17,10 @@
 METRIC = 18
 EARLY = 5
 LATE = 13
+PLANE = 2 * LATE - 2
 FLUID = 7
-EARLY_LAYERS = 2 * EARLY + 3 * FLUID + 3
+EARLY_LAYERS = 2 * EARLY + 3 * FLUID + 2
+SPARE = EARLY_LAYERS - 2
 HBM = pl.BlockSpec(memory_space=pltpu.HBM)
 GRANT = 24 * 1024 * 1024
 VMEM = pl.BlockSpec(memory_space=pltpu.VMEM)
@@ -48,6 +50,19 @@
 
 def slow_side():
     return lax.rem(lax.axis_index(RING[-1]), 2)
+
+
+def coarse_rows(ny):
+    first, count = ny // 4 - 1, ny // 2 + 2
+    parts = []
+    for n in range(3):
+        done = 0
+        while done < count:
+            at = n * count + done
+            step = min(count - done, ny - at % ny)
+            parts.append((n, first + done, step, at // ny, at % ny))
+            done += step
+    return parts
 
 
 def send_early(copies, group, side, lapse, conf, shift, dens, mom, ener, velo, pres, buf):
@@ -63,23 +78,39 @@
     copies.start(group, ener.at[0, rows], buf.at[pl.ds(at + 12, 3)])
     copies.start(group, velo.at[0, 0, rows], buf.at[pl.ds(at + 15, 3)])
     copies.start(group, pres.at[0, rows], buf.at[pl.ds(at + 18, 3)])
-    at = at + 3 * FLUID
-    copies.start(group, lapse.at[2], buf.at[at])
-    copies.start(group, conf.at[2], buf.at[at + 1])
-    copies.start(group, shift.at[0, 2], buf.at[at + 2])
 
 
 def send_late(copies, group, side, mean, metric, curv, buf, at):
     layer = mean.shape[1:]
     rows = pl.ds(side * (mean.shape[0] - 2), 2)
-    copies.start(group, mean.at[rows], buf.at[pl.ds(at, 2)])
-    copies.start(group, metric.at[:, rows], buf.at[pl.ds(at + 2, 12)].reshape(6, 2, *layer))
-    copies.start(group, curv.at[:, rows], buf.at[pl.ds(at + 14, 12)].reshape(6, 2, *layer))
-
-
-def pack_kernel(lapse, conf, shift, dens, mom, ener, velo, pres, buf, sems):
+    copies.start(group, metric.at[:, rows], buf.at[pl.ds(at, 12)].reshape(6, 2, *layer))
+    copies.start(group, curv.at[:, rows], buf.at[pl.ds(at + 12, 12)].reshape(6, 2, *layer))
+    copies.start(group, mean.at[rows], buf.at[pl.ds(at + 24, 2)])
+
+
+def fill_spare(up, third, mean, buf):
+    @pl.when(up)
+    def _():
+        for k in range(2):
+            buf[SPARE + k] = mean(k)
+
+    @pl.when(jnp.logical_not(up))
+    def _():
+        for n, row, count, layer, at in coarse_rows(buf.shape[1]):
+            buf[SPARE + layer, pl.ds(at, count), :] = third(n, pl.ds(row, count))
+
+
+def pack_kernel(lapse, conf, shift, mean, dens, mom, ener, velo, pres, buf, third, high, sems):
     copies = Copies(sems)
-    send_early(copies, 0, slow_side(), lapse, conf, shift, dens, mom, ener, velo, pres, buf)
+    side = slow_side()
+    copies.start("s", lapse.at[2], third.at[0])
+    copies.start("s", conf.at[2], third.at[1])
+    copies.start("s", shift.at[0, 2], third.at[2])
+    copies.start("s", mean.at[pl.ds(mean.shape[0] - 2, 2)], high)
+    send_early(copies, 0, side, lapse, conf, shift, dens, mom, ener, velo, pres, buf)
+    buf[EARLY_LAYERS - 1] = jnp.zeros(buf.shape[1:], F32)
+    copies.wait("s")
+    fill_spare(side == 1, lambda n, sl: third[n, sl, :], lambda k: high[k], buf)
     copies.wait_all()
 
 
@@ -379,11 +410,18 @@
     restrict_planes(
         [pair(l) for l in range(nx)],
         rows,
-        [(sources, l + 1) for l in range(nx - 1)] + [(late, 2 * LATE)],
-    )
-    fast[plane] = late[2 * LATE]
+        [(sources, l + 1) for l in range(nx - 1)] + [(fast, plane)],
+    )
     sources[0] = jnp.zeros((ny, nz), F32)
+    for k in range(2):
+        fast[SPARE + k] = jnp.zeros((ny, nz), F32)
+    for n, row, count, layer, at in coarse_rows(ny):
+        fast[SPARE + layer, pl.ds(at, count), :] = state[(0, 1, 15)[n], 4, pl.ds(row, count), :]
     copies.wait_all()
+
+    @pl.when(slow_side() == 1)
+    def _():
+        late[PLANE] = fast[plane]
 
 
 def inner_kernel(state, flux, sources, rates, hydro, stage, hstage, sems):
@@ -419,14 +457,15 @@
     for k in range(2):
         for n, field in enumerate((0, 1, 15, 16, 17)):
             state[field, halo + k] = recv[2 * n + k]
-    for n, field in enumerate((0, 1, 15)):
-        state[field, nx + 4] = recv[2 * EARLY + 3 * FLUID + n]
+    for n, row, count, layer, at in coarse_rows(ny):
+        state[(0, 1, 15)[n], nx + 4, pl.ds(row, count), :] = recv[SPARE + layer, pl.ds(at, count), :]
     if complete:
 
         @pl.loop(0, LATE)
         def _(n):
             for k in range(2):
-                state[2 + n, halo + k] = recv[EARLY_LAYERS + 2 * n + k]
+                field = jnp.where(n == LATE - 1, 2, n + 3)
+                state[field, halo + k] = recv[EARLY_LAYERS + 2 * n + k]
 
     place = lax.axis_index(RING[-1])
     outer = jnp.where(side == 0, place == 0, place == lax.axis_size(RING[-1]) - 1)
@@ -494,7 +533,7 @@
     copies.wait_all()
 
 
-def late_kernel(recv, stage_in, state, rates_in, rates, stage, sems):
+def late_kernel(recv, early, stage_in, state, rates_in, rates, stage, sems):
     nx = rates.shape[1]
     copies = Copies(sems)
     side = slow_side()
@@ -509,11 +548,14 @@
         step = state[15, first + 2 + k] * (1.0 / 12.0)
         for field in range(15):
             value = stage_in[field, k]
+            if field == 2:
+                values = [jnp.where(low, early[SPARE + n], recv[PLANE + n]) for n in range(2)]
+            elif field > 2:
+                values = [recv[2 * (field - 3) + n] for n in range(2)]
             if field >= 2:
-                at = 2 * (field - 2)
-                value = value + step * (taps[k][0] * recv[at] + taps[k][1] * recv[at + 1])
+                value = value + step * (taps[k][0] * values[0] + taps[k][1] * values[1])
             if field == 2 and k == 0:
-                value = value + pick(4.0 * math.pi, 0.0) * state[0, 2] * recv[2 * LATE]
+                value = value + pick(4.0 * math.pi, 0.0) * state[0, 2] * recv[PLANE]
             stage[field, k] = value
     copies.start("o", stage, rates.at[:, pl.ds(first, 2)])
     copies.wait_all()
@@ -521,7 +563,7 @@
 
 def substep(*fields):
     fields = [pltpu.with_memory_space_constraint(field, pltpu.HBM) for field in fields]
-    lapse, conf, _, _, _, shift, dens, mom, ener, velo, pres = fields
+    lapse, conf, mean, _, _, shift, dens, mom, ener, velo, pres = fields
     nx, ny, nz = lapse.shape
     fx = dens.shape[1]
     layer = (ny, nz)
@@ -549,12 +591,12 @@
     early = pl.pallas_call(
         pack_kernel,
         out_shape=shape(EARLY_LAYERS),
-        in_specs=[HBM] * 8,
+        in_specs=[HBM] * 9,
         out_specs=VMEM,
-        scratch_shapes=[sems(16)],
+        scratch_shapes=[vmem(3), vmem(2), sems(16)],
         compiler_params=params,
         name="pack",
-    )(lapse, conf, shift, dens, mom, ener, velo, pres)
+    )(lapse, conf, shift, mean, dens, mom, ener, velo, pres)
     packed = early
     early = lax.ppermute(early, RING, slow_pairs)
     local = pl.pallas_call(
@@ -565,7 +607,7 @@
             shape(nx),
             shape(9, fx),
             shape(EARLY_LAYERS + 2 * LATE + 1),
-            shape(2 * LATE + 1),
+            shape(2 * LATE),
         ),
         in_specs=[VMEM] + [HBM] * 11,
         out_specs=[VMEM] * 6,
@@ -613,13 +655,13 @@
     rates = pl.pallas_call(
         late_kernel,
         out_shape=shape(15, nx),
-        in_specs=[VMEM] * 3 + [HBM],
+        in_specs=[VMEM] * 4 + [HBM],
         out_specs=HBM,
-        input_output_aliases={3: 0},
+        input_output_aliases={4: 0},
         scratch_shapes=[vmem(15, 2), sems(4)],
         compiler_params=params,
         name="late",
-    )(late, stage, state, rates)
+    )(late, early, stage, state, rates)
     return rates, hydro
 
 

time: 31.6 us -> 30.9 us (0.978)
  waiting for transfers between devices: 9.68 us -> 8.97 us
    ppermute x1, waiting for transfers between devices: 8.58 us -> 8.06 us  [substep(): early = lax.ppermute(early, RING, slow_pairs)]
  transfers between devices with their start and end apart: 3 -> 3, of which waited for: 2 -> 2; matrix products, arithmetic and copies ran while one was open for 0% -> 0% of each run, Pallas kernels for 41% -> 42%
where the time goes in v7:
time: 30.9 us; the launch traced here: 30.7 us
  Pallas kernels  18.4 us (60%)
  waiting for transfers between devices  8.97 us (29%)
  starting transfers between devices  2.67 us (9%)
  between operations  0.69 us (2%)
    ppermute x1, waiting for transfers between devices, substep(): early = lax.ppermute(early, RING, slow_pairs)  8.06 us
    pallas_call x1, Pallas kernels, substep(): pl.pallas_call(inner_kernel, out_shape=(shape(15, nx), shape(1, 5, fx)),...  4.74 us
    pallas_call x1, Pallas kernels, substep(): pl.pallas_call(fast_kernel, out_shape=(shape(15, nx), shape(1, 5, fx), sh...  4.49 us
    pallas_call x1, Pallas kernels, substep(): pl.pallas_call(slow_kernel, out_shape=(shape(1, 5, fx), shape(METRIC, nx...  3.65 us
    pallas_call x1, Pallas kernels, substep(): state, flux, sources, fluid, fast, late = local(packed, *fields)  3.32 us
    ppermute x1, starting transfers between devices, substep(): early = lax.ppermute(early, RING, slow_pairs)  2.52 us
    pallas_call x1, Pallas kernels, substep(): pl.pallas_call(pack_kernel, out_shape=shape(EARLY_LAYERS), in_specs=[HBM]...  1.25 us
    pallas_call x1, Pallas kernels, substep(): pl.pallas_call(late_kernel, out_shape=shape(15, nx), in_specs=[VMEM] * 4...  0.91 us
  transfers between devices with their start and end apart: 3, of which 2 were waited for; matrix products, arithmetic and copies ran while one was open for 0% of the time, Pallas kernels for 42%

profile of v7, /device:TPU:1, one launch (start us, length us, event | category | flops | bytes accessed | tf_op | source)
XLA Modules:
  0.0 30.7 jit_solution(12029282811502902270)
XLA Ops:
  0.6 1.2 %pack.1.packed = f32[33,16,256]{2,1,0:T(8,128)S(1)} custom-call(f32[8,16,256]{2,1,0:T(8,128)} %lapse.3, f32[8,16,256]{2,1,0:T(8,128)} %conf.3, f32[3,8,16,256]{3,2,1,0:T(8,128)} %shift.3, f32[8,16,256]{2,1,0:T(8,128)} %mean.3, f32[1,16,16,256]{3,2,1,0:T(8,128)} %dens.3, f32[1,3,16,16,256]{4,3,2,1,0:T(8,128)} %mom.3, f32[1,16,16,256]{3,2,1,0:T(8,128)} %ener.3, ...), custom_call_target="tpu_custom_call" | custom-call | tf_op jit(solution)/shard_map/pack/pallas_call | solution.py:591
  1.9 3.3 %local.1 = (f32[18,13,16,256]{3,2,1,0:T(8,128)S(1)}, f32[10,22,16,256]{3,2,1,0:T(8,128)S(1)}, f32[8,16,256]{2,1,0:T(8,128)S(1)}, f32[9,16,16,256]{3,2,1,0:T(8,12...) custom-call(f32[33,16,256]{2,1,0:T(8,128)S(1)} %pack.1.packed, f32[8,16,256]{2,1,0:T(8,128)} %lapse.3, ...), custom_call_target="tpu_custom_call" | custom-call | flops 200000000 | bytes 6000000 | tf_op jit(solution)/shard_map/local/pallas_call | solution.py:619
  5.2 0.1 collective-permute-start.2
  5.3 2.5 %collective-permute-start.1 = (f32[33,16,256]{2,1,0:T(8,128)S(1)}, f32[33,16,256]{2,1,0:T(8,128)S(1)}, u32[]{:S(2)}, u32[]{:S(2)}) collective-permute-start(f32[33,16,256]{2,1,0:T(8,128)S(1)} %pack.1.packed), channel_id=1, source_target_pairs={{0,31},{1,2},{2,1},{3,4},{4,3},{5,6},{6,5},{7,8},{8,7},{9,10},{10,... | collective-permute-start | bytes 1622024 | tf_op jit(solution)/shard_map/ppermute | solution.py:601
  7.8 0.1 collective-permute-start
  7.9 4.7 %inner.1 = (f32[15,8,16,256]{3,2,1,0:T(8,128)}, f32[1,5,16,16,256]{4,3,2,1,0:T(8,128)}) custom-call(f32[18,13,16,256]{3,2,1,0:T(8,128)S(1)} %get-tuple-element.19.state.state_in, f32[10,22,16,256]{3,2,1,0:T(8,128)S(1)} %get-tuple-element.20.flux.flux_in, f32[8,16,256]{2,1,0:T(8,128)S(1)} %get-tuple-element.21.sources), custom_call_target="tpu_custom_call" | custom-call | flops 400000000 | bytes 6000000 | tf_op jit(solution)/shard_map/inner/pallas_call | solution.py:622
  12.6 0.0 collective-permute-done.2.recv
  12.7 4.5 %fast.1 = (f32[15,8,16,256]{3,2,1,0:T(8,128)}, f32[1,5,16,16,256]{4,3,2,1,0:T(8,128)}, f32[18,13,16,256]{3,2,1,0:T(8,128)S(1)}, f32[10,22,16,256]{3,2,1,0:T(8,128)S(1)}) custom-call(f32[60,16,256]{2,1,0:T(8,128)S(1)} %collective-permute-done.2.recv, ...), custom_call_target="tpu_custom_call", output_to_operand_aliasing={{0}: (1, {}), {1}: (2, {}), {2}: (3, {}), {3}: (4, {})} | custom-call | flops 300000000 | bytes 6000000 | tf_op jit(solution)/shard_map/fast/pallas_call | solution.py:633
  17.2 8.1 %collective-permute-done.1.recv.early = f32[33,16,256]{2,1,0:T(8,128)S(1)} collective-permute-done((f32[33,16,256]{2,1,0:T(8,128)S(1)}, f32[33,16,256]{2,1,0:T(8,128)S(1)}, u32[]{:S(2)}, u32[]{:S(2)}) %collective-permute-start.1) | collective-permute-done | bytes 540704 | tf_op jit(solution)/shard_map/ppermute | solution.py:601
  25.2 3.6 %slow.1 = (f32[1,5,16,16,256]{4,3,2,1,0:T(8,128)}, f32[18,13,16,256]{3,2,1,0:T(8,128)S(1)}, f32[10,22,16,256]{3,2,1,0:T(8,128)S(1)}, f32[15,2,16,256]{3,2,1,0:T(8,128)S(1)}) custom-call(f32[33,16,256]{2,1,0:T(8,128)S(1)} %collective-permute-done.1.recv.early, ...), custom_call_target="tpu_custom_call", output_to_operand_aliasing={{0}: (1, {}), {1}: (2, {}), {2}: (3, {})} | custom-call | flops 300000000 | bytes 6000000 | tf_op jit(solution)/shard_map/slow/pallas_call | solution.py:644
  28.9 0.9 %collective-permute-done.recv = f32[26,16,256]{2,1,0:T(8,128)S(1)} collective-permute-done((f32[26,16,256]{2,1,0:T(8,128)S(1)}, f32[26,16,256]{2,1,0:T(8,128)S(1)}, u32[]{:S(2)}, u32[]{:S(2)}) %collective-permute-start) | collective-permute-done | bytes 426016 | tf_op jit(solution)/shard_map/ppermute | solution.py:621
  29.8 0.9 %late.1 = f32[15,8,16,256]{3,2,1,0:T(8,128)} custom-call(f32[26,16,256]{2,1,0:T(8,128)S(1)} %collective-permute-done.recv, f32[33,16,256]{2,1,0:T(8,128)S(1)} %collective-permute-done.1.recv.early, f32[15,2,16,256]{3,2,1,0:T(8,128)S(1)} %get-tuple-element.28.stage_in, ...), custom_call_target="tpu_custom_call", output_to_operand_aliasing={{}: (4, {})} | custom-call | tf_op jit(solution)/shard_map/late/pallas_call | solution.py:655
Async XLA Ops:
  5.2 7.4 %collective-permute-start.2 = (f32[60,16,256]{2,1,0:T(8,128)S(1)}, f32[60,16,256]{2,1,0:T(8,128)S(1)}, u32[]{:S(2)}, u32[]{:S(2)}) collective-permute-start(f32[60,16,256]{2,1,0:T(8,128)S(1)} %get-tuple-element.18), channel_id=1, source_target_pairs={{0,1},{1,0},{2,3},{3,2},{4,5},{5,4},{6,7},{7,6},{8,9},{9,8},{10,11... | collective-permute-start | bytes 2949128 | tf_op jit(solution)/shard_map/ppermute | solution.py:620
  5.3 19.9 %collective-permute-start.1 = (f32[33,16,256]{2,1,0:T(8,128)S(1)}, f32[33,16,256]{2,1,0:T(8,128)S(1)}, u32[]{:S(2)}, u32[]{:S(2)}) collective-permute-start(f32[33,16,256]{2,1,0:T(8,128)S(1)} %pack.1.packed), channel_id=1, source_target_pairs={{0,31},{1,2},{2,1},{3,4},{4,3},{5,6},{6,5},{7,8},{8,7},{9,10},{10,... | collective-permute-start | bytes 1622024 | tf_op jit(solution)/shard_map/ppermute | solution.py:601
  7.8 22.0 %collective-permute-start = (f32[26,16,256]{2,1,0:T(8,128)S(1)}, f32[26,16,256]{2,1,0:T(8,128)S(1)}, u32[]{:S(2)}, u32[]{:S(2)}) collective-permute-start(f32[26,16,256]{2,1,0:T(8,128)S(1)} %get-tuple-element.17), channel_id=1, source_target_pairs={{0,31},{1,2},{2,1},{3,4},{4,3},{5,6},{6,5},{7,8},{8,7},{9,10},{10,... | collective-permute-start | bytes 1277960 | tf_op jit(solution)/shard_map/ppermute | solution.py:621

commit v8 on v7

--- a/solution.py
+++ b/solution.py
@@ -17,7 +17,8 @@
 METRIC = 18
 EARLY = 5
 LATE = 13
-PLANE = 2 * LATE - 2
+LAST = 3
+PLANE = 2 * (LATE - LAST) - 2
 FLUID = 7
 EARLY_LAYERS = 2 * EARLY + 3 * FLUID + 2
 SPARE = EARLY_LAYERS - 2
@@ -351,7 +352,7 @@
 
 def local_kernel(
     packed, lapse, conf, mean, metric, curv, shift, dens, mom, ener, velo, pres,
-    state, flux, sources, fluid, fast, late,
+    state, flux, sources, fluid, fast, late, last,
     coarse, rows, sems,
 ):
     nx, ny, nz = lapse.shape
@@ -368,7 +369,12 @@
     copies.start("f", pres.at[0], fluid.at[6])
     copies.start("f", velo.at[0, pl.ds(1, 2)], fluid.at[pl.ds(7, 2)])
     side = slow_side()
-    send_late(copies, "o", side, mean, metric, curv, late, 0)
+    layer = (ny, nz)
+    edge = pl.ds(side * (nx - 2), 2)
+    copies.start("o", metric.at[pl.ds(LAST, 3), edge], late.at[pl.ds(0, 6)].reshape(3, 2, *layer))
+    copies.start("o", curv.at[:, edge], late.at[pl.ds(6, 12)].reshape(6, 2, *layer))
+    copies.start("o", mean.at[edge], late.at[pl.ds(18, 2)])
+    copies.start("o", metric.at[pl.ds(0, LAST), edge], last.at[...].reshape(LAST, 2, *layer))
     send_early(copies, "o", 1 - side, lapse, conf, shift, dens, mom, ener, velo, pres, fast)
     send_late(copies, "o", 1 - side, mean, metric, curv, fast, EARLY_LAYERS)
     copies.start("o", mean, state.at[2, inner])
@@ -533,9 +539,8 @@
     copies.wait_all()
 
 
-def late_kernel(recv, early, stage_in, state, rates_in, rates, stage, sems):
+def late_rates(copies, groups, tap, extra, stage_in, state, rates, stage):
     nx = rates.shape[1]
-    copies = Copies(sems)
     side = slow_side()
     low = side == 0
 
@@ -544,20 +549,39 @@
 
     taps = ((pick(1.0, -1.0), pick(-8.0, 0.0)), (pick(0.0, 8.0), pick(1.0, -1.0)))
     first = side * (nx - 2)
-    for k in range(2):
-        step = state[15, first + 2 + k] * (1.0 / 12.0)
-        for field in range(15):
-            value = stage_in[field, k]
-            if field == 2:
-                values = [jnp.where(low, early[SPARE + n], recv[PLANE + n]) for n in range(2)]
-            elif field > 2:
-                values = [recv[2 * (field - 3) + n] for n in range(2)]
-            if field >= 2:
-                value = value + step * (taps[k][0] * values[0] + taps[k][1] * values[1])
-            if field == 2 and k == 0:
-                value = value + pick(4.0 * math.pi, 0.0) * state[0, 2] * recv[PLANE]
-            stage[field, k] = value
-    copies.start("o", stage, rates.at[:, pl.ds(first, 2)])
+    layers = pl.ds(first, 2)
+    steps = [state[15, first + 2 + k] * (1.0 / 12.0) for k in range(2)]
+    for begin, end in groups:
+        for field in range(begin, end):
+            values = [tap(low, field, n) for n in range(2)]
+            for k in range(2):
+                value = stage_in[field, k] + steps[k] * (taps[k][0] * values[0] + taps[k][1] * values[1])
+                if field == 2 and k == 0:
+                    value = value + pick(4.0 * math.pi, 0.0) * extra()
+                stage[field, k] = value
+        group = pl.ds(begin, end - begin)
+        copies.start("o", stage.at[group], rates.at[group, layers])
+
+
+def late_kernel(recv, early, stage_in, state, rates_in, rates, stage, sems):
+    copies = Copies(sems)
+    layers = pl.ds(slow_side() * (rates.shape[1] - 2), 2)
+    copies.start("o", stage_in.at[pl.ds(0, 2)], rates.at[pl.ds(0, 2), layers])
+
+    def tap(low, field, n):
+        if field == 2:
+            return jnp.where(low, early[SPARE + n], recv[PLANE + n])
+        return recv[2 * (field - 3 - LAST) + n]
+
+    groups = ((3 + LAST, 9), (9, 12), (12, 15), (2, 3))
+    late_rates(copies, groups, tap, lambda: state[0, 2] * recv[PLANE], stage_in, state, rates, stage)
+    copies.wait_all()
+
+
+def last_kernel(recv, stage_in, state, rates_in, rates, stage, sems):
+    copies = Copies(sems)
+    groups = tuple((n, n + 1) for n in range(3, 3 + LAST))
+    late_rates(copies, groups, lambda low, field, n: recv[2 * (field - 3) + n], None, stage_in, state, rates, stage)
     copies.wait_all()
 
 
@@ -607,18 +631,20 @@
             shape(nx),
             shape(9, fx),
             shape(EARLY_LAYERS + 2 * LATE + 1),
-            shape(2 * LATE),
+            shape(2 * (LATE - LAST)),
+            shape(2 * LAST),
         ),
         in_specs=[VMEM] + [HBM] * 11,
-        out_specs=[VMEM] * 6,
+        out_specs=[VMEM] * 7,
         scratch_shapes=[vmem(3, nx), row_scratch(3 * nx), sems(40)],
         cost_estimate=cost(200_000_000),
         compiler_params=params,
         name="local",
     )
-    state, flux, sources, fluid, fast, late = local(packed, *fields)
+    state, flux, sources, fluid, fast, late, last = local(packed, *fields)
     fast = lax.ppermute(fast, RING, fast_pairs)
     late = lax.ppermute(late, RING, slow_pairs)
+    last = lax.ppermute(last, RING, slow_pairs)
     rates, hydro = pl.pallas_call(
         inner_kernel,
         out_shape=(shape(15, nx), shape(1, 5, fx)),
@@ -652,16 +678,27 @@
         compiler_params=params,
         name="slow",
     )(early, hydro, state, flux, sources, fluid)
-    rates = pl.pallas_call(
+    late_call = pl.pallas_call(
         late_kernel,
         out_shape=shape(15, nx),
         in_specs=[VMEM] * 4 + [HBM],
         out_specs=HBM,
         input_output_aliases={4: 0},
-        scratch_shapes=[vmem(15, 2), sems(4)],
+        scratch_shapes=[vmem(15, 2), sems(8)],
         compiler_params=params,
         name="late",
-    )(late, early, stage, state, rates)
+    )
+    rates = late_call(late, early, stage, state, rates)
+    rates = pl.pallas_call(
+        last_kernel,
+        out_shape=shape(15, nx),
+        in_specs=[VMEM] * 3 + [HBM],
+        out_specs=HBM,
+        input_output_aliases={3: 0},
+        scratch_shapes=[vmem(15, 2), sems(8)],
+        compiler_params=params,
+        name="last",
+    )(last, stage, state, rates)
     return rates, hydro
 
 

time: 30.9 us -> 32.3 us (1.045)
  the two profiles are of different devices: /device:TPU:1 before, /device:TPU:0 now
where the time goes in v8:
time: 32.3 us; the launch traced here: 32 us
  Pallas kernels  18.8 us (58%)
  starting transfers between devices  12.5 us (39%)
  between operations  0.71 us (2%)
    ppermute x1, starting transfers between devices, substep(): early = lax.ppermute(early, RING, slow_pairs)  6.42 us
    ppermute x1, starting transfers between devices, substep(): last = lax.ppermute(last, RING, slow_pairs)  5.3 us
    pallas_call x1, Pallas kernels, substep(): pl.pallas_call(inner_kernel, out_shape=(shape(15, nx), shape(1, 5, fx)),...  4.74 us
    pallas_call x1, Pallas kernels, substep(): pl.pallas_call(fast_kernel, out_shape=(shape(15, nx), shape(1, 5, fx), sh...  4.49 us
    pallas_call x1, Pallas kernels, substep(): pl.pallas_call(slow_kernel, out_shape=(shape(1, 5, fx), shape(METRIC, nx...  3.65 us
    pallas_call x1, Pallas kernels, substep(): state, flux, sources, fluid, fast, late, last = local(packed, *fields)  3.16 us
    pallas_call x1, Pallas kernels, substep(): pl.pallas_call(pack_kernel, out_shape=shape(EARLY_LAYERS), in_specs=[HBM]...  1.25 us
    pallas_call x1, Pallas kernels, substep(): rates = late_call(late, early, stage, state, rates)  0.82 us
  transfers between devices with their start and end apart: 4, of which 0 were waited for; matrix products, arithmetic and copies ran while one was open for 0% of the time, Pallas kernels for 43%

profile of v8, /device:TPU:0, one launch (start us, length us, event | category | flops | bytes accessed | tf_op | source)
XLA Modules:
  0.0 32.0 jit_solution(18317532636449655057)
XLA Ops:
  0.6 1.2 %pack.1.packed = f32[33,16,256]{2,1,0:T(8,128)S(1)} custom-call(f32[8,16,256]{2,1,0:T(8,128)} %lapse.3, f32[8,16,256]{2,1,0:T(8,128)} %conf.3, f32[3,8,16,256]{3,2,1,0:T(8,128)} %shift.3, f32[8,16,256]{2,1,0:T(8,128)} %mean.3, f32[1,16,16,256]{3,2,1,0:T(8,128)} %dens.3, f32[1,3,16,16,256]{4,3,2,1,0:T(8,128)} %mom.3, f32[1,16,16,256]{3,2,1,0:T(8,128)} %ener.3, ...), custom_call_target="tpu_custom_call" | custom-call | tf_op jit(solution)/shard_map/pack/pallas_call | solution.py:615
  1.9 3.2 %local.1 = (f32[18,13,16,256]{3,2,1,0:T(8,128)S(1)}, f32[10,22,16,256]{3,2,1,0:T(8,128)S(1)}, f32[8,16,256]{2,1,0:T(8,128)S(1)}, f32[9,16,16,256]{3,2,1,0:T(8,12...) custom-call(f32[33,16,256]{2,1,0:T(8,128)S(1)} %pack.1.packed, ...), custom_call_target="tpu_custom_call" | custom-call | flops 200000000 | bytes 6000000 | tf_op jit(solution)/shard_map/local/pallas_call | solution.py:644
  5.1 0.7 %collective-permute-start.2 = (f32[60,16,256]{2,1,0:T(8,128)S(1)}, f32[60,16,256]{2,1,0:T(8,128)S(1)}, u32[]{:S(2)}, u32[]{:S(2)}) collective-permute-start(f32[60,16,256]{2,1,0:T(8,128)S(1)} %get-tuple-element.19), channel_id=1, source_target_pairs={{0,1},{1,0},{2,3},{3,2},{4,5},{5,4},{6,7},{7,6},{8,9},{9,8},{10,11... | collective-permute-start | bytes 2949128 | tf_op jit(solution)/shard_map/ppermute | solution.py:645
  5.8 6.4 %collective-permute-start.1 = (f32[33,16,256]{2,1,0:T(8,128)S(1)}, f32[33,16,256]{2,1,0:T(8,128)S(1)}, u32[]{:S(2)}, u32[]{:S(2)}) collective-permute-start(f32[33,16,256]{2,1,0:T(8,128)S(1)} %pack.1.packed), channel_id=1, source_target_pairs={{0,31},{1,2},{2,1},{3,4},{4,3},{5,6},{6,5},{7,8},{8,7},{9,10},{10,... | collective-permute-start | bytes 1622024 | tf_op jit(solution)/shard_map/ppermute | solution.py:625
  12.2 0.0 collective-permute-start.3
  12.2 5.3 %collective-permute-start = (f32[6,16,256]{2,1,0:T(8,128)S(1)}, f32[6,16,256]{2,1,0:T(8,128)S(1)}, u32[]{:S(2)}, u32[]{:S(2)}) collective-permute-start(f32[6,16,256]{2,1,0:T(8,128)S(1)} %get-tuple-element.18), channel_id=1, source_target_pairs={{0,31},{1,2},{2,1},{3,4},{4,3},{5,6},{6,5},{7,8},{8,7},{9,10},{10,... | collective-permute-start | bytes 294920 | tf_op jit(solution)/shard_map/ppermute | solution.py:647
  17.5 4.7 %inner.1 = (f32[15,8,16,256]{3,2,1,0:T(8,128)}, f32[1,5,16,16,256]{4,3,2,1,0:T(8,128)}) custom-call(f32[18,13,16,256]{3,2,1,0:T(8,128)S(1)} %get-tuple-element.20.state.state_in, f32[10,22,16,256]{3,2,1,0:T(8,128)S(1)} %get-tuple-element.21.flux.flux_in, f32[8,16,256]{2,1,0:T(8,128)S(1)} %get-tuple-element.22.sources), custom_call_target="tpu_custom_call" | custom-call | flops 400000000 | bytes 6000000 | tf_op jit(solution)/shard_map/inner/pallas_call | solution.py:648
  22.3 0.0 collective-permute-done.2.recv
  22.3 4.5 %fast.1 = (f32[15,8,16,256]{3,2,1,0:T(8,128)}, f32[1,5,16,16,256]{4,3,2,1,0:T(8,128)}, f32[18,13,16,256]{3,2,1,0:T(8,128)S(1)}, f32[10,22,16,256]{3,2,1,0:T(8,128)S(1)}) custom-call(f32[60,16,256]{2,1,0:T(8,128)S(1)} %collective-permute-done.2.recv, ...), custom_call_target="tpu_custom_call", output_to_operand_aliasing={{0}: (1, {}), {1}: (2, {}), {2}: (3, {}), {3}: (4, {})} | custom-call | flops 300000000 | bytes 6000000 | tf_op jit(solution)/shard_map/fast/pallas_call | solution.py:659
  26.8 0.0 collective-permute-done.1.recv.early
  26.8 3.6 %slow.1 = (f32[1,5,16,16,256]{4,3,2,1,0:T(8,128)}, f32[18,13,16,256]{3,2,1,0:T(8,128)S(1)}, f32[10,22,16,256]{3,2,1,0:T(8,128)S(1)}, f32[15,2,16,256]{3,2,1,0:T(8,128)S(1)}) custom-call(f32[33,16,256]{2,1,0:T(8,128)S(1)} %collective-permute-done.1.recv.early, ...), custom_call_target="tpu_custom_call", output_to_operand_aliasing={{0}: (1, {}), {1}: (2, {}), {2}: (3, {})} | custom-call | flops 300000000 | bytes 6000000 | tf_op jit(solution)/shard_map/slow/pallas_call | solution.py:670
  30.5 0.0 collective-permute-done.3.recv
  30.5 0.8 %late.1.rates_in = f32[15,8,16,256]{3,2,1,0:T(8,128)} custom-call(f32[20,16,256]{2,1,0:T(8,128)S(1)} %collective-permute-done.3.recv, f32[33,16,256]{2,1,0:T(8,128)S(1)} %collective-permute-done.1.recv.early, f32[15,2,16,256]{3,2,1,0:T(8,128)S(1)} %get-tuple-element.29.stage_in, ...), custom_call_target="tpu_custom_call", output_to_operand_aliasing={{}: (4, {})} | custom-call | tf_op jit(solution)/shard_map/late/pallas_call | solution.py:691
  31.3 0.0 collective-permute-done.recv
  31.3 0.7 %last.1 = f32[15,8,16,256]{3,2,1,0:T(8,128)} custom-call(f32[6,16,256]{2,1,0:T(8,128)S(1)} %collective-permute-done.recv, f32[15,2,16,256]{3,2,1,0:T(8,128)S(1)} %get-tuple-element.29.stage_in, f32[18,13,16,256]{3,2,1,0:T(8,128)S(1)} %get-tuple-element.30.state, f32[15,8,16,256]{3,2,1,0:T(8,128)} %late.1.rates_in), custom_call_target="tpu_custom_call", output_to_operand_aliasing={{}: (3, {})} | custom-call | tf_op jit(solution)/shard_map/last/pallas_call | solution.py:692
Async XLA Ops:
  5.1 17.2 %collective-permute-start.2 = (f32[60,16,256]{2,1,0:T(8,128)S(1)}, f32[60,16,256]{2,1,0:T(8,128)S(1)}, u32[]{:S(2)}, u32[]{:S(2)}) collective-permute-start(f32[60,16,256]{2,1,0:T(8,128)S(1)} %get-tuple-element.19), channel_id=1, source_target_pairs={{0,1},{1,0},{2,3},{3,2},{4,5},{5,4},{6,7},{7,6},{8,9},{9,8},{10,11... | collective-permute-start | bytes 2949128 | tf_op jit(solution)/shard_map/ppermute | solution.py:645
  5.8 21.0 %collective-permute-start.1 = (f32[33,16,256]{2,1,0:T(8,128)S(1)}, f32[33,16,256]{2,1,0:T(8,128)S(1)}, u32[]{:S(2)}, u32[]{:S(2)}) collective-permute-start(f32[33,16,256]{2,1,0:T(8,128)S(1)} %pack.1.packed), channel_id=1, source_target_pairs={{0,31},{1,2},{2,1},{3,4},{4,3},{5,6},{6,5},{7,8},{8,7},{9,10},{10,... | collective-permute-start | bytes 1622024 | tf_op jit(solution)/shard_map/ppermute | solution.py:625
  12.2 18.3 %collective-permute-start.3 = (f32[20,16,256]{2,1,0:T(8,128)S(1)}, f32[20,16,256]{2,1,0:T(8,128)S(1)}, u32[]{:S(2)}, u32[]{:S(2)}) collective-permute-start(f32[20,16,256]{2,1,0:T(8,128)S(1)} %get-tuple-element.31), channel_id=1, source_target_pairs={{0,31},{1,2},{2,1},{3,4},{4,3},{5,6},{6,5},{7,8},{8,7},{9,10},{10,... | collective-permute-start | bytes 983048 | tf_op jit(solution)/shard_map/ppermute | solution.py:646
  12.2 19.1 %collective-permute-start = (f32[6,16,256]{2,1,0:T(8,128)S(1)}, f32[6,16,256]{2,1,0:T(8,128)S(1)}, u32[]{:S(2)}, u32[]{:S(2)}) collective-permute-start(f32[6,16,256]{2,1,0:T(8,128)S(1)} %get-tuple-element.18), channel_id=1, source_target_pairs={{0,31},{1,2},{2,1},{3,4},{4,3},{5,6},{6,5},{7,8},{8,7},{9,10},{10,... | collective-permute-start | bytes 294920 | tf_op jit(solution)/shard_map/ppermute | solution.py:647
